TPU v7x, 512 devices: a whole 4x8x8 slice. The times are simulated.
512 devices in a mesh: batch: 128 (over x, y_lo, z), mp: 4 (over y_hi, core).
Axes of the slice: x: 4, y: 8 (y_hi: 2, y_lo: 4; y = y_hi * 4 + y_lo), z: 8, core: 2. Of those that a mesh axis runs over, the one named last changes fastest.
Arguments:
- img_feat: bfloat16 [2048, 1536], P('batch'), may hold values from -6 to 6
- txt_feat: bfloat16 [2048, 1536], P('batch'), may hold values from -6 to 6
- w_img: bfloat16 [1536, 1152], P('batch', 'mp'), may hold values from -0.15625 to 0.15625
- w_txt: bfloat16 [1536, 1152], P('batch', 'mp'), may hold values from -0.15625 to 0.15625
- pair_index: int32 [2048], P('batch'), may hold values from 0 to 2047, each once
- log_scale: float32 [1], replicated, may hold values from 2 to 2.6
- bias: float32 [1], replicated, may hold values from -6 to -4
Outputs:
- image_grad: float32 [2048, 1152], P('batch', 'mp')
- text_grad: float32 [2048, 1152], P(('batch', 'mp'))
Inputs may be any that keep to these rules, and one draw needn't show every extreme that they name: `pair_index`: each text index appears exactly once.
All inputs are finite; a program needn't handle non-finite values.
Results may differ from a plain program's by a relative error of at most 0.0046.
Values may be sent and summed in bfloat16 or wider, within the bound.
No kernel may reach another device: no remote copies, remote signals or barrier semaphores. Data moves between devices by JAX's collectives and lax.ppermute only.
A program may use at most 64 MiB of HBM per device.

v0:
```python
import jax
import jax.numpy as jnp
from jax import lax
from jax.sharding import Mesh
from jax.sharding import PartitionSpec as P

BATCH = ("batch_0", "batch_1", "batch_2")
MP = ("mp_0", "mp_1")
BATCH_MP = ("batch_0", "batch_1", "batch_2", "mp_0", "mp_1")


epsilon = 1e-06


def joined_along(pieces, dim):
    lengths = list(pieces.shape[1:])
    lengths[dim] *= pieces.shape[0]
    return jnp.moveaxis(pieces, 0, dim).reshape(lengths)


def stacked_from(x, axes, order):
    pieces = x[None]
    for k in order:
        pieces = lax.all_gather(pieces, axes[k], axis=0, tiled=True)
    current = [lax.axis_size(axes[k]) for k in reversed(order)]
    pieces = pieces.reshape(*current, *x.shape)
    turned = sorted(range(len(order)), key=lambda place: order[len(order) - 1 - place])
    return pieces.transpose(*turned, *range(len(order), pieces.ndim)).reshape(-1, *x.shape)


def gathered_by_axis(x, axes, order, dim):
    return joined_along(stacked_from(x, axes, order), dim)


def from_behind(value, axis, steps):
    count = lax.axis_size(axis)
    pairs = [(source, (source + steps) % count) for source in range(count)]
    return lax.ppermute(value, axis, pairs)


def in_blocks(x, dim, size):
    before, after = (x.shape[:dim], x.shape[dim + 1 :])
    return jnp.moveaxis(x.reshape(*before, size, -1, *after), dim, 0)


def sent_and_summed(x, axis, dim):
    pieces = in_blocks(x, dim, lax.axis_size(axis))
    arrived = lax.all_to_all(pieces, axis, split_axis=0, concat_axis=0, tiled=True)
    return arrived.sum(axis=0)


def normalize(pre):
    values = pre.astype(jnp.float32)
    norm = lax.rsqrt(jnp.sum(values * values, axis=1, keepdims=True) + epsilon)
    return (values * norm).astype(jnp.bfloat16)


def block_update(image, pairing, scale, offset, text, first):
    count = text.shape[0]
    scores = lax.dot_general(
        image, text, (((1,), (1,)), ((), ())), preferred_element_type=jnp.float32
    )
    logits = scale * scores + offset
    columns = first + jnp.arange(count, dtype=jnp.int32)
    label = jnp.where(pairing[:, None] == columns[None, :], 1.0, -1.0).astype(jnp.float32)
    coef = (-label * jax.nn.sigmoid(-label * logits)).astype(jnp.bfloat16)
    image_term = jnp.dot(coef, text, preferred_element_type=jnp.float32)
    text_term = lax.dot_general(
        coef, image, (((0,), (0,)), ((), ())), preferred_element_type=jnp.float32
    )
    return (image_term, text_term)


def local(img_feat, txt_feat, w_img, w_txt, pair_index, log_scale, bias):
    rows = img_feat.shape[0]
    cycle_size = lax.axis_size(BATCH)
    group_size = lax.axis_size(MP)
    here = lax.axis_index(BATCH)
    member = lax.axis_index(MP)
    piece_rows = rows // group_size
    columns_part = w_img.shape[1]
    width = group_size * columns_part
    span = min(cycle_size, 32)
    half = span // 2
    first = jnp.dot(
        img_feat, gathered_by_axis(w_img, BATCH, (1, 2, 0), 0), preferred_element_type=jnp.float32
    )
    second = jnp.dot(
        txt_feat, gathered_by_axis(w_txt, BATCH, (1, 2, 0), 0), preferred_element_type=jnp.float32
    )
    full_img, full_txt = (
        gathered_by_axis(first.astype(jnp.bfloat16), MP, (0, 1), 1),
        gathered_by_axis(second.astype(jnp.bfloat16), MP, (0, 1), 1),
    )
    image = normalize(full_img)
    own_start = member * piece_rows
    text = normalize(lax.dynamic_slice_in_dim(full_txt, own_start, piece_rows, 0))
    scale = jnp.exp(log_scale[0])
    offset = bias[0]
    image_total = jnp.zeros((rows, width), jnp.float32)
    start_grads = jnp.zeros((piece_rows, width), jnp.float32)

    def first_row(anchor):
        return anchor * rows + member * piece_rows

    def turn_front(step, carry):
        front, front_acc, totals = carry
        anchor = (here - step) % cycle_size
        image_term, text_term = block_update(
            image, pair_index, scale, offset, front, first_row(anchor)
        )
        front = from_behind(front, BATCH, 1)
        front_acc = from_behind(front_acc + text_term, BATCH, 1)
        return (front, front_acc, totals + image_term)

    def turn_rear(step, carry):
        rear, rear_acc, totals = carry
        rear = from_behind(rear, BATCH, -1)
        rear_acc = from_behind(rear_acc, BATCH, -1)
        anchor = (here + step + 1) % cycle_size
        image_term, text_term = block_update(
            image, pair_index, scale, offset, rear, first_row(anchor)
        )
        return (rear, rear_acc + text_term, totals + image_term)

    front, front_acc, image_total = lax.fori_loop(
        0, half, turn_front, (text, start_grads, image_total)
    )
    rear, rear_acc, image_total = lax.fori_loop(
        0, half, turn_rear, (text, start_grads, image_total)
    )
    front_back = from_behind(front_acc, BATCH, -half)
    rear_back = from_behind(rear_acc, BATCH, half)
    text_total = front_back + rear_back
    image_part = sent_and_summed(image_total, MP, 1)
    return (scale * image_part, scale * text_total)


def solution(mesh):
    finer = Mesh(
        mesh.devices.reshape(4, 4, 8, 2, 2), ("batch_0", "batch_1", "batch_2", "mp_0", "mp_1")
    )
    in_specs = (P(BATCH, None), P(BATCH, None), P(BATCH, MP), P(BATCH, MP), P(BATCH), P(), P())
    out_specs = (P(BATCH, MP), P(BATCH_MP, None))
    return jax.shard_map(local, mesh=finer, in_specs=in_specs, out_specs=out_specs, check_vma=False)
```

profile of v0, /device:TPU:1, one launch (start us, length us, event | category | flops | bytes accessed | tf_op | source)
XLA Modules:
  0.0 614.7 jit_solution(6283159459050296204)
XLA Ops:
  0.7 11.5 %all-gather.4 = bf16[4,12,288]{2,1,0:T(8,128)(2,1)S(1)} all-gather(bf16[1,12,288]{2,1,0:T(8,128)(2,1)} %bitcast.76), channel_id=2, replica_groups=mesh['batch_0'=4,'batch_1'=4,'batch_2'=8,'mp_0'=2,'mp_1'=2] {'batch_1'}, dimensions={0}, use_global_device_ids=true | all-gather | bytes 34560 | tf_op jit(solution)/shard_map/all_gather | solution.py:24
  12.1 26.0 %all_gather.31 = bf16[32,12,288]{2,1,0:T(8,128)(2,1)S(1)} all-gather(bf16[4,12,288]{2,1,0:T(8,128)(2,1)S(1)} %all-gather.4), channel_id=1, replica_groups=mesh['batch_0'=4,'batch_1'=4,'batch_2'=8,'mp_0'=2,'mp_1'=2] {'batch_2'}, dimensions={0}, use_global_device_ids=true | all-gather | bytes 248832 | tf_op jit(solution)/shard_map/all_gather | solution.py:24
  38.2 12.2 %all_gather.32 = bf16[128,12,288]{2,0,1:T(8,128)(2,1)S(1)} all-gather(bf16[32,12,288]{2,0,1:T(8,128)(2,1)S(1)} %copy.24), channel_id=1, replica_groups=mesh['batch_0'=4,'batch_1'=4,'batch_2'=8,'mp_0'=2,'mp_1'=2] {'batch_0'}, dimensions={0}, use_global_device_ids=true | all-gather | bytes 1105920 | tf_op jit(solution)/shard_map/all_gather | solution.py:24
  52.4 7.2 %all-gather.1 = bf16[32,288]{1,0:T(8,128)(2,1)S(1)} all-gather(bf16[16,288]{1,0:T(8,128)(2,1)S(1)} %convolution_convert_fusion.1), channel_id=3, replica_groups=mesh['batch_0'=4,'batch_1'=4,'batch_2'=8,'mp_0'=2,'mp_1'=2] {'mp_0'}, dimensions={0}, use_global_device_ids=true | all-gather | bytes 27648 | tf_op jit(solution)/shard_map/all_gather | solution.py:24
  59.6 14.0 %all_gather.34 = bf16[4,16,288]{2,1,0:T(8,128)(2,1)S(1)} all-gather(bf16[2,16,288]{2,1,0:T(8,128)(2,1)S(1)} %bitcast.74), channel_id=1, replica_groups=mesh['batch_0'=4,'batch_1'=4,'batch_2'=8,'mp_0'=2,'mp_1'=2] {'mp_1'}, dimensions={0}, use_global_device_ids=true | all-gather | bytes 55296 | tf_op jit(solution)/shard_map/all_gather | solution.py:24
  73.9 10.2 %all-gather.5 = bf16[4,12,288]{2,1,0:T(8,128)(2,1)S(1)} all-gather(bf16[1,12,288]{2,1,0:T(8,128)(2,1)S(1)} %bitcast.77), channel_id=4, replica_groups=mesh['batch_0'=4,'batch_1'=4,'batch_2'=8,'mp_0'=2,'mp_1'=2] {'batch_1'}, dimensions={0}, use_global_device_ids=true | all-gather | bytes 34560 | tf_op jit(solution)/shard_map/all_gather | solution.py:24
  84.2 19.4 %all_gather.36 = bf16[32,12,288]{2,1,0:T(8,128)(2,1)S(1)} all-gather(bf16[4,12,288]{2,1,0:T(8,128)(2,1)S(1)} %all-gather.5), channel_id=1, replica_groups=mesh['batch_0'=4,'batch_1'=4,'batch_2'=8,'mp_0'=2,'mp_1'=2] {'batch_2'}, dimensions={0}, use_global_device_ids=true | all-gather | bytes 248832 | tf_op jit(solution)/shard_map/all_gather | solution.py:24
  103.6 11.8 %all_gather.37 = bf16[128,12,288]{2,0,1:T(8,128)(2,1)S(1)} all-gather(bf16[32,12,288]{2,0,1:T(8,128)(2,1)S(1)} %copy.28), channel_id=1, replica_groups=mesh['batch_0'=4,'batch_1'=4,'batch_2'=8,'mp_0'=2,'mp_1'=2] {'batch_0'}, dimensions={0}, use_global_device_ids=true | all-gather | bytes 1105920 | tf_op jit(solution)/shard_map/all_gather | solution.py:24
  117.5 7.2 %all-gather.3 = bf16[32,288]{1,0:T(8,128)(2,1)S(1)} all-gather(bf16[16,288]{1,0:T(8,128)(2,1)S(1)} %convolution_convert_fusion), channel_id=5, replica_groups=mesh['batch_0'=4,'batch_1'=4,'batch_2'=8,'mp_0'=2,'mp_1'=2] {'mp_0'}, dimensions={0}, use_global_device_ids=true | all-gather | bytes 27648 | tf_op jit(solution)/shard_map/all_gather | solution.py:24
  124.7 14.2 %all_gather.39 = bf16[4,16,288]{2,1,0:T(8,128)(2,1)S(1)} all-gather(bf16[2,16,288]{2,1,0:T(8,128)(2,1)S(1)} %bitcast.75), channel_id=1, replica_groups=mesh['batch_0'=4,'batch_1'=4,'batch_2'=8,'mp_0'=2,'mp_1'=2] {'mp_1'}, dimensions={0}, use_global_device_ids=true | all-gather | bytes 55296 | tf_op jit(solution)/shard_map/all_gather | solution.py:24
  140.0 215.3 %while.40 = (s32[]{:T(128)}, bf16[4,1152]{1,0:T(4,128)(2,1)S(1)}, f32[4,1152]{1,0:T(4,128)S(1)}, f32[16,1152]{1,0:T(8,128)S(1)}, s32[16]{0:T(128)S(1)}, /*index=...) while((s32[]{:T(128)}, bf16[4,1152]{1,0:T(4,128)(2,1)S(1)}, ...), condition=%wide.region_3.4_spmd.clone, body=%wide.region_2.3_spmd.clone.sunk | while | flops 484565 | bytes 406372 | solution.py:126
  140.0 2.9 collective-permute-start
  146.0 4.4 collective-permute-done
  150.4 3.9 collective-permute-done.1
  159.4 5.4 collective-permute-done
  164.8 3.0 collective-permute-done.1
  172.8 5.4 collective-permute-done
  178.2 3.0 collective-permute-done.1
  186.2 5.4 collective-permute-done
  191.6 3.0 collective-permute-done.1
  199.6 5.4 collective-permute-done
  205.0 3.0 collective-permute-done.1
  213.0 5.4 collective-permute-done
  218.4 3.0 collective-permute-done.1
  226.4 5.4 collective-permute-done
  231.8 3.0 collective-permute-done.1
  239.7 5.4 collective-permute-done
  245.2 3.0 collective-permute-done.1
  253.1 5.4 collective-permute-done
  258.5 3.0 collective-permute-done.1
  266.5 5.6 collective-permute-done
  272.1 2.8 collective-permute-done.1
  279.9 5.4 collective-permute-done
  285.3 3.0 collective-permute-done.1
  293.3 5.4 collective-permute-done
  298.7 3.0 collective-permute-done.1
  306.7 5.4 collective-permute-done
  312.1 3.0 collective-permute-done.1
  320.1 5.4 collective-permute-done
  325.5 3.0 collective-permute-done.1
  333.5 5.4 collective-permute-done
  338.9 3.0 collective-permute-done.1
  346.9 5.4 collective-permute-done
  352.3 3.0 collective-permute-done.1
  355.3 196.7 %while.41 = (s32[]{:T(128)}, bf16[4,1152]{1,0:T(4,128)(2,1)S(1)}, f32[4,1152]{1,0:T(4,128)S(1)}, f32[16,1152]{1,0:T(8,128)S(1)}, s32[16]{0:T(128)S(1)}, /*index=...) while((s32[]{:T(128)}, bf16[4,1152]{1,0:T(4,128)(2,1)S(1)}, ...), condition=%wide.region_5.6_spmd.clone, body=%wide.region_4.5_spmd.clone.sunk | while | flops 470742 | bytes 443248 | solution.py:129
  355.3 3.4 collective-permute-start.2
  363.3 7.9 %collective-permute-start.2 = (bf16[4,1152]{1,0:T(4,128)(2,1)S(1)}, bf16[4,1152]{1,0:T(4,128)(2,1)S(1)}, u32[]{:S(2)}, u32[]{:S(2)}) collective-permute-start(bf16[4,1152]{1,0:T(4,128)(2,1)S(1)} %get-tuple-element.787), channel_id=1, source_target_pairs={{0,508},{4,0},{8,4},{12,8},{16,12},{20,16},{24,20},{28,24},{32,28}... | collective-permute-start | bytes 27656 | tf_op jit(solution)/shard_map/while/body/eval_jaxpr/ppermute | solution.py:38
  375.8 7.9 %collective-permute-start.2 = (bf16[4,1152]{1,0:T(4,128)(2,1)S(1)}, bf16[4,1152]{1,0:T(4,128)(2,1)S(1)}, u32[]{:S(2)}, u32[]{:S(2)}) collective-permute-start(bf16[4,1152]{1,0:T(4,128)(2,1)S(1)} %get-tuple-element.787), channel_id=1, source_target_pairs={{0,508},{4,0},{8,4},{12,8},{16,12},{20,16},{24,20},{28,24},{32,28}... | collective-permute-start | bytes 27656 | tf_op jit(solution)/shard_map/while/body/eval_jaxpr/ppermute | solution.py:38
  388.4 7.9 %collective-permute-start.2 = (bf16[4,1152]{1,0:T(4,128)(2,1)S(1)}, bf16[4,1152]{1,0:T(4,128)(2,1)S(1)}, u32[]{:S(2)}, u32[]{:S(2)}) collective-permute-start(bf16[4,1152]{1,0:T(4,128)(2,1)S(1)} %get-tuple-element.787), channel_id=1, source_target_pairs={{0,508},{4,0},{8,4},{12,8},{16,12},{20,16},{24,20},{28,24},{32,28}... | collective-permute-start | bytes 27656 | tf_op jit(solution)/shard_map/while/body/eval_jaxpr/ppermute | solution.py:38
  401.0 7.9 %collective-permute-start.2 = (bf16[4,1152]{1,0:T(4,128)(2,1)S(1)}, bf16[4,1152]{1,0:T(4,128)(2,1)S(1)}, u32[]{:S(2)}, u32[]{:S(2)}) collective-permute-start(bf16[4,1152]{1,0:T(4,128)(2,1)S(1)} %get-tuple-element.787), channel_id=1, source_target_pairs={{0,508},{4,0},{8,4},{12,8},{16,12},{20,16},{24,20},{28,24},{32,28}... | collective-permute-start | bytes 27656 | tf_op jit(solution)/shard_map/while/body/eval_jaxpr/ppermute | solution.py:38
  413.6 7.9 %collective-permute-start.2 = (bf16[4,1152]{1,0:T(4,128)(2,1)S(1)}, bf16[4,1152]{1,0:T(4,128)(2,1)S(1)}, u32[]{:S(2)}, u32[]{:S(2)}) collective-permute-start(bf16[4,1152]{1,0:T(4,128)(2,1)S(1)} %get-tuple-element.787), channel_id=1, source_target_pairs={{0,508},{4,0},{8,4},{12,8},{16,12},{20,16},{24,20},{28,24},{32,28}... | collective-permute-start | bytes 27656 | tf_op jit(solution)/shard_map/while/body/eval_jaxpr/ppermute | solution.py:38
  426.2 7.9 %collective-permute-start.2 = (bf16[4,1152]{1,0:T(4,128)(2,1)S(1)}, bf16[4,1152]{1,0:T(4,128)(2,1)S(1)}, u32[]{:S(2)}, u32[]{:S(2)}) collective-permute-start(bf16[4,1152]{1,0:T(4,128)(2,1)S(1)} %get-tuple-element.787), channel_id=1, source_target_pairs={{0,508},{4,0},{8,4},{12,8},{16,12},{20,16},{24,20},{28,24},{32,28}... | collective-permute-start | bytes 27656 | tf_op jit(solution)/shard_map/while/body/eval_jaxpr/ppermute | solution.py:38
  438.8 7.9 %collective-permute-start.2 = (bf16[4,1152]{1,0:T(4,128)(2,1)S(1)}, bf16[4,1152]{1,0:T(4,128)(2,1)S(1)}, u32[]{:S(2)}, u32[]{:S(2)}) collective-permute-start(bf16[4,1152]{1,0:T(4,128)(2,1)S(1)} %get-tuple-element.787), channel_id=1, source_target_pairs={{0,508},{4,0},{8,4},{12,8},{16,12},{20,16},{24,20},{28,24},{32,28}... | collective-permute-start | bytes 27656 | tf_op jit(solution)/shard_map/while/body/eval_jaxpr/ppermute | solution.py:38
  451.3 7.9 %collective-permute-start.2 = (bf16[4,1152]{1,0:T(4,128)(2,1)S(1)}, bf16[4,1152]{1,0:T(4,128)(2,1)S(1)}, u32[]{:S(2)}, u32[]{:S(2)}) collective-permute-start(bf16[4,1152]{1,0:T(4,128)(2,1)S(1)} %get-tuple-element.787), channel_id=1, source_target_pairs={{0,508},{4,0},{8,4},{12,8},{16,12},{20,16},{24,20},{28,24},{32,28}... | collective-permute-start | bytes 27656 | tf_op jit(solution)/shard_map/while/body/eval_jaxpr/ppermute | solution.py:38
  463.9 7.9 %collective-permute-start.2 = (bf16[4,1152]{1,0:T(4,128)(2,1)S(1)}, bf16[4,1152]{1,0:T(4,128)(2,1)S(1)}, u32[]{:S(2)}, u32[]{:S(2)}) collective-permute-start(bf16[4,1152]{1,0:T(4,128)(2,1)S(1)} %get-tuple-element.787), channel_id=1, source_target_pairs={{0,508},{4,0},{8,4},{12,8},{16,12},{20,16},{24,20},{28,24},{32,28}... | collective-permute-start | bytes 27656 | tf_op jit(solution)/shard_map/while/body/eval_jaxpr/ppermute | solution.py:38
  476.5 7.9 %collective-permute-start.2 = (bf16[4,1152]{1,0:T(4,128)(2,1)S(1)}, bf16[4,1152]{1,0:T(4,128)(2,1)S(1)}, u32[]{:S(2)}, u32[]{:S(2)}) collective-permute-start(bf16[4,1152]{1,0:T(4,128)(2,1)S(1)} %get-tuple-element.787), channel_id=1, source_target_pairs={{0,508},{4,0},{8,4},{12,8},{16,12},{20,16},{24,20},{28,24},{32,28}... | collective-permute-start | bytes 27656 | tf_op jit(solution)/shard_map/while/body/eval_jaxpr/ppermute | solution.py:38
  489.1 7.9 %collective-permute-start.2 = (bf16[4,1152]{1,0:T(4,128)(2,1)S(1)}, bf16[4,1152]{1,0:T(4,128)(2,1)S(1)}, u32[]{:S(2)}, u32[]{:S(2)}) collective-permute-start(bf16[4,1152]{1,0:T(4,128)(2,1)S(1)} %get-tuple-element.787), channel_id=1, source_target_pairs={{0,508},{4,0},{8,4},{12,8},{16,12},{20,16},{24,20},{28,24},{32,28}... | collective-permute-start | bytes 27656 | tf_op jit(solution)/shard_map/while/body/eval_jaxpr/ppermute | solution.py:38
  501.7 7.9 %collective-permute-start.2 = (bf16[4,1152]{1,0:T(4,128)(2,1)S(1)}, bf16[4,1152]{1,0:T(4,128)(2,1)S(1)}, u32[]{:S(2)}, u32[]{:S(2)}) collective-permute-start(bf16[4,1152]{1,0:T(4,128)(2,1)S(1)} %get-tuple-element.787), channel_id=1, source_target_pairs={{0,508},{4,0},{8,4},{12,8},{16,12},{20,16},{24,20},{28,24},{32,28}... | collective-permute-start | bytes 27656 | tf_op jit(solution)/shard_map/while/body/eval_jaxpr/ppermute | solution.py:38
  514.2 7.9 %collective-permute-start.2 = (bf16[4,1152]{1,0:T(4,128)(2,1)S(1)}, bf16[4,1152]{1,0:T(4,128)(2,1)S(1)}, u32[]{:S(2)}, u32[]{:S(2)}) collective-permute-start(bf16[4,1152]{1,0:T(4,128)(2,1)S(1)} %get-tuple-element.787), channel_id=1, source_target_pairs={{0,508},{4,0},{8,4},{12,8},{16,12},{20,16},{24,20},{28,24},{32,28}... | collective-permute-start | bytes 27656 | tf_op jit(solution)/shard_map/while/body/eval_jaxpr/ppermute | solution.py:38
  526.8 7.9 %collective-permute-start.2 = (bf16[4,1152]{1,0:T(4,128)(2,1)S(1)}, bf16[4,1152]{1,0:T(4,128)(2,1)S(1)}, u32[]{:S(2)}, u32[]{:S(2)}) collective-permute-start(bf16[4,1152]{1,0:T(4,128)(2,1)S(1)} %get-tuple-element.787), channel_id=1, source_target_pairs={{0,508},{4,0},{8,4},{12,8},{16,12},{20,16},{24,20},{28,24},{32,28}... | collective-permute-start | bytes 27656 | tf_op jit(solution)/shard_map/while/body/eval_jaxpr/ppermute | solution.py:38
  539.4 7.9 %collective-permute-start.2 = (bf16[4,1152]{1,0:T(4,128)(2,1)S(1)}, bf16[4,1152]{1,0:T(4,128)(2,1)S(1)}, u32[]{:S(2)}, u32[]{:S(2)}) collective-permute-start(bf16[4,1152]{1,0:T(4,128)(2,1)S(1)} %get-tuple-element.787), channel_id=1, source_target_pairs={{0,508},{4,0},{8,4},{12,8},{16,12},{20,16},{24,20},{28,24},{32,28}... | collective-permute-start | bytes 27656 | tf_op jit(solution)/shard_map/while/body/eval_jaxpr/ppermute | solution.py:38
  553.9 6.4 %collective-permute-start.4 = (f32[4,1152]{1,0:T(4,128)S(1)}, f32[4,1152]{1,0:T(4,128)S(1)}, u32[]{:S(2)}, u32[]{:S(2)}) collective-permute-start(f32[4,1152]{1,0:T(4,128)S(1)} %get-tuple-element.496), channel_id=1, source_target_pairs={{0,448},{4,452},{8,456},{12,460},{16,464},{20,468},{24,472},{28,47... | collective-permute-start | bytes 55304 | tf_op jit(solution)/shard_map/ppermute | solution.py:38
  561.1 45.8 %all-to-all-start = ((f32[4,16,288]{2,1,0:T(8,128)}), f32[4,16,288]{2,1,0:T(8,128)S(1)}, u32[]{:S(2)}, u32[]{:S(2)}) async-start(f32[4,16,288]{2,1,0:T(8,128)} %copy.32), calls=%async_computation | async-start | bytes 196608 | tf_op jit(solution)/shard_map/all_to_all | solution.py:48
  607.5 6.6 %all-to-all-done = f32[4,16,288]{2,1,0:T(8,128)S(1)} async-done(((f32[4,16,288]{2,1,0:T(8,128)}), f32[4,16,288]{2,1,0:T(8,128)S(1)}, u32[]{:S(2)}, u32[]{:S(2)}) %all-to-all-start) | async-done | bytes 73760 | tf_op jit(solution)/shard_map/all_to_all | solution.py:48
  (303 shorter events, 159.3 us)
Async XLA Ops:
  140.0 10.4 %collective-permute-start = (bf16[4,1152]{1,0:T(4,128)(2,1)S(1)}, bf16[4,1152]{1,0:T(4,128)(2,1)S(1)}, u32[]{:S(2)}, u32[]{:S(2)}) collective-permute-start(bf16[4,1152]{1,0:T(4,128)(2,1)S(1)} %copy.38), channel_id=1, source_target_pairs={{0,4},{4,8},{8,12},{12,16},{16,20},{20,24},{24,28},{28,32},{32,36}... | collective-permute-start | bytes 27656 | tf_op jit(solution)/shard_map/while/body/eval_jaxpr/ppermute | solution.py:38
  143.9 10.5 %collective-permute-start.1 = (f32[4,1152]{1,0:T(4,128)S(1)}, f32[4,1152]{1,0:T(4,128)S(1)}, u32[]{:S(2)}, u32[]{:S(2)}) collective-permute-start(f32[4,1152]{1,0:T(4,128)S(1)} %convolution_add_fusion.8), channel_id=1, source_target_pairs={{0,4},{4,8},{8,12},{12,16},{16,20},{20,24},{24,28},{28,32},{32,36}... | collective-permute-start | bytes 55304 | tf_op jit(solution)/shard_map/while/body/eval_jaxpr/ppermute | solution.py:38
  154.4 10.4 %collective-permute-start = (bf16[4,1152]{1,0:T(4,128)(2,1)S(1)}, bf16[4,1152]{1,0:T(4,128)(2,1)S(1)}, u32[]{:S(2)}, u32[]{:S(2)}) collective-permute-start(bf16[4,1152]{1,0:T(4,128)(2,1)S(1)} %copy.38), channel_id=1, source_target_pairs={{0,4},{4,8},{8,12},{12,16},{16,20},{20,24},{24,28},{28,32},{32,36}... | collective-permute-start | bytes 27656 | tf_op jit(solution)/shard_map/while/body/eval_jaxpr/ppermute | solution.py:38
  157.3 10.5 %collective-permute-start.1 = (f32[4,1152]{1,0:T(4,128)S(1)}, f32[4,1152]{1,0:T(4,128)S(1)}, u32[]{:S(2)}, u32[]{:S(2)}) collective-permute-start(f32[4,1152]{1,0:T(4,128)S(1)} %convolution_add_fusion.8), channel_id=1, source_target_pairs={{0,4},{4,8},{8,12},{12,16},{16,20},{20,24},{24,28},{28,32},{32,36}... | collective-permute-start | bytes 55304 | tf_op jit(solution)/shard_map/while/body/eval_jaxpr/ppermute | solution.py:38
  167.8 10.4 %collective-permute-start = (bf16[4,1152]{1,0:T(4,128)(2,1)S(1)}, bf16[4,1152]{1,0:T(4,128)(2,1)S(1)}, u32[]{:S(2)}, u32[]{:S(2)}) collective-permute-start(bf16[4,1152]{1,0:T(4,128)(2,1)S(1)} %copy.38), channel_id=1, source_target_pairs={{0,4},{4,8},{8,12},{12,16},{16,20},{20,24},{24,28},{28,32},{32,36}... | collective-permute-start | bytes 27656 | tf_op jit(solution)/shard_map/while/body/eval_jaxpr/ppermute | solution.py:38
  170.7 10.5 %collective-permute-start.1 = (f32[4,1152]{1,0:T(4,128)S(1)}, f32[4,1152]{1,0:T(4,128)S(1)}, u32[]{:S(2)}, u32[]{:S(2)}) collective-permute-start(f32[4,1152]{1,0:T(4,128)S(1)} %convolution_add_fusion.8), channel_id=1, source_target_pairs={{0,4},{4,8},{8,12},{12,16},{16,20},{20,24},{24,28},{28,32},{32,36}... | collective-permute-start | bytes 55304 | tf_op jit(solution)/shard_map/while/body/eval_jaxpr/ppermute | solution.py:38
  181.2 10.4 %collective-permute-start = (bf16[4,1152]{1,0:T(4,128)(2,1)S(1)}, bf16[4,1152]{1,0:T(4,128)(2,1)S(1)}, u32[]{:S(2)}, u32[]{:S(2)}) collective-permute-start(bf16[4,1152]{1,0:T(4,128)(2,1)S(1)} %copy.38), channel_id=1, source_target_pairs={{0,4},{4,8},{8,12},{12,16},{16,20},{20,24},{24,28},{28,32},{32,36}... | collective-permute-start | bytes 27656 | tf_op jit(solution)/shard_map/while/body/eval_jaxpr/ppermute | solution.py:38
  184.0 10.5 %collective-permute-start.1 = (f32[4,1152]{1,0:T(4,128)S(1)}, f32[4,1152]{1,0:T(4,128)S(1)}, u32[]{:S(2)}, u32[]{:S(2)}) collective-permute-start(f32[4,1152]{1,0:T(4,128)S(1)} %convolution_add_fusion.8), channel_id=1, source_target_pairs={{0,4},{4,8},{8,12},{12,16},{16,20},{20,24},{24,28},{28,32},{32,36}... | collective-permute-start | bytes 55304 | tf_op jit(solution)/shard_map/while/body/eval_jaxpr/ppermute | solution.py:38
  194.6 10.4 %collective-permute-start = (bf16[4,1152]{1,0:T(4,128)(2,1)S(1)}, bf16[4,1152]{1,0:T(4,128)(2,1)S(1)}, u32[]{:S(2)}, u32[]{:S(2)}) collective-permute-start(bf16[4,1152]{1,0:T(4,128)(2,1)S(1)} %copy.38), channel_id=1, source_target_pairs={{0,4},{4,8},{8,12},{12,16},{16,20},{20,24},{24,28},{28,32},{32,36}... | collective-permute-start | bytes 27656 | tf_op jit(solution)/shard_map/while/body/eval_jaxpr/ppermute | solution.py:38
  197.4 10.5 %collective-permute-start.1 = (f32[4,1152]{1,0:T(4,128)S(1)}, f32[4,1152]{1,0:T(4,128)S(1)}, u32[]{:S(2)}, u32[]{:S(2)}) collective-permute-start(f32[4,1152]{1,0:T(4,128)S(1)} %convolution_add_fusion.8), channel_id=1, source_target_pairs={{0,4},{4,8},{8,12},{12,16},{16,20},{20,24},{24,28},{28,32},{32,36}... | collective-permute-start | bytes 55304 | tf_op jit(solution)/shard_map/while/body/eval_jaxpr/ppermute | solution.py:38
  208.0 10.4 %collective-permute-start = (bf16[4,1152]{1,0:T(4,128)(2,1)S(1)}, bf16[4,1152]{1,0:T(4,128)(2,1)S(1)}, u32[]{:S(2)}, u32[]{:S(2)}) collective-permute-start(bf16[4,1152]{1,0:T(4,128)(2,1)S(1)} %copy.38), channel_id=1, source_target_pairs={{0,4},{4,8},{8,12},{12,16},{16,20},{20,24},{24,28},{28,32},{32,36}... | collective-permute-start | bytes 27656 | tf_op jit(solution)/shard_map/while/body/eval_jaxpr/ppermute | solution.py:38
  210.8 10.5 %collective-permute-start.1 = (f32[4,1152]{1,0:T(4,128)S(1)}, f32[4,1152]{1,0:T(4,128)S(1)}, u32[]{:S(2)}, u32[]{:S(2)}) collective-permute-start(f32[4,1152]{1,0:T(4,128)S(1)} %convolution_add_fusion.8), channel_id=1, source_target_pairs={{0,4},{4,8},{8,12},{12,16},{16,20},{20,24},{24,28},{28,32},{32,36}... | collective-permute-start | bytes 55304 | tf_op jit(solution)/shard_map/while/body/eval_jaxpr/ppermute | solution.py:38
  221.4 10.4 %collective-permute-start = (bf16[4,1152]{1,0:T(4,128)(2,1)S(1)}, bf16[4,1152]{1,0:T(4,128)(2,1)S(1)}, u32[]{:S(2)}, u32[]{:S(2)}) collective-permute-start(bf16[4,1152]{1,0:T(4,128)(2,1)S(1)} %copy.38), channel_id=1, source_target_pairs={{0,4},{4,8},{8,12},{12,16},{16,20},{20,24},{24,28},{28,32},{32,36}... | collective-permute-start | bytes 27656 | tf_op jit(solution)/shard_map/while/body/eval_jaxpr/ppermute | solution.py:38
  224.2 10.5 %collective-permute-start.1 = (f32[4,1152]{1,0:T(4,128)S(1)}, f32[4,1152]{1,0:T(4,128)S(1)}, u32[]{:S(2)}, u32[]{:S(2)}) collective-permute-start(f32[4,1152]{1,0:T(4,128)S(1)} %convolution_add_fusion.8), channel_id=1, source_target_pairs={{0,4},{4,8},{8,12},{12,16},{16,20},{20,24},{24,28},{28,32},{32,36}... | collective-permute-start | bytes 55304 | tf_op jit(solution)/shard_map/while/body/eval_jaxpr/ppermute | solution.py:38
  234.7 10.4 %collective-permute-start = (bf16[4,1152]{1,0:T(4,128)(2,1)S(1)}, bf16[4,1152]{1,0:T(4,128)(2,1)S(1)}, u32[]{:S(2)}, u32[]{:S(2)}) collective-permute-start(bf16[4,1152]{1,0:T(4,128)(2,1)S(1)} %copy.38), channel_id=1, source_target_pairs={{0,4},{4,8},{8,12},{12,16},{16,20},{20,24},{24,28},{28,32},{32,36}... | collective-permute-start | bytes 27656 | tf_op jit(solution)/shard_map/while/body/eval_jaxpr/ppermute | solution.py:38
  237.6 10.5 %collective-permute-start.1 = (f32[4,1152]{1,0:T(4,128)S(1)}, f32[4,1152]{1,0:T(4,128)S(1)}, u32[]{:S(2)}, u32[]{:S(2)}) collective-permute-start(f32[4,1152]{1,0:T(4,128)S(1)} %convolution_add_fusion.8), channel_id=1, source_target_pairs={{0,4},{4,8},{8,12},{12,16},{16,20},{20,24},{24,28},{28,32},{32,36}... | collective-permute-start | bytes 55304 | tf_op jit(solution)/shard_map/while/body/eval_jaxpr/ppermute | solution.py:38
  248.1 10.4 %collective-permute-start = (bf16[4,1152]{1,0:T(4,128)(2,1)S(1)}, bf16[4,1152]{1,0:T(4,128)(2,1)S(1)}, u32[]{:S(2)}, u32[]{:S(2)}) collective-permute-start(bf16[4,1152]{1,0:T(4,128)(2,1)S(1)} %copy.38), channel_id=1, source_target_pairs={{0,4},{4,8},{8,12},{12,16},{16,20},{20,24},{24,28},{28,32},{32,36}... | collective-permute-start | bytes 27656 | tf_op jit(solution)/shard_map/while/body/eval_jaxpr/ppermute | solution.py:38
  251.0 10.5 %collective-permute-start.1 = (f32[4,1152]{1,0:T(4,128)S(1)}, f32[4,1152]{1,0:T(4,128)S(1)}, u32[]{:S(2)}, u32[]{:S(2)}) collective-permute-start(f32[4,1152]{1,0:T(4,128)S(1)} %convolution_add_fusion.8), channel_id=1, source_target_pairs={{0,4},{4,8},{8,12},{12,16},{16,20},{20,24},{24,28},{28,32},{32,36}... | collective-permute-start | bytes 55304 | tf_op jit(solution)/shard_map/while/body/eval_jaxpr/ppermute | solution.py:38
  261.5 10.6 %collective-permute-start = (bf16[4,1152]{1,0:T(4,128)(2,1)S(1)}, bf16[4,1152]{1,0:T(4,128)(2,1)S(1)}, u32[]{:S(2)}, u32[]{:S(2)}) collective-permute-start(bf16[4,1152]{1,0:T(4,128)(2,1)S(1)} %copy.38), channel_id=1, source_target_pairs={{0,4},{4,8},{8,12},{12,16},{16,20},{20,24},{24,28},{28,32},{32,36}... | collective-permute-start | bytes 27656 | tf_op jit(solution)/shard_map/while/body/eval_jaxpr/ppermute | solution.py:38
  264.4 10.5 %collective-permute-start.1 = (f32[4,1152]{1,0:T(4,128)S(1)}, f32[4,1152]{1,0:T(4,128)S(1)}, u32[]{:S(2)}, u32[]{:S(2)}) collective-permute-start(f32[4,1152]{1,0:T(4,128)S(1)} %convolution_add_fusion.8), channel_id=1, source_target_pairs={{0,4},{4,8},{8,12},{12,16},{16,20},{20,24},{24,28},{28,32},{32,36}... | collective-permute-start | bytes 55304 | tf_op jit(solution)/shard_map/while/body/eval_jaxpr/ppermute | solution.py:38
  274.9 10.4 %collective-permute-start = (bf16[4,1152]{1,0:T(4,128)(2,1)S(1)}, bf16[4,1152]{1,0:T(4,128)(2,1)S(1)}, u32[]{:S(2)}, u32[]{:S(2)}) collective-permute-start(bf16[4,1152]{1,0:T(4,128)(2,1)S(1)} %copy.38), channel_id=1, source_target_pairs={{0,4},{4,8},{8,12},{12,16},{16,20},{20,24},{24,28},{28,32},{32,36}... | collective-permute-start | bytes 27656 | tf_op jit(solution)/shard_map/while/body/eval_jaxpr/ppermute | solution.py:38
  277.8 10.5 %collective-permute-start.1 = (f32[4,1152]{1,0:T(4,128)S(1)}, f32[4,1152]{1,0:T(4,128)S(1)}, u32[]{:S(2)}, u32[]{:S(2)}) collective-permute-start(f32[4,1152]{1,0:T(4,128)S(1)} %convolution_add_fusion.8), channel_id=1, source_target_pairs={{0,4},{4,8},{8,12},{12,16},{16,20},{20,24},{24,28},{28,32},{32,36}... | collective-permute-start | bytes 55304 | tf_op jit(solution)/shard_map/while/body/eval_jaxpr/ppermute | solution.py:38
  288.3 10.4 %collective-permute-start = (bf16[4,1152]{1,0:T(4,128)(2,1)S(1)}, bf16[4,1152]{1,0:T(4,128)(2,1)S(1)}, u32[]{:S(2)}, u32[]{:S(2)}) collective-permute-start(bf16[4,1152]{1,0:T(4,128)(2,1)S(1)} %copy.38), channel_id=1, source_target_pairs={{0,4},{4,8},{8,12},{12,16},{16,20},{20,24},{24,28},{28,32},{32,36}... | collective-permute-start | bytes 27656 | tf_op jit(solution)/shard_map/while/body/eval_jaxpr/ppermute | solution.py:38
  291.2 10.5 %collective-permute-start.1 = (f32[4,1152]{1,0:T(4,128)S(1)}, f32[4,1152]{1,0:T(4,128)S(1)}, u32[]{:S(2)}, u32[]{:S(2)}) collective-permute-start(f32[4,1152]{1,0:T(4,128)S(1)} %convolution_add_fusion.8), channel_id=1, source_target_pairs={{0,4},{4,8},{8,12},{12,16},{16,20},{20,24},{24,28},{28,32},{32,36}... | collective-permute-start | bytes 55304 | tf_op jit(solution)/shard_map/while/body/eval_jaxpr/ppermute | solution.py:38
  301.7 10.4 %collective-permute-start = (bf16[4,1152]{1,0:T(4,128)(2,1)S(1)}, bf16[4,1152]{1,0:T(4,128)(2,1)S(1)}, u32[]{:S(2)}, u32[]{:S(2)}) collective-permute-start(bf16[4,1152]{1,0:T(4,128)(2,1)S(1)} %copy.38), channel_id=1, source_target_pairs={{0,4},{4,8},{8,12},{12,16},{16,20},{20,24},{24,28},{28,32},{32,36}... | collective-permute-start | bytes 27656 | tf_op jit(solution)/shard_map/while/body/eval_jaxpr/ppermute | solution.py:38
  304.6 10.5 %collective-permute-start.1 = (f32[4,1152]{1,0:T(4,128)S(1)}, f32[4,1152]{1,0:T(4,128)S(1)}, u32[]{:S(2)}, u32[]{:S(2)}) collective-permute-start(f32[4,1152]{1,0:T(4,128)S(1)} %convolution_add_fusion.8), channel_id=1, source_target_pairs={{0,4},{4,8},{8,12},{12,16},{16,20},{20,24},{24,28},{28,32},{32,36}... | collective-permute-start | bytes 55304 | tf_op jit(solution)/shard_map/while/body/eval_jaxpr/ppermute | solution.py:38
  315.1 10.4 %collective-permute-start = (bf16[4,1152]{1,0:T(4,128)(2,1)S(1)}, bf16[4,1152]{1,0:T(4,128)(2,1)S(1)}, u32[]{:S(2)}, u32[]{:S(2)}) collective-permute-start(bf16[4,1152]{1,0:T(4,128)(2,1)S(1)} %copy.38), channel_id=1, source_target_pairs={{0,4},{4,8},{8,12},{12,16},{16,20},{20,24},{24,28},{28,32},{32,36}... | collective-permute-start | bytes 27656 | tf_op jit(solution)/shard_map/while/body/eval_jaxpr/ppermute | solution.py:38
  317.9 10.5 %collective-permute-start.1 = (f32[4,1152]{1,0:T(4,128)S(1)}, f32[4,1152]{1,0:T(4,128)S(1)}, u32[]{:S(2)}, u32[]{:S(2)}) collective-permute-start(f32[4,1152]{1,0:T(4,128)S(1)} %convolution_add_fusion.8), channel_id=1, source_target_pairs={{0,4},{4,8},{8,12},{12,16},{16,20},{20,24},{24,28},{28,32},{32,36}... | collective-permute-start | bytes 55304 | tf_op jit(solution)/shard_map/while/body/eval_jaxpr/ppermute | solution.py:38
  328.5 10.4 %collective-permute-start = (bf16[4,1152]{1,0:T(4,128)(2,1)S(1)}, bf16[4,1152]{1,0:T(4,128)(2,1)S(1)}, u32[]{:S(2)}, u32[]{:S(2)}) collective-permute-start(bf16[4,1152]{1,0:T(4,128)(2,1)S(1)} %copy.38), channel_id=1, source_target_pairs={{0,4},{4,8},{8,12},{12,16},{16,20},{20,24},{24,28},{28,32},{32,36}... | collective-permute-start | bytes 27656 | tf_op jit(solution)/shard_map/while/body/eval_jaxpr/ppermute | solution.py:38
  331.3 10.5 %collective-permute-start.1 = (f32[4,1152]{1,0:T(4,128)S(1)}, f32[4,1152]{1,0:T(4,128)S(1)}, u32[]{:S(2)}, u32[]{:S(2)}) collective-permute-start(f32[4,1152]{1,0:T(4,128)S(1)} %convolution_add_fusion.8), channel_id=1, source_target_pairs={{0,4},{4,8},{8,12},{12,16},{16,20},{20,24},{24,28},{28,32},{32,36}... | collective-permute-start | bytes 55304 | tf_op jit(solution)/shard_map/while/body/eval_jaxpr/ppermute | solution.py:38
  341.9 10.4 %collective-permute-start = (bf16[4,1152]{1,0:T(4,128)(2,1)S(1)}, bf16[4,1152]{1,0:T(4,128)(2,1)S(1)}, u32[]{:S(2)}, u32[]{:S(2)}) collective-permute-start(bf16[4,1152]{1,0:T(4,128)(2,1)S(1)} %copy.38), channel_id=1, source_target_pairs={{0,4},{4,8},{8,12},{12,16},{16,20},{20,24},{24,28},{28,32},{32,36}... | collective-permute-start | bytes 27656 | tf_op jit(solution)/shard_map/while/body/eval_jaxpr/ppermute | solution.py:38
  344.7 10.5 %collective-permute-start.1 = (f32[4,1152]{1,0:T(4,128)S(1)}, f32[4,1152]{1,0:T(4,128)S(1)}, u32[]{:S(2)}, u32[]{:S(2)}) collective-permute-start(f32[4,1152]{1,0:T(4,128)S(1)} %convolution_add_fusion.8), channel_id=1, source_target_pairs={{0,4},{4,8},{8,12},{12,16},{16,20},{20,24},{24,28},{28,32},{32,36}... | collective-permute-start | bytes 55304 | tf_op jit(solution)/shard_map/while/body/eval_jaxpr/ppermute | solution.py:38
  355.3 5.3 collective-permute-start.2
  358.6 4.5 collective-permute-start.3
  363.3 9.9 %collective-permute-start.2 = (bf16[4,1152]{1,0:T(4,128)(2,1)S(1)}, bf16[4,1152]{1,0:T(4,128)(2,1)S(1)}, u32[]{:S(2)}, u32[]{:S(2)}) collective-permute-start(bf16[4,1152]{1,0:T(4,128)(2,1)S(1)} %get-tuple-element.787), channel_id=1, source_target_pairs={{0,508},{4,0},{8,4},{12,8},{16,12},{20,16},{24,20},{28,24},{32,28}... | collective-permute-start | bytes 27656 | tf_op jit(solution)/shard_map/while/body/eval_jaxpr/ppermute | solution.py:38
  371.2 4.5 collective-permute-start.3
  375.8 9.9 %collective-permute-start.2 = (bf16[4,1152]{1,0:T(4,128)(2,1)S(1)}, bf16[4,1152]{1,0:T(4,128)(2,1)S(1)}, u32[]{:S(2)}, u32[]{:S(2)}) collective-permute-start(bf16[4,1152]{1,0:T(4,128)(2,1)S(1)} %get-tuple-element.787), channel_id=1, source_target_pairs={{0,508},{4,0},{8,4},{12,8},{16,12},{20,16},{24,20},{28,24},{32,28}... | collective-permute-start | bytes 27656 | tf_op jit(solution)/shard_map/while/body/eval_jaxpr/ppermute | solution.py:38
  383.8 4.5 collective-permute-start.3
  388.4 9.9 %collective-permute-start.2 = (bf16[4,1152]{1,0:T(4,128)(2,1)S(1)}, bf16[4,1152]{1,0:T(4,128)(2,1)S(1)}, u32[]{:S(2)}, u32[]{:S(2)}) collective-permute-start(bf16[4,1152]{1,0:T(4,128)(2,1)S(1)} %get-tuple-element.787), channel_id=1, source_target_pairs={{0,508},{4,0},{8,4},{12,8},{16,12},{20,16},{24,20},{28,24},{32,28}... | collective-permute-start | bytes 27656 | tf_op jit(solution)/shard_map/while/body/eval_jaxpr/ppermute | solution.py:38
  396.4 4.5 collective-permute-start.3
  401.0 9.9 %collective-permute-start.2 = (bf16[4,1152]{1,0:T(4,128)(2,1)S(1)}, bf16[4,1152]{1,0:T(4,128)(2,1)S(1)}, u32[]{:S(2)}, u32[]{:S(2)}) collective-permute-start(bf16[4,1152]{1,0:T(4,128)(2,1)S(1)} %get-tuple-element.787), channel_id=1, source_target_pairs={{0,508},{4,0},{8,4},{12,8},{16,12},{20,16},{24,20},{28,24},{32,28}... | collective-permute-start | bytes 27656 | tf_op jit(solution)/shard_map/while/body/eval_jaxpr/ppermute | solution.py:38
  409.0 4.5 collective-permute-start.3
  413.6 9.9 %collective-permute-start.2 = (bf16[4,1152]{1,0:T(4,128)(2,1)S(1)}, bf16[4,1152]{1,0:T(4,128)(2,1)S(1)}, u32[]{:S(2)}, u32[]{:S(2)}) collective-permute-start(bf16[4,1152]{1,0:T(4,128)(2,1)S(1)} %get-tuple-element.787), channel_id=1, source_target_pairs={{0,508},{4,0},{8,4},{12,8},{16,12},{20,16},{24,20},{28,24},{32,28}... | collective-permute-start | bytes 27656 | tf_op jit(solution)/shard_map/while/body/eval_jaxpr/ppermute | solution.py:38
  421.5 4.5 collective-permute-start.3
  426.2 9.9 %collective-permute-start.2 = (bf16[4,1152]{1,0:T(4,128)(2,1)S(1)}, bf16[4,1152]{1,0:T(4,128)(2,1)S(1)}, u32[]{:S(2)}, u32[]{:S(2)}) collective-permute-start(bf16[4,1152]{1,0:T(4,128)(2,1)S(1)} %get-tuple-element.787), channel_id=1, source_target_pairs={{0,508},{4,0},{8,4},{12,8},{16,12},{20,16},{24,20},{28,24},{32,28}... | collective-permute-start | bytes 27656 | tf_op jit(solution)/shard_map/while/body/eval_jaxpr/ppermute | solution.py:38
  434.1 4.5 collective-permute-start.3
  438.8 9.9 %collective-permute-start.2 = (bf16[4,1152]{1,0:T(4,128)(2,1)S(1)}, bf16[4,1152]{1,0:T(4,128)(2,1)S(1)}, u32[]{:S(2)}, u32[]{:S(2)}) collective-permute-start(bf16[4,1152]{1,0:T(4,128)(2,1)S(1)} %get-tuple-element.787), channel_id=1, source_target_pairs={{0,508},{4,0},{8,4},{12,8},{16,12},{20,16},{24,20},{28,24},{32,28}... | collective-permute-start | bytes 27656 | tf_op jit(solution)/shard_map/while/body/eval_jaxpr/ppermute | solution.py:38
  446.7 4.5 collective-permute-start.3
  451.3 9.9 %collective-permute-start.2 = (bf16[4,1152]{1,0:T(4,128)(2,1)S(1)}, bf16[4,1152]{1,0:T(4,128)(2,1)S(1)}, u32[]{:S(2)}, u32[]{:S(2)}) collective-permute-start(bf16[4,1152]{1,0:T(4,128)(2,1)S(1)} %get-tuple-element.787), channel_id=1, source_target_pairs={{0,508},{4,0},{8,4},{12,8},{16,12},{20,16},{24,20},{28,24},{32,28}... | collective-permute-start | bytes 27656 | tf_op jit(solution)/shard_map/while/body/eval_jaxpr/ppermute | solution.py:38
  459.3 4.5 collective-permute-start.3
  463.9 9.9 %collective-permute-start.2 = (bf16[4,1152]{1,0:T(4,128)(2,1)S(1)}, bf16[4,1152]{1,0:T(4,128)(2,1)S(1)}, u32[]{:S(2)}, u32[]{:S(2)}) collective-permute-start(bf16[4,1152]{1,0:T(4,128)(2,1)S(1)} %get-tuple-element.787), channel_id=1, source_target_pairs={{0,508},{4,0},{8,4},{12,8},{16,12},{20,16},{24,20},{28,24},{32,28}... | collective-permute-start | bytes 27656 | tf_op jit(solution)/shard_map/while/body/eval_jaxpr/ppermute | solution.py:38
  471.9 4.5 collective-permute-start.3
  476.5 9.9 %collective-permute-start.2 = (bf16[4,1152]{1,0:T(4,128)(2,1)S(1)}, bf16[4,1152]{1,0:T(4,128)(2,1)S(1)}, u32[]{:S(2)}, u32[]{:S(2)}) collective-permute-start(bf16[4,1152]{1,0:T(4,128)(2,1)S(1)} %get-tuple-element.787), channel_id=1, source_target_pairs={{0,508},{4,0},{8,4},{12,8},{16,12},{20,16},{24,20},{28,24},{32,28}... | collective-permute-start | bytes 27656 | tf_op jit(solution)/shard_map/while/body/eval_jaxpr/ppermute | solution.py:38
  484.5 4.5 collective-permute-start.3
  489.1 9.9 %collective-permute-start.2 = (bf16[4,1152]{1,0:T(4,128)(2,1)S(1)}, bf16[4,1152]{1,0:T(4,128)(2,1)S(1)}, u32[]{:S(2)}, u32[]{:S(2)}) collective-permute-start(bf16[4,1152]{1,0:T(4,128)(2,1)S(1)} %get-tuple-element.787), channel_id=1, source_target_pairs={{0,508},{4,0},{8,4},{12,8},{16,12},{20,16},{24,20},{28,24},{32,28}... | collective-permute-start | bytes 27656 | tf_op jit(solution)/shard_map/while/body/eval_jaxpr/ppermute | solution.py:38
  497.0 4.5 collective-permute-start.3
  501.7 9.9 %collective-permute-start.2 = (bf16[4,1152]{1,0:T(4,128)(2,1)S(1)}, bf16[4,1152]{1,0:T(4,128)(2,1)S(1)}, u32[]{:S(2)}, u32[]{:S(2)}) collective-permute-start(bf16[4,1152]{1,0:T(4,128)(2,1)S(1)} %get-tuple-element.787), channel_id=1, source_target_pairs={{0,508},{4,0},{8,4},{12,8},{16,12},{20,16},{24,20},{28,24},{32,28}... | collective-permute-start | bytes 27656 | tf_op jit(solution)/shard_map/while/body/eval_jaxpr/ppermute | solution.py:38
  509.6 4.5 collective-permute-start.3
  514.2 9.9 %collective-permute-start.2 = (bf16[4,1152]{1,0:T(4,128)(2,1)S(1)}, bf16[4,1152]{1,0:T(4,128)(2,1)S(1)}, u32[]{:S(2)}, u32[]{:S(2)}) collective-permute-start(bf16[4,1152]{1,0:T(4,128)(2,1)S(1)} %get-tuple-element.787), channel_id=1, source_target_pairs={{0,508},{4,0},{8,4},{12,8},{16,12},{20,16},{24,20},{28,24},{32,28}... | collective-permute-start | bytes 27656 | tf_op jit(solution)/shard_map/while/body/eval_jaxpr/ppermute | solution.py:38
  526.8 9.9 %collective-permute-start.2 = (bf16[4,1152]{1,0:T(4,128)(2,1)S(1)}, bf16[4,1152]{1,0:T(4,128)(2,1)S(1)}, u32[]{:S(2)}, u32[]{:S(2)}) collective-permute-start(bf16[4,1152]{1,0:T(4,128)(2,1)S(1)} %get-tuple-element.787), channel_id=1, source_target_pairs={{0,508},{4,0},{8,4},{12,8},{16,12},{20,16},{24,20},{28,24},{32,28}... | collective-permute-start | bytes 27656 | tf_op jit(solution)/shard_map/while/body/eval_jaxpr/ppermute | solution.py:38
  539.4 9.9 %collective-permute-start.2 = (bf16[4,1152]{1,0:T(4,128)(2,1)S(1)}, bf16[4,1152]{1,0:T(4,128)(2,1)S(1)}, u32[]{:S(2)}, u32[]{:S(2)}) collective-permute-start(bf16[4,1152]{1,0:T(4,128)(2,1)S(1)} %get-tuple-element.787), channel_id=1, source_target_pairs={{0,508},{4,0},{8,4},{12,8},{16,12},{20,16},{24,20},{28,24},{32,28}... | collective-permute-start | bytes 27656 | tf_op jit(solution)/shard_map/while/body/eval_jaxpr/ppermute | solution.py:38
  552.0 54.8 %collective-permute-start.5 = (f32[4,1152]{1,0:T(4,128)S(1)}, f32[4,1152]{1,0:T(4,128)S(1)}, u32[]{:S(2)}, u32[]{:S(2)}) collective-permute-start(f32[4,1152]{1,0:T(4,128)S(1)} %get-tuple-element.497), channel_id=1, source_target_pairs={{0,64},{4,68},{8,72},{12,76},{16,80},{20,84},{24,88},{28,92},{32,9... | collective-permute-start | bytes 55304 | tf_op jit(solution)/shard_map/ppermute | solution.py:38
  553.9 52.9 %collective-permute-start.4 = (f32[4,1152]{1,0:T(4,128)S(1)}, f32[4,1152]{1,0:T(4,128)S(1)}, u32[]{:S(2)}, u32[]{:S(2)}) collective-permute-start(f32[4,1152]{1,0:T(4,128)S(1)} %get-tuple-element.496), channel_id=1, source_target_pairs={{0,448},{4,452},{8,456},{12,460},{16,464},{20,468},{24,472},{28,47... | collective-permute-start | bytes 55304 | tf_op jit(solution)/shard_map/ppermute | solution.py:38
  561.1 53.0 %all-to-all-start = ((f32[4,16,288]{2,1,0:T(8,128)}), f32[4,16,288]{2,1,0:T(8,128)S(1)}, u32[]{:S(2)}, u32[]{:S(2)}) async-start(f32[4,16,288]{2,1,0:T(8,128)} %copy.32), calls=%async_computation | async-start | bytes 196608 | tf_op jit(solution)/shard_map/all_to_all | solution.py:48
  (10 other events, 390.7 us)
where the time goes:
time: 618 us; the launch traced here: 615 us
  starting transfers between devices  269 us (44%)
  waiting for transfers between devices  165 us (27%)
  blocking collectives  133 us (22%)
  matrix products  36.3 us (6%)
    ppermute x66, starting transfers between devices, from_behind(): return lax.ppermute(value, axis, pairs)  223 us
    ppermute x66, waiting for transfers between devices, from_behind(): return lax.ppermute(value, axis, pairs)  158 us
    all_gather x10, blocking collectives, stacked_from(): pieces = lax.all_gather(pieces, axes[k], axis=0, tiled=True)  133 us
    all_to_all x1, starting transfers between devices, sent_and_summed(): lax.all_to_all(pieces, axis, split_axis=0, concat_axis=0, tiled=True)  45.8 us
    dot_general x32, matrix products, block_update(): lax.dot_general(image, text, (((1,), (1,)), ((), ())), preferred_element_...  24.9 us
  transfers between devices with their start and end apart: 67, of which 49 were waited for; matrix products, arithmetic and copies ran while one was open for 6% of the time, Pallas kernels for 0%

commit v1 on v0

v1 whole, which is shorter than its diff:
```python
import jax
import jax.numpy as jnp
from jax import lax
from jax.experimental import pallas as pl
from jax.experimental.pallas import tpu as pltpu
from jax.sharding import Mesh
from jax.sharding import PartitionSpec as P

BATCH = ("x", "y", "z")
MP = ("m0", "m1")
bf16 = jnp.bfloat16
f32 = jnp.float32
epsilon = 1e-06
DELTA = (-2, -1, 1, 2)


def call(body, out_shape, scratch, *args, smem=()):
    specs = [
        pl.BlockSpec(memory_space=pltpu.SMEM if k in smem else pltpu.VMEM)
        for k in range(len(args))
    ]
    outs = jax.tree.map(lambda _: pl.BlockSpec(memory_space=pltpu.VMEM), out_shape)
    return pl.pallas_call(
        body, out_shape=out_shape, in_specs=specs, out_specs=outs, scratch_shapes=scratch
    )(*args)


def project(w_ref, left_ref, own_ref, right_ref, out_ref):
    r = lax.broadcasted_iota(jnp.int32, (384, 384), 0)
    c = lax.broadcasted_iota(jnp.int32, (384, 384), 1)
    second = r >= 192
    k = jnp.where(second, r - 192, r)
    source = k + 12 * ((k * 171) >> 11) + jnp.where(second, 12, 0)
    sort = jnp.where(c == source, 1.0, 0.0).astype(bf16)
    half_a = jnp.dot(sort, w_ref[0:384, :], preferred_element_type=f32).astype(bf16)
    half_b = jnp.dot(sort, w_ref[384:768, :], preferred_element_type=f32).astype(bf16)
    blocks = [left_ref[0], left_ref[1]] + [own_ref[k] for k in range(4)]
    blocks += [right_ref[0], right_ref[1]]
    parts = []
    for which in range(2):
        rows = jnp.concatenate([b[16 * which : 16 * which + 16] for b in blocks], axis=0)
        part = jnp.dot(
            rows[:, 0:192], half_a[192 * which : 192 * which + 192], preferred_element_type=f32
        ) + jnp.dot(
            rows[:, 192:384], half_b[192 * which : 192 * which + 192], preferred_element_type=f32
        )
        parts.append(part.astype(bf16))
    for y in range(4):
        for m in range(4):
            for place, block in enumerate((y + 2, y + 2 + DELTA[m])):
                for which in range(2):
                    start = 32 * place + 16 * which
                    out_ref[4 * y + m, start : start + 16, :] = parts[which][
                        16 * block : 16 * block + 16
                    ]


def embed(where_ref, got_ref, pair_ref, own_ref, out_ref, rows_ref):
    z = where_ref[1]
    m = where_ref[2]
    pres = []
    total = None
    for col in range(4):
        pre = got_ref[col].astype(f32)
        for part in range(1, 4):
            pre = pre + got_ref[4 * part + col].astype(f32)
        pre = pre.astype(bf16).astype(f32)
        square = jnp.sum(pre * pre, axis=1, keepdims=True)
        total = square if total is None else total + square
        pres.append(pre)
    norm = lax.rsqrt(total + epsilon)
    for col in range(4):
        rows_ref[:, 288 * col : 288 * col + 288] = (pres[col] * norm).astype(bf16)
    for place in range(2):
        high = jnp.broadcast_to(pair_ref[place, 0:1, :], (8, 128))
        low = jnp.broadcast_to(pair_ref[place, 1:2, :], (8, 128))
        tile = jnp.concatenate([high, low], axis=0).astype(bf16)
        rows_ref[32 * place : 32 * place + 16, 1152:1280] = tile
        rows_ref[32 * place + 16 : 32 * place + 32, 1152:1280] = jnp.zeros((16, 128), bf16)
    own_ref[...] = rows_ref[0:32, 0:1152]
    middle = (m == 1) | (m == 2)
    for to in range(8):
        other_img = middle | ((m == 0) & (z >= to)) | ((m == 3) & (z < to))
        other_txt = middle | ((m == 0) & (z > to)) | ((m == 3) & (z <= to))
        at = pl.multiple_of(jnp.where(other_img, 32, 0), 32)
        out_ref[to, 0:16, :] = rows_ref[pl.ds(at, 16), :]
        at = pl.multiple_of(jnp.where(other_txt, 48, 16), 16)
        out_ref[to, 16:32, :] = rows_ref[pl.ds(at, 16), :]


def score(where_ref, scale_ref, bias_ref, pair_ref, own_ref, got_ref, out_ref):
    octet = where_ref[0]
    z = where_ref[1]
    m = where_ref[2]
    scale = jnp.exp(jnp.full((16, 128), scale_ref[0], f32))
    scale_one = scale[:, 0:1]
    offset = bias_ref[0]
    imgs = jnp.concatenate([got_ref[k, 0:16, 0:1152] for k in range(8)], axis=0)
    txts = jnp.concatenate([got_ref[k, 16:32, 0:1152] for k in range(8)], axis=0)
    codes = got_ref[0, 0:16, 1152:1280].astype(f32)
    for k in range(1, 8):
        codes = codes + got_ref[k, 0:16, 1152:1280].astype(f32)
    pair_window = codes[0:1] * 64.0 + codes[8:9]
    lane = lax.broadcasted_iota(jnp.int32, (16, 128), 1)
    row = lax.broadcasted_iota(jnp.int32, (16, 128), 0)
    there = lane >> 4
    behind = jnp.where(there > z, -2, 0)
    ahead = jnp.where(there > z, 0, 2)
    delta = jnp.where(m == 0, behind, jnp.where(m == 3, ahead, jnp.where(m == 1, -1, 1)))
    block = (8 * (octet + delta) + there) & 127
    text_index = block * 16 + (lane & 15)
    match_img = pair_ref[...] == text_index
    own_text = (octet * 8 + z) * 16 + row
    match_txt = pair_window == own_text.astype(f32)

    def grads(own, window, match):
        scores = lax.dot_general(own, window, (((1,), (1,)), ((), ())), preferred_element_type=f32)
        logits = scale * scores + offset
        label = jnp.where(match, 1.0, -1.0)
        coef = (-label / (1.0 + jnp.exp(label * logits))).astype(bf16)
        return scale_one * jnp.dot(coef, window, preferred_element_type=f32)

    image_part = grads(own_ref[0:16, :], txts, match_img)
    text_part = grads(own_ref[16:32, :], imgs, match_txt)
    for to in range(4):
        out_ref[to, 0:16, :] = image_part[:, 288 * to : 288 * to + 288].astype(out_ref.dtype)
        rows = text_part[4 * to : 4 * to + 4]
        out_ref[to, 16:32, :] = jnp.concatenate(
            [rows[:, 288 * c : 288 * c + 288] for c in range(4)], axis=0
        ).astype(out_ref.dtype)


def finish(got_ref, image_ref, text_ref):
    total = got_ref[0].astype(f32)
    for k in range(1, 4):
        total = total + got_ref[k].astype(f32)
    image_ref[...] = total[0:16]
    for c in range(4):
        text_ref[:, 288 * c : 288 * c + 288] = total[16 + 4 * c : 20 + 4 * c]


def exchange(value, axes):
    return lax.all_to_all(value, axes, split_axis=0, concat_axis=0, tiled=True)


def local(img_feat, txt_feat, w_img, w_txt, pair_index, log_scale, bias):
    x, y, z = (lax.axis_index(a) for a in BATCH)
    m = lax.axis_index(MP)
    octet = 4 * x + y
    where = jnp.stack([octet, z, m]).astype(jnp.int32)

    lane = jnp.arange(384, dtype=jnp.int32)
    spread = jnp.tile(pair_index, 24)
    here = (lane // 16) == z
    codes = jnp.stack([jnp.where(here, spread // 64, 0), jnp.where(here, spread % 64, 0)])
    codes = jnp.concatenate([codes.astype(bf16), jnp.zeros((6, 384), bf16)], axis=0)
    feats = jnp.concatenate([img_feat, txt_feat], axis=0).reshape(32, 4, 4, 96)
    feats = feats.transpose(2, 0, 1, 3).reshape(4, 32, 384)
    sent = jnp.concatenate([feats, jnp.broadcast_to(codes, (4, 8, 384))], axis=1)
    own = exchange(sent, "y")
    up = [(s, (s + 1) % 4) for s in range(4)]
    down = [(s, (s - 1) % 4) for s in range(4)]
    left = lax.ppermute(own[2:4], "x", up)
    right = lax.ppermute(own[0:2], "x", down)

    weights = jnp.concatenate([w_img, w_txt], axis=0)
    weights = exchange(jnp.broadcast_to(weights, (32, 24, 288)), ("x", "z"))
    weights = weights.reshape(768, 288)

    sent = call(
        project, jax.ShapeDtypeStruct((16, 64, 288), bf16), [], weights, left, own, right
    )
    got = exchange(sent, ("y",) + MP)

    codes = jnp.concatenate([a[:, 32:34, 0:128] for a in (left, own, right)], axis=0)
    codes = codes.astype(f32)
    delta = jnp.where(m < 2, m - 2, m - 1)
    pairs = jnp.concatenate(
        [
            lax.dynamic_slice_in_dim(codes, y + 2, 1, 0),
            lax.dynamic_slice_in_dim(codes, y + 2 + delta, 1, 0),
        ],
        axis=0,
    )
    mine, sent = call(
        embed,
        (jax.ShapeDtypeStruct((32, 1152), bf16), jax.ShapeDtypeStruct((8, 32, 1280), bf16)),
        [pltpu.VMEM((64, 1280), bf16)],
        where,
        got,
        pairs,
        smem=(0,),
    )
    got = exchange(sent, "z")
    sent = call(
        score,
        jax.ShapeDtypeStruct((4, 32, 288), f32),
        [],
        where,
        log_scale,
        bias,
        pair_index.reshape(16, 1),
        mine,
        got,
        smem=(0, 1, 2),
    )
    got = exchange(sent, MP)
    return call(
        finish,
        (jax.ShapeDtypeStruct((16, 288), f32), jax.ShapeDtypeStruct((4, 1152), f32)),
        [],
        got,
    )


def solution(mesh):
    finer = Mesh(mesh.devices.reshape(4, 4, 8, 2, 2), BATCH + MP)
    in_specs = (P(BATCH, None), P(BATCH, None), P(BATCH, MP), P(BATCH, MP), P(BATCH), P(), P())
    out_specs = (P(BATCH, MP), P(BATCH + MP, None))
    return jax.shard_map(local, mesh=finer, in_specs=in_specs, out_specs=out_specs, check_vma=False)
```

time: 618 us -> 126 us (0.20)
  starting transfers between devices: 269 us -> 40.3 us
  blocking collectives: 133 us -> 13 us
  waiting for transfers between devices: 165 us -> 49.7 us
  matrix products: 36.3 us -> 0 us
  Pallas kernels: 0 us -> 9.61 us
    ppermute x66 -> x2, starting transfers between devices: 223 us -> 6.49 us  [the longest x1 3.35 us: local(): right = lax.ppermute(own[0:2], 'x', down)]
    ppermute x66 -> x2, waiting for transfers between devices: 158 us -> 1.93 us  [the longest x1 1.09 us: local(): left = lax.ppermute(own[2:4], 'x', up)]
    all_gather x10 -> x0, blocking collectives: 133 us -> none  [stacked_from(): pieces = lax.all_gather(pieces, axes[k], axis=0, tiled=True)]
    all_to_all x1 -> x4, waiting for transfers between devices: 6.63 us -> 47.8 us  [exchange(): return lax.all_to_all(value, axes, split_axis=0, concat_axis=0, tiled=True)]
    dot_general x98 -> x0, matrix products: 36.3 us -> none  [the longest x32 24.9 us: block_update(): lax.dot_general(image, text, (((1,), (1,)), ((), ())), preferred_element_...]
    all_to_all x0 -> x1, blocking collectives: none -> 13 us  [exchange(): return lax.all_to_all(value, axes, split_axis=0, concat_axis=0, tiled=True)]
    all_to_all x1 -> x4, starting transfers between devices: 45.8 us -> 33.8 us  [exchange(): return lax.all_to_all(value, axes, split_axis=0, concat_axis=0, tiled=True)]
    pallas_call x0 -> x4, Pallas kernels: none -> 9.61 us  [call(): pl.pallas_call(body, out_shape=out_shape, in_specs=specs, out_specs=outs,...]
  transfers between devices with their start and end apart: 67 -> 6, of which waited for: 49 -> 6; matrix products, arithmetic and copies ran while one was open for 6% -> 3% of each run, Pallas kernels for 0% -> 0%
where the time goes in v1:
time: 126 us; the launch traced here: 125 us
  waiting for transfers between devices  49.7 us (39%)
  starting transfers between devices  40.3 us (32%)
  blocking collectives  13 us (10%)
  Pallas kernels  9.61 us (8%)
  local copies, waits for them, and re-layouts  7.34 us (6%)
  other arithmetic  2.78 us (2%)
  between operations  2.06 us (2%)
    all_to_all x4, waiting for transfers between devices, exchange(): return lax.all_to_all(value, axes, split_axis=0, concat_axis=0, tiled=True)  47.8 us
    all_to_all x4, starting transfers between devices, exchange(): return lax.all_to_all(value, axes, split_axis=0, concat_axis=0, tiled=True)  33.8 us
    all_to_all x1, blocking collectives, exchange(): return lax.all_to_all(value, axes, split_axis=0, concat_axis=0, tiled=True)  13 us
    pallas_call x4, Pallas kernels, call(): pl.pallas_call(body, out_shape=out_shape, in_specs=specs, out_specs=outs,...  9.61 us
    ppermute x1, starting transfers between devices, local(): right = lax.ppermute(own[0:2], 'x', down)  3.35 us
    unnamed x18, local copies, waits for them, and re-layouts  3.28 us
    ppermute x1, starting transfers between devices, local(): left = lax.ppermute(own[2:4], 'x', up)  3.14 us
  transfers between devices with their start and end apart: 6, of which 6 were waited for; matrix products, arithmetic and copies ran while one was open for 3% of the time, Pallas kernels for 0%

profile of v1, /device:TPU:1, one launch (start us, length us, event | category | flops | bytes accessed | tf_op | source)
XLA Modules:
  0.0 124.7 jit_solution(9822979116126285668)
XLA Ops:
  0.6 0.0 copy-start.8
  0.6 0.6 copy-done.8
  1.3 0.1 tile.10
  1.4 0.8 pad_maximum_fusion.1
  2.2 0.1 reshape.165
  2.4 0.1 copy.14
  2.4 0.1 reshape.166
  2.6 0.7 pad_maximum_fusion
  3.3 0.0 copy-start.6
  3.3 0.0 copy-start.7
  3.3 5.5 %all-to-all-start.1 = ((bf16[4,40,384]{2,1,0:T(8,128)(2,1)}), bf16[4,40,384]{2,1,0:T(8,128)(2,1)S(1)}, u32[]{:S(2)}, u32[]{:S(2)}) async-start(bf16[4,40,384]{2,1,0:T(8,128)(2,1)} %pad_maximum_fusion), calls=%async_computation.1 | async-start | bytes 245760 | tf_op jit(solution)/shard_map/all_to_all | solution.py:143
  8.8 0.0 copy-done.6
  8.8 0.0 copy-done.7
  8.8 4.7 %all-to-all-done.1.own_ref = bf16[4,40,384]{2,1,0:T(8,128)(2,1)S(1)} async-done(((bf16[4,40,384]{2,1,0:T(8,128)(2,1)}), bf16[4,40,384]{2,1,0:T(8,128)(2,1)S(1)}, u32[]{:S(2)}, u32[]{:S(2)}) %all-to-all-start.1) | async-done | bytes 122912 | tf_op jit(solution)/shard_map/all_to_all | solution.py:143
  13.6 0.0 copy-start.3
  13.6 0.9 broadcast_in_dim.10
  14.4 12.9 %all-to-all-start = ((bf16[32,24,288]{2,1,0:T(8,128)(2,1)}), bf16[32,24,288]{2,1,0:T(8,128)(2,1)S(1)}, u32[]{:S(2)}, u32[]{:S(2)}) async-start(bf16[32,24,288]{2,1,0:T(8,128)(2,1)} %broadcast_in_dim.10), calls=%async_computation | async-start | bytes 1179648 | tf_op jit(solution)/shard_map/all_to_all | solution.py:143
  27.3 0.0 copy-done.3
  27.4 3.1 %collective-permute-start = (bf16[2,40,384]{2,1,0:T(8,128)(2,1)S(1)}, bf16[2,40,384]{2,1,0:T(8,128)(2,1)S(1)}, u32[]{:S(2)}, u32[]{:S(2)}) collective-permute-start(bf16[2,40,384]{2,1,0:T(8,128)(2,1)S(1)} %get-tuple-element.7), channel_id=1, source_target_pairs={{0,128},{128,256},{256,384},{384,0},{1,129},{129,257},{257,385},{3... | collective-permute-start | bytes 184328 | tf_op jit(solution)/shard_map/ppermute | solution.py:163
  30.5 3.4 %collective-permute-start.1 = (bf16[2,40,384]{2,1,0:T(8,128)(2,1)S(1)}, bf16[2,40,384]{2,1,0:T(8,128)(2,1)S(1)}, u32[]{:S(2)}, u32[]{:S(2)}) collective-permute-start(bf16[2,40,384]{2,1,0:T(8,128)(2,1)S(1)} %get-tuple-element.6), channel_id=1, source_target_pairs={{0,384},{128,0},{256,128},{384,256},{1,385},{129,1},{257,129},{385... | collective-permute-start | bytes 184328 | tf_op jit(solution)/shard_map/ppermute | solution.py:164
  33.9 1.1 collective-permute-done.left_ref
  35.0 0.0 copy-start.4
  35.0 0.8 collective-permute-done.1.right_ref
  35.8 0.0 copy-start.5
  35.8 5.3 %all-to-all-done = bf16[32,24,288]{2,1,0:T(8,128)(2,1)S(1)} async-done(((bf16[32,24,288]{2,1,0:T(8,128)(2,1)}), bf16[32,24,288]{2,1,0:T(8,128)(2,1)S(1)}, u32[]{:S(2)}, u32[]{:S(2)}) %all-to-all-start) | async-done | bytes 442400 | tf_op jit(solution)/shard_map/all_to_all | solution.py:143
  41.1 0.0 copy-start.2
  41.1 0.0 copy-done.4
  41.1 0.0 copy-done.5
  41.1 0.8 copy-done.2
  42.0 2.8 %shard_map.86 = bf16[16,64,288]{2,1,0:T(8,128)(2,1)} custom-call(bf16[768,288]{1,0:T(8,128)(2,1)} %bitcast.8, bf16[2,40,384]{2,1,0:T(8,128)(2,1)} %copy-done.4, bf16[4,40,384]{2,1,0:T(8,128)(2,1)} %copy-done.3, bf16[2,40,384]{2,1,0:T(8,128)(2,1)} %copy-done.5), custom_call_target="tpu_custom_call" | custom-call | tf_op jit(solution)/shard_map/pallas_call | solution.py:23
  44.8 11.6 %all-to-all-start.2 = ((bf16[16,64,288]{2,1,0:T(8,128)(2,1)}), bf16[16,64,288]{2,1,0:T(8,128)(2,1)S(1)}, u32[]{:S(2)}, u32[]{:S(2)}) async-start(bf16[16,64,288]{2,1,0:T(8,128)(2,1)} %shard_map.86), calls=%async_computation.2 | async-start | bytes 1572864 | tf_op jit(solution)/shard_map/all_to_all | solution.py:143
  56.4 0.7 pad_add_fusion.where_ref
  57.0 0.7 slice.23
  57.7 0.7 slice.22
  58.4 0.7 slice.24
  59.1 0.6 pad_maximum_fusion.3.pair_ref
  59.7 18.9 %all-to-all-done.2.got_ref = bf16[16,64,288]{2,1,0:T(8,128)(2,1)S(1)} async-done(((bf16[16,64,288]{2,1,0:T(8,128)(2,1)}), bf16[16,64,288]{2,1,0:T(8,128)(2,1)S(1)}, u32[]{:S(2)}, u32[]{:S(2)}) %all-to-all-start.2) | async-done | bytes 589856 | tf_op jit(solution)/shard_map/all_to_all | solution.py:143
  78.6 0.0 copy-start
  78.6 0.9 copy-done
  79.5 2.5 %shard_map.87 = (bf16[32,1152]{1,0:T(8,128)(2,1)}, bf16[8,32,1280]{2,1,0:T(8,128)(2,1)}) custom-call(s32[3]{0:T(128)} %pad_add_fusion.where_ref, bf16[16,64,288]{2,1,0:T(8,128)(2,1)} %copy-done, f32[2,2,128]{2,1,0:T(2,128)} %pad_maximum_fusion.3.pair_ref), custom_call_target="tpu_custom_call" | custom-call | tf_op jit(solution)/shard_map/pallas_call | solution.py:23
  81.9 3.8 %all-to-all-start.3 = ((bf16[8,32,1280]{2,1,0:T(8,128)(2,1)}), bf16[8,32,1280]{2,1,0:T(8,128)(2,1)S(1)}, u32[]{:S(2)}, u32[]{:S(2)}) async-start(bf16[8,32,1280]{2,1,0:T(8,128)(2,1)} %get-tuple-element.5), calls=%async_computation.3 | async-start | bytes 1310720 | tf_op jit(solution)/shard_map/all_to_all | solution.py:143
  85.7 0.7 copy.12.pair_ref
  87.7 18.8 %all-to-all-done.3.got_ref = bf16[8,32,1280]{2,1,0:T(8,128)(2,1)S(1)} async-done(((bf16[8,32,1280]{2,1,0:T(8,128)(2,1)}), bf16[8,32,1280]{2,1,0:T(8,128)(2,1)S(1)}, u32[]{:S(2)}, u32[]{:S(2)}) %all-to-all-start.3) | async-done | bytes 655392 | tf_op jit(solution)/shard_map/all_to_all | solution.py:143
  106.5 0.0 copy-start.1
  106.5 0.9 copy-done.1
  107.4 2.8 %shard_map.88 = f32[4,32,288]{2,1,0:T(8,128)} custom-call(s32[3]{0:T(128)} %pad_add_fusion.where_ref, f32[1]{0:T(128)S(6)} %copy.15.scale_ref, f32[1]{0:T(128)S(6)} %copy.16.bias_ref, s32[16,1]{1,0:T(8,128)} %copy.12.pair_ref, bf16[32,1152]{1,0:T(8,128)(2,1)} %get-tuple-element.4.own_ref, bf16[8,32,1280]{2,1,0:T(8,128)(2,1)} %copy-done.1), custom_call_target="tpu_custom_call" | custom-call | tf_op jit(solution)/shard_map/pallas_call | solution.py:23
  110.1 13.0 %all_to_all.25.got_ref = f32[4,32,288]{2,1,0:T(8,128)} all-to-all(f32[4,32,288]{2,1,0:T(8,128)} %shard_map.88), channel_id=1, replica_groups=mesh['x'=4,'y'=4,'z'=8,'m0'=2,'m1'=2] {'m0','m1'}, dimensions={0} | all-to-all | bytes 294912 | tf_op jit(solution)/shard_map/all_to_all | solution.py:143
  123.1 1.6 %shard_map.89 = (f32[16,288]{1,0:T(8,128)}, f32[4,1152]{1,0:T(4,128)}) custom-call(f32[4,32,288]{2,1,0:T(8,128)} %all_to_all.25.got_ref), custom_call_target="tpu_custom_call" | custom-call | tf_op jit(solution)/shard_map/pallas_call | solution.py:23
  (8 shorter events, 0.1 us)
Async XLA Ops:
  0.6 0.7 copy-start.8
  3.3 5.5 %copy-start.6 = (bf16[12,288]{1,0:T(8,128)(2,1)S(1)}, bf16[12,288]{1,0:T(8,128)(2,1)}, u32[]{:S(2)}) copy-start(bf16[12,288]{1,0:T(8,128)(2,1)} %param.10) | copy-start | bytes 20740
  3.3 5.5 %copy-start.7 = (bf16[12,288]{1,0:T(8,128)(2,1)S(1)}, bf16[12,288]{1,0:T(8,128)(2,1)}, u32[]{:S(2)}) copy-start(bf16[12,288]{1,0:T(8,128)(2,1)} %param.9) | copy-start | bytes 20740
  3.3 10.3 %all-to-all-start.1 = ((bf16[4,40,384]{2,1,0:T(8,128)(2,1)}), bf16[4,40,384]{2,1,0:T(8,128)(2,1)S(1)}, u32[]{:S(2)}, u32[]{:S(2)}) async-start(bf16[4,40,384]{2,1,0:T(8,128)(2,1)} %pad_maximum_fusion), calls=%async_computation.1 | async-start | bytes 245760 | tf_op jit(solution)/shard_map/all_to_all | solution.py:143
  13.6 13.8 %copy-start.3 = (bf16[4,40,384]{2,1,0:T(8,128)(2,1)}, bf16[4,40,384]{2,1,0:T(8,128)(2,1)S(1)}, u32[]{:S(2)}) copy-start(bf16[4,40,384]{2,1,0:T(8,128)(2,1)S(1)} %all-to-all-done.1.own_ref) | copy-start | bytes 368644
  14.4 26.7 %all-to-all-start = ((bf16[32,24,288]{2,1,0:T(8,128)(2,1)}), bf16[32,24,288]{2,1,0:T(8,128)(2,1)S(1)}, u32[]{:S(2)}, u32[]{:S(2)}) async-start(bf16[32,24,288]{2,1,0:T(8,128)(2,1)} %broadcast_in_dim.10), calls=%async_computation | async-start | bytes 1179648 | tf_op jit(solution)/shard_map/all_to_all | solution.py:143
  27.4 7.6 %collective-permute-start = (bf16[2,40,384]{2,1,0:T(8,128)(2,1)S(1)}, bf16[2,40,384]{2,1,0:T(8,128)(2,1)S(1)}, u32[]{:S(2)}, u32[]{:S(2)}) collective-permute-start(bf16[2,40,384]{2,1,0:T(8,128)(2,1)S(1)} %get-tuple-element.7), channel_id=1, source_target_pairs={{0,128},{128,256},{256,384},{384,0},{1,129},{129,257},{257,385},{3... | collective-permute-start | bytes 184328 | tf_op jit(solution)/shard_map/ppermute | solution.py:163
  30.5 5.3 %collective-permute-start.1 = (bf16[2,40,384]{2,1,0:T(8,128)(2,1)S(1)}, bf16[2,40,384]{2,1,0:T(8,128)(2,1)S(1)}, u32[]{:S(2)}, u32[]{:S(2)}) collective-permute-start(bf16[2,40,384]{2,1,0:T(8,128)(2,1)S(1)} %get-tuple-element.6), channel_id=1, source_target_pairs={{0,384},{128,0},{256,128},{384,256},{1,385},{129,1},{257,129},{385... | collective-permute-start | bytes 184328 | tf_op jit(solution)/shard_map/ppermute | solution.py:164
  35.0 6.2 %copy-start.4 = (bf16[2,40,384]{2,1,0:T(8,128)(2,1)}, bf16[2,40,384]{2,1,0:T(8,128)(2,1)S(1)}, u32[]{:S(2)}) copy-start(bf16[2,40,384]{2,1,0:T(8,128)(2,1)S(1)} %collective-permute-done.left_ref) | copy-start | bytes 184324
  35.8 5.3 %copy-start.5 = (bf16[2,40,384]{2,1,0:T(8,128)(2,1)}, bf16[2,40,384]{2,1,0:T(8,128)(2,1)S(1)}, u32[]{:S(2)}) copy-start(bf16[2,40,384]{2,1,0:T(8,128)(2,1)S(1)} %collective-permute-done.1.right_ref) | copy-start | bytes 184324
  41.1 0.9 copy-start.2
  44.8 33.8 %all-to-all-start.2 = ((bf16[16,64,288]{2,1,0:T(8,128)(2,1)}), bf16[16,64,288]{2,1,0:T(8,128)(2,1)S(1)}, u32[]{:S(2)}, u32[]{:S(2)}) async-start(bf16[16,64,288]{2,1,0:T(8,128)(2,1)} %shard_map.86), calls=%async_computation.2 | async-start | bytes 1572864 | tf_op jit(solution)/shard_map/all_to_all | solution.py:143
  78.6 0.9 copy-start
  81.9 24.6 %all-to-all-start.3 = ((bf16[8,32,1280]{2,1,0:T(8,128)(2,1)}), bf16[8,32,1280]{2,1,0:T(8,128)(2,1)S(1)}, u32[]{:S(2)}, u32[]{:S(2)}) async-start(bf16[8,32,1280]{2,1,0:T(8,128)(2,1)} %get-tuple-element.5), calls=%async_computation.3 | async-start | bytes 1310720 | tf_op jit(solution)/shard_map/all_to_all | solution.py:143
  106.5 0.9 copy-start.1

commit v2 on v1

--- a/solution.py
+++ b/solution.py
@@ -21,7 +21,8 @@
     ]
     outs = jax.tree.map(lambda _: pl.BlockSpec(memory_space=pltpu.VMEM), out_shape)
     return pl.pallas_call(
-        body, out_shape=out_shape, in_specs=specs, out_specs=outs, scratch_shapes=scratch
+        body, out_shape=out_shape, in_specs=specs, out_specs=outs, scratch_shapes=scratch,
+        compiler_params=pltpu.CompilerParams(vmem_limit_bytes=16 << 20),
     )(*args)
 
 
@@ -64,7 +65,6 @@
         pre = got_ref[col].astype(f32)
         for part in range(1, 4):
             pre = pre + got_ref[4 * part + col].astype(f32)
-        pre = pre.astype(bf16).astype(f32)
         square = jnp.sum(pre * pre, axis=1, keepdims=True)
         total = square if total is None else total + square
         pres.append(pre)
@@ -194,7 +194,7 @@
     got = exchange(sent, "z")
     sent = call(
         score,
-        jax.ShapeDtypeStruct((4, 32, 288), f32),
+        jax.ShapeDtypeStruct((4, 32, 288), bf16),
         [],
         where,
         log_scale,

time: 126 us -> 116 us (0.921)
  local copies, waits for them, and re-layouts: 7.34 us -> 2.06 us
  Pallas kernels: 9.61 us -> 5.62 us
  waiting for transfers between devices: 49.7 us -> 53.5 us
  blocking collectives: 13 us -> 10.1 us
    pallas_call x4, Pallas kernels: 9.61 us -> 5.62 us  [call(): pl.pallas_call(body, out_shape=out_shape, in_specs=specs, out_specs=outs,...]
    all_to_all x4, waiting for transfers between devices: 47.8 us -> 51.5 us  [exchange(): return lax.all_to_all(value, axes, split_axis=0, concat_axis=0, tiled=True)]
    all_to_all x1, blocking collectives: 13 us -> 10.1 us  [exchange(): return lax.all_to_all(value, axes, split_axis=0, concat_axis=0, tiled=True)]
    unnamed x18 -> x6, local copies, waits for them, and re-layouts: 3.28 us -> 0.66 us
    slice x3, local copies, waits for them, and re-layouts: 2.07 us -> 0.01 us  [local(): a[:, 32:34, 0:128]]
  transfers between devices with their start and end apart: 6 -> 6, of which waited for: 6 -> 6; matrix products, arithmetic and copies ran while one was open for 3% -> 0% of each run, Pallas kernels for 0% -> 0%
where the time goes in v2:
time: 116 us; the launch traced here: 115 us
  waiting for transfers between devices  53.5 us (46%)
  starting transfers between devices  40.3 us (35%)
  blocking collectives  10.1 us (9%)
  Pallas kernels  5.62 us (5%)
  between operations  2.07 us (2%)
  local copies, waits for them, and re-layouts  2.06 us (2%)
  other arithmetic  1.64 us (1%)
    all_to_all x4, waiting for transfers between devices, exchange(): return lax.all_to_all(value, axes, split_axis=0, concat_axis=0, tiled=True)  51.5 us
    all_to_all x4, starting transfers between devices, exchange(): return lax.all_to_all(value, axes, split_axis=0, concat_axis=0, tiled=True)  33.8 us
    all_to_all x1, blocking collectives, exchange(): return lax.all_to_all(value, axes, split_axis=0, concat_axis=0, tiled=True)  10.1 us
    pallas_call x4, Pallas kernels, call(): pl.pallas_call(body, out_shape=out_shape, in_specs=specs, out_specs=outs,...  5.62 us
    ppermute x1, starting transfers between devices, local(): right = lax.ppermute(own[0:2], 'x', down)  3.35 us
    ppermute x1, starting transfers between devices, local(): left = lax.ppermute(own[2:4], 'x', up)  3.14 us
  transfers between devices with their start and end apart: 6, of which 6 were waited for; matrix products, arithmetic and copies ran while one was open for 0% of the time, Pallas kernels for 0%

profile of v2, /device:TPU:1, one launch (start us, length us, event | category | flops | bytes accessed | tf_op | source)
XLA Modules:
  0.0 115.3 jit_solution(3750719208716846165)
XLA Ops:
  0.6 0.0 copy-start.2
  0.6 0.6 copy-done.2
  1.3 0.1 tile.10
  1.4 0.8 pad_maximum_fusion.1
  2.2 0.1 reshape.165
  2.4 0.1 copy.14
  2.4 0.1 reshape.166
  2.6 0.7 pad_maximum_fusion
  3.3 0.0 copy-start
  3.3 0.0 copy-start.1
  3.3 5.5 %all-to-all-start.1 = ((bf16[4,40,384]{2,1,0:T(8,128)(2,1)}), bf16[4,40,384]{2,1,0:T(8,128)(2,1)S(1)}, u32[]{:S(2)}, u32[]{:S(2)}) async-start(bf16[4,40,384]{2,1,0:T(8,128)(2,1)} %pad_maximum_fusion), calls=%async_computation.1 | async-start | bytes 245760 | tf_op jit(solution)/shard_map/all_to_all | solution.py:143
  8.8 0.0 copy-done
  8.8 0.0 copy-done.1
  8.9 4.7 %all-to-all-done.1.own_ref = bf16[4,40,384]{2,1,0:T(8,128)(2,1)S(1)} async-done(((bf16[4,40,384]{2,1,0:T(8,128)(2,1)}), bf16[4,40,384]{2,1,0:T(8,128)(2,1)S(1)}, u32[]{:S(2)}, u32[]{:S(2)}) %all-to-all-start.1) | async-done | bytes 122912 | tf_op jit(solution)/shard_map/all_to_all | solution.py:143
  13.6 0.9 broadcast_in_dim.10
  14.5 12.9 %all-to-all-start = ((bf16[32,24,288]{2,1,0:T(8,128)(2,1)}), bf16[32,24,288]{2,1,0:T(8,128)(2,1)S(1)}, u32[]{:S(2)}, u32[]{:S(2)}) async-start(bf16[32,24,288]{2,1,0:T(8,128)(2,1)} %broadcast_in_dim.10), calls=%async_computation | async-start | bytes 1179648 | tf_op jit(solution)/shard_map/all_to_all | solution.py:143
  27.4 3.1 %collective-permute-start = (bf16[2,40,384]{2,1,0:T(8,128)(2,1)S(1)}, bf16[2,40,384]{2,1,0:T(8,128)(2,1)S(1)}, u32[]{:S(2)}, u32[]{:S(2)}) collective-permute-start(bf16[2,40,384]{2,1,0:T(8,128)(2,1)S(1)} %get-tuple-element.7), channel_id=1, source_target_pairs={{0,128},{128,256},{256,384},{384,0},{1,129},{129,257},{257,385},{3... | collective-permute-start | bytes 184328 | tf_op jit(solution)/shard_map/ppermute | solution.py:163
  30.5 3.4 %collective-permute-start.1 = (bf16[2,40,384]{2,1,0:T(8,128)(2,1)S(1)}, bf16[2,40,384]{2,1,0:T(8,128)(2,1)S(1)}, u32[]{:S(2)}, u32[]{:S(2)}) collective-permute-start(bf16[2,40,384]{2,1,0:T(8,128)(2,1)S(1)} %get-tuple-element.6), channel_id=1, source_target_pairs={{0,384},{128,0},{256,128},{384,256},{1,385},{129,1},{257,129},{385... | collective-permute-start | bytes 184328 | tf_op jit(solution)/shard_map/ppermute | solution.py:164
  33.9 1.1 collective-permute-done.left_ref
  35.0 0.8 collective-permute-done.1.right_ref
  35.8 5.3 %all-to-all-done = bf16[32,24,288]{2,1,0:T(8,128)(2,1)S(1)} async-done(((bf16[32,24,288]{2,1,0:T(8,128)(2,1)}), bf16[32,24,288]{2,1,0:T(8,128)(2,1)S(1)}, u32[]{:S(2)}, u32[]{:S(2)}) %all-to-all-start) | async-done | bytes 442400 | tf_op jit(solution)/shard_map/all_to_all | solution.py:143
  41.1 1.7 %shard_map.86 = bf16[16,64,288]{2,1,0:T(8,128)(2,1)} custom-call(bf16[768,288]{1,0:T(8,128)(2,1)S(1)} %bitcast.8, bf16[2,40,384]{2,1,0:T(8,128)(2,1)S(1)} %collective-permute-done.left_ref, bf16[4,40,384]{2,1,0:T(8,128)(2,1)S(1)} %all-to-all-done.1.own_ref, bf16[2,40,384]{2,1,0:T(8,128)(2,1)S(1)} %collective-permute-done.1.right_ref), custom_call_target="tpu_custom_call" | custom-call | tf_op jit(solution)/shard_map/pallas_call | solution.py:23
  42.8 11.6 %all-to-all-start.2 = ((bf16[16,64,288]{2,1,0:T(8,128)(2,1)}), bf16[16,64,288]{2,1,0:T(8,128)(2,1)S(1)}, u32[]{:S(2)}, u32[]{:S(2)}) async-start(bf16[16,64,288]{2,1,0:T(8,128)(2,1)} %shard_map.86), calls=%async_computation.2 | async-start | bytes 1572864 | tf_op jit(solution)/shard_map/all_to_all | solution.py:143
  54.4 0.1 pad_add_fusion.where_ref
  54.6 22.1 %all-to-all-done.2.got_ref = bf16[16,64,288]{2,1,0:T(8,128)(2,1)S(1)} async-done(((bf16[16,64,288]{2,1,0:T(8,128)(2,1)}), bf16[16,64,288]{2,1,0:T(8,128)(2,1)S(1)}, u32[]{:S(2)}, u32[]{:S(2)}) %all-to-all-start.2) | async-done | bytes 589856 | tf_op jit(solution)/shard_map/all_to_all | solution.py:143
  76.6 1.8 %shard_map.87 = (bf16[32,1152]{1,0:T(8,128)(2,1)S(1)}, bf16[8,32,1280]{2,1,0:T(8,128)(2,1)}) custom-call(s32[3]{0:T(128)S(1)} %pad_add_fusion.where_ref, bf16[16,64,288]{2,1,0:T(8,128)(2,1)S(1)} %all-to-all-done.2.got_ref, f32[2,2,128]{2,1,0:T(2,128)S(1)} %pad_maximum_fusion.3.pair_ref), custom_call_target="tpu_custom_call" | custom-call | tf_op jit(solution)/shard_map/pallas_call | solution.py:23
  78.4 3.8 %all-to-all-start.3 = ((bf16[8,32,1280]{2,1,0:T(8,128)(2,1)}), bf16[8,32,1280]{2,1,0:T(8,128)(2,1)S(1)}, u32[]{:S(2)}, u32[]{:S(2)}) async-start(bf16[8,32,1280]{2,1,0:T(8,128)(2,1)} %get-tuple-element.5), calls=%async_computation.3 | async-start | bytes 1310720 | tf_op jit(solution)/shard_map/all_to_all | solution.py:143
  82.2 0.1 copy.12.pair_ref
  83.6 19.4 %all-to-all-done.3.got_ref = bf16[8,32,1280]{2,1,0:T(8,128)(2,1)S(1)} async-done(((bf16[8,32,1280]{2,1,0:T(8,128)(2,1)}), bf16[8,32,1280]{2,1,0:T(8,128)(2,1)S(1)}, u32[]{:S(2)}, u32[]{:S(2)}) %all-to-all-start.3) | async-done | bytes 655392 | tf_op jit(solution)/shard_map/all_to_all | solution.py:143
  103.0 1.5 %shard_map.88 = bf16[4,32,288]{2,1,0:T(8,128)(2,1)S(1)} custom-call(s32[3]{0:T(128)S(1)} %pad_add_fusion.where_ref, f32[1]{0:T(128)S(6)} %copy.15.scale_ref, f32[1]{0:T(128)S(6)} %copy.16.bias_ref, s32[16,1]{1,0:T(8,128)S(1)} %copy.12.pair_ref, bf16[32,1152]{1,0:T(8,128)(2,1)S(1)} %get-tuple-element.4.own_ref, bf16[8,32,1280]{2,1,0:T(8,128)(2,1)S(1)} %all-to-all-done.3.got_ref), custom_call_target="tpu_custom_call" | custom-call | tf_op jit(solution)/shard_map/pallas_call | solution.py:23
  104.5 10.1 %all_to_all.25.got_ref = bf16[4,32,288]{2,1,0:T(8,128)(2,1)S(1)} all-to-all(bf16[4,32,288]{2,1,0:T(8,128)(2,1)S(1)} %shard_map.88), channel_id=1, replica_groups=mesh['x'=4,'y'=4,'z'=8,'m0'=2,'m1'=2] {'m0','m1'}, dimensions={0} | all-to-all | bytes 147456 | tf_op jit(solution)/shard_map/all_to_all | solution.py:143
  114.6 0.7 shard_map.89
  (12 shorter events, 0.1 us)
Async XLA Ops:
  0.6 0.7 copy-start.2
  3.3 5.5 %copy-start = (bf16[12,288]{1,0:T(8,128)(2,1)S(1)}, bf16[12,288]{1,0:T(8,128)(2,1)}, u32[]{:S(2)}) copy-start(bf16[12,288]{1,0:T(8,128)(2,1)} %param.10) | copy-start | bytes 20740
  3.3 5.5 %copy-start.1 = (bf16[12,288]{1,0:T(8,128)(2,1)S(1)}, bf16[12,288]{1,0:T(8,128)(2,1)}, u32[]{:S(2)}) copy-start(bf16[12,288]{1,0:T(8,128)(2,1)} %param.9) | copy-start | bytes 20740
  3.3 10.3 %all-to-all-start.1 = ((bf16[4,40,384]{2,1,0:T(8,128)(2,1)}), bf16[4,40,384]{2,1,0:T(8,128)(2,1)S(1)}, u32[]{:S(2)}, u32[]{:S(2)}) async-start(bf16[4,40,384]{2,1,0:T(8,128)(2,1)} %pad_maximum_fusion), calls=%async_computation.1 | async-start | bytes 245760 | tf_op jit(solution)/shard_map/all_to_all | solution.py:143
  14.5 26.7 %all-to-all-start = ((bf16[32,24,288]{2,1,0:T(8,128)(2,1)}), bf16[32,24,288]{2,1,0:T(8,128)(2,1)S(1)}, u32[]{:S(2)}, u32[]{:S(2)}) async-start(bf16[32,24,288]{2,1,0:T(8,128)(2,1)} %broadcast_in_dim.10), calls=%async_computation | async-start | bytes 1179648 | tf_op jit(solution)/shard_map/all_to_all | solution.py:143
  27.4 7.6 %collective-permute-start = (bf16[2,40,384]{2,1,0:T(8,128)(2,1)S(1)}, bf16[2,40,384]{2,1,0:T(8,128)(2,1)S(1)}, u32[]{:S(2)}, u32[]{:S(2)}) collective-permute-start(bf16[2,40,384]{2,1,0:T(8,128)(2,1)S(1)} %get-tuple-element.7), channel_id=1, source_target_pairs={{0,128},{128,256},{256,384},{384,0},{1,129},{129,257},{257,385},{3... | collective-permute-start | bytes 184328 | tf_op jit(solution)/shard_map/ppermute | solution.py:163
  30.5 5.3 %collective-permute-start.1 = (bf16[2,40,384]{2,1,0:T(8,128)(2,1)S(1)}, bf16[2,40,384]{2,1,0:T(8,128)(2,1)S(1)}, u32[]{:S(2)}, u32[]{:S(2)}) collective-permute-start(bf16[2,40,384]{2,1,0:T(8,128)(2,1)S(1)} %get-tuple-element.6), channel_id=1, source_target_pairs={{0,384},{128,0},{256,128},{384,256},{1,385},{129,1},{257,129},{385... | collective-permute-start | bytes 184328 | tf_op jit(solution)/shard_map/ppermute | solution.py:164
  42.8 33.8 %all-to-all-start.2 = ((bf16[16,64,288]{2,1,0:T(8,128)(2,1)}), bf16[16,64,288]{2,1,0:T(8,128)(2,1)S(1)}, u32[]{:S(2)}, u32[]{:S(2)}) async-start(bf16[16,64,288]{2,1,0:T(8,128)(2,1)} %shard_map.86), calls=%async_computation.2 | async-start | bytes 1572864 | tf_op jit(solution)/shard_map/all_to_all | solution.py:143
  78.4 24.6 %all-to-all-start.3 = ((bf16[8,32,1280]{2,1,0:T(8,128)(2,1)}), bf16[8,32,1280]{2,1,0:T(8,128)(2,1)S(1)}, u32[]{:S(2)}, u32[]{:S(2)}) async-start(bf16[8,32,1280]{2,1,0:T(8,128)(2,1)} %get-tuple-element.5), calls=%async_computation.3 | async-start | bytes 1310720 | tf_op jit(solution)/shard_map/all_to_all | solution.py:143

commit v3 on v2

--- a/solution.py
+++ b/solution.py
@@ -5,6 +5,7 @@
 from jax.experimental.pallas import tpu as pltpu
 from jax.sharding import Mesh
 from jax.sharding import PartitionSpec as P
+
 
 BATCH = ("x", "y", "z")
 MP = ("m0", "m1")
@@ -26,54 +27,101 @@
     )(*args)
 
 
-def project(w_ref, left_ref, own_ref, right_ref, out_ref):
+def pack(img_ref, txt_ref, out_ref):
+    both = jnp.concatenate([img_ref[...].astype(f32), txt_ref[...].astype(f32)], axis=0)
+    tail = jnp.concatenate([both[6 * g : 6 * g + 6, 256:288] for g in range(4)], axis=1)
+    rows = [both[:, 0:128], both[:, 128:256], tail, jnp.zeros((2, 128), f32)]
+    rows = jnp.concatenate(rows, axis=0).astype(bf16)
+    for k in range(out_ref.shape[0]):
+        out_ref[k] = rows
+
+
+def project(where_ref, w_ref, r0_ref, r1_ref, r2_ref, r3_ref, out_ref, codes_ref, feat_ref):
     r = lax.broadcasted_iota(jnp.int32, (384, 384), 0)
     c = lax.broadcasted_iota(jnp.int32, (384, 384), 1)
     second = r >= 192
     k = jnp.where(second, r - 192, r)
     source = k + 12 * ((k * 171) >> 11) + jnp.where(second, 12, 0)
     sort = jnp.where(c == source, 1.0, 0.0).astype(bf16)
-    half_a = jnp.dot(sort, w_ref[0:384, :], preferred_element_type=f32).astype(bf16)
-    half_b = jnp.dot(sort, w_ref[384:768, :], preferred_element_type=f32).astype(bf16)
-    blocks = [left_ref[0], left_ref[1]] + [own_ref[k] for k in range(4)]
-    blocks += [right_ref[0], right_ref[1]]
+    k = lax.broadcasted_iota(jnp.int32, (192, 128), 0)
+    c = lax.broadcasted_iota(jnp.int32, (192, 128), 1)
+    group = (k * 171) >> 11
+    inner = k - 12 * group
+    low = jnp.where((inner < 6) & (c == 8 * group + inner), 1.0, 0.0).astype(bf16)
+    high = jnp.where((inner >= 6) & (c == 8 * group + inner - 6), 1.0, 0.0).astype(bf16)
+    weights = [[], []]
+    for half in range(2):
+        some = w_ref[16 * half : 16 * half + 16]
+        main = jnp.concatenate(
+            [some[:, 0:24].reshape(384, 128), some[:, 24:48].reshape(384, 128)], axis=1
+        )
+        tail = some[:, 48:56].reshape(128, 128)
+        main = jnp.dot(sort, main, preferred_element_type=f32).astype(bf16)
+        low_tail = jnp.dot(low, tail, preferred_element_type=f32)
+        high_tail = jnp.dot(high, tail, preferred_element_type=f32)
+        for which in range(2):
+            at = 64 * which
+            tail = low_tail[:, at : at + 32] + high_tail[:, at + 32 : at + 64]
+            tail = tail.astype(bf16)
+            weights[which].append(
+                jnp.concatenate([main[192 * which : 192 * which + 192]] + [tail] * 4, axis=1)
+            )
+    y = where_ref[3]
+    for k, ref in enumerate((r0_ref, r1_ref, r2_ref, r3_ref)):
+        feat_ref[(y - k) & 3] = ref[...]
+    blocks = [(2, 1), (3, 1), (0, 0), (1, 0), (2, 0), (3, 0), (0, 1), (1, 1)]
+    for j, (source, kind) in enumerate(blocks):
+        codes_ref[j] = feat_ref[source, kind, 32:40, 0:128].astype(f32)
     parts = []
     for which in range(2):
-        rows = jnp.concatenate([b[16 * which : 16 * which + 16] for b in blocks], axis=0)
-        part = jnp.dot(
-            rows[:, 0:192], half_a[192 * which : 192 * which + 192], preferred_element_type=f32
-        ) + jnp.dot(
-            rows[:, 192:384], half_b[192 * which : 192 * which + 192], preferred_element_type=f32
-        )
+        rows = jnp.concatenate(
+            [feat_ref[s, kind, 16 * which : 16 * which + 16, :] for s, kind in blocks], axis=0
+        )
+        part = jnp.dot(rows[:, 0:192], weights[which][0], preferred_element_type=f32)
+        part = part + jnp.dot(rows[:, 192:384], weights[which][1], preferred_element_type=f32)
         parts.append(part.astype(bf16))
     for y in range(4):
         for m in range(4):
             for place, block in enumerate((y + 2, y + 2 + DELTA[m])):
                 for which in range(2):
-                    start = 32 * place + 16 * which
-                    out_ref[4 * y + m, start : start + 16, :] = parts[which][
-                        16 * block : 16 * block + 16
+                    piece = 2 * place + which
+                    rows = parts[which][16 * block : 16 * block + 16]
+                    to = 4 * y + m
+                    at = 16 * piece
+                    out_ref[to, at : at + 16, :] = rows[:, 0:128]
+                    out_ref[to, 64 + at : 80 + at, :] = rows[:, 128:256]
+                    out_ref[to, 128:144, 32 * piece : 32 * piece + 32] = rows[
+                        :, 256 + 32 * piece : 288 + 32 * piece
                     ]
 
 
 def embed(where_ref, got_ref, pair_ref, own_ref, out_ref, rows_ref):
     z = where_ref[1]
     m = where_ref[2]
-    pres = []
-    total = None
+    total = jnp.zeros((64, 1), f32)
+    mains = []
+    tails = []
     for col in range(4):
         pre = got_ref[col].astype(f32)
         for part in range(1, 4):
             pre = pre + got_ref[4 * part + col].astype(f32)
-        square = jnp.sum(pre * pre, axis=1, keepdims=True)
-        total = square if total is None else total + square
-        pres.append(pre)
+        mains += [pre[0:64], pre[64:128]]
+        last = pre[128:144]
+        tails.append(
+            jnp.concatenate([last[:, 32 * g : 32 * g + 32] for g in range(4)], axis=0)
+        )
+    mains.append(jnp.concatenate(tails, axis=1))
+    for pre in mains:
+        total = total + jnp.sum(pre * pre, axis=1, keepdims=True)
     norm = lax.rsqrt(total + epsilon)
-    for col in range(4):
-        rows_ref[:, 288 * col : 288 * col + 288] = (pres[col] * norm).astype(bf16)
+    for tile, pre in enumerate(mains):
+        rows_ref[:, 128 * tile : 128 * tile + 128] = (pre * norm).astype(bf16)
+    other = where_ref[3] + 2 + jnp.where(m < 2, m - 2, m - 1)
     for place in range(2):
-        high = jnp.broadcast_to(pair_ref[place, 0:1, :], (8, 128))
-        low = jnp.broadcast_to(pair_ref[place, 1:2, :], (8, 128))
+        at = where_ref[3] + 2 if place == 0 else other
+        code = pair_ref[at]
+        high = jnp.broadcast_to(code[0:1, :], (8, 128))
+        low = jnp.broadcast_to(code[1:2, :], (8, 128))
         tile = jnp.concatenate([high, low], axis=0).astype(bf16)
         rows_ref[32 * place : 32 * place + 16, 1152:1280] = tile
         rows_ref[32 * place + 16 : 32 * place + 32, 1152:1280] = jnp.zeros((16, 128), bf16)
@@ -123,10 +171,23 @@
     image_part = grads(own_ref[0:16, :], txts, match_img)
     text_part = grads(own_ref[16:32, :], imgs, match_txt)
     for to in range(4):
-        out_ref[to, 0:16, :] = image_part[:, 288 * to : 288 * to + 288].astype(out_ref.dtype)
+        out_ref[to, 0:16, :] = jnp.concatenate(
+            [
+                image_part[:, 256 * to : 256 * to + 256],
+                image_part[:, 1024 + 32 * to : 1056 + 32 * to],
+            ],
+            axis=1,
+        ).astype(out_ref.dtype)
         rows = text_part[4 * to : 4 * to + 4]
         out_ref[to, 16:32, :] = jnp.concatenate(
-            [rows[:, 288 * c : 288 * c + 288] for c in range(4)], axis=0
+            [
+                jnp.concatenate(
+                    [rows[:, 256 * c : 256 * c + 256], rows[:, 1024 + 32 * c : 1056 + 32 * c]],
+                    axis=1,
+                )
+                for c in range(4)
+            ],
+            axis=0,
         ).astype(out_ref.dtype)
 
 
@@ -147,7 +208,10 @@
     x, y, z = (lax.axis_index(a) for a in BATCH)
     m = lax.axis_index(MP)
     octet = 4 * x + y
-    where = jnp.stack([octet, z, m]).astype(jnp.int32)
+    where = jnp.stack([octet, z, m, y]).astype(jnp.int32)
+
+    sent = call(pack, jax.ShapeDtypeStruct((32, 56, 128), bf16), [], w_img, w_txt)
+    weights = exchange(sent, ("x", "z"))
 
     lane = jnp.arange(384, dtype=jnp.int32)
     spread = jnp.tile(pair_index, 24)
@@ -156,39 +220,37 @@
     codes = jnp.concatenate([codes.astype(bf16), jnp.zeros((6, 384), bf16)], axis=0)
     feats = jnp.concatenate([img_feat, txt_feat], axis=0).reshape(32, 4, 4, 96)
     feats = feats.transpose(2, 0, 1, 3).reshape(4, 32, 384)
-    sent = jnp.concatenate([feats, jnp.broadcast_to(codes, (4, 8, 384))], axis=1)
-    own = exchange(sent, "y")
-    up = [(s, (s + 1) % 4) for s in range(4)]
-    down = [(s, (s - 1) % 4) for s in range(4)]
-    left = lax.ppermute(own[2:4], "x", up)
-    right = lax.ppermute(own[0:2], "x", down)
-
-    weights = jnp.concatenate([w_img, w_txt], axis=0)
-    weights = exchange(jnp.broadcast_to(weights, (32, 24, 288)), ("x", "z"))
-    weights = weights.reshape(768, 288)
-
-    sent = call(
-        project, jax.ShapeDtypeStruct((16, 64, 288), bf16), [], weights, left, own, right
+    feats = jnp.concatenate([feats, jnp.broadcast_to(codes, (4, 8, 384))], axis=1)
+    pairs = []
+    for s in range(16):
+        up, slot = divmod(s, 4)
+        pairs.append((s, 4 * ((up + (1 if slot > 1 else -1)) % 4) + slot))
+    far = lax.ppermute(feats, ("x", "y"), pairs)
+    both = jnp.stack([feats, far], axis=1)
+    received = [lax.dynamic_index_in_dim(both, y, 0, keepdims=False)]
+    for k in range(1, 4):
+        chosen = lax.dynamic_index_in_dim(both, (y + k) % 4, 0, keepdims=False)
+        received.append(
+            lax.ppermute(chosen, "y", [(s, (s + k) % 4) for s in range(4)])
+        )
+
+    sent, codes = call(
+        project,
+        (jax.ShapeDtypeStruct((16, 144, 128), bf16), jax.ShapeDtypeStruct((8, 8, 128), f32)),
+        [pltpu.VMEM((4, 2, 40, 384), bf16)],
+        where,
+        weights,
+        *received,
+        smem=(0,),
     )
     got = exchange(sent, ("y",) + MP)
-
-    codes = jnp.concatenate([a[:, 32:34, 0:128] for a in (left, own, right)], axis=0)
-    codes = codes.astype(f32)
-    delta = jnp.where(m < 2, m - 2, m - 1)
-    pairs = jnp.concatenate(
-        [
-            lax.dynamic_slice_in_dim(codes, y + 2, 1, 0),
-            lax.dynamic_slice_in_dim(codes, y + 2 + delta, 1, 0),
-        ],
-        axis=0,
-    )
     mine, sent = call(
         embed,
         (jax.ShapeDtypeStruct((32, 1152), bf16), jax.ShapeDtypeStruct((8, 32, 1280), bf16)),
         [pltpu.VMEM((64, 1280), bf16)],
         where,
         got,
-        pairs,
+        codes,
         smem=(0,),
     )
     got = exchange(sent, "z")
@@ -217,4 +279,5 @@
     finer = Mesh(mesh.devices.reshape(4, 4, 8, 2, 2), BATCH + MP)
     in_specs = (P(BATCH, None), P(BATCH, None), P(BATCH, MP), P(BATCH, MP), P(BATCH), P(), P())
     out_specs = (P(BATCH, MP), P(BATCH + MP, None))
+
     return jax.shard_map(local, mesh=finer, in_specs=in_specs, out_specs=out_specs, check_vma=False)

time: 116 us -> 111 us (0.957)
  blocking collectives: 10.1 us -> 38.4 us
  waiting for transfers between devices: 53.5 us -> 25.9 us
  starting transfers between devices: 40.3 us -> 34.7 us
  other arithmetic: 1.64 us -> 0.18 us
    all_to_all x4 -> x2, waiting for transfers between devices: 51.5 us -> 19.4 us  [exchange(): return lax.all_to_all(value, axes, split_axis=0, concat_axis=0, tiled=True)]
    all_to_all x1 -> x2, blocking collectives: 10.1 us -> 38.4 us  [exchange(): return lax.all_to_all(value, axes, split_axis=0, concat_axis=0, tiled=True)]
    all_to_all x4 -> x2, starting transfers between devices: 33.8 us -> 20.4 us  [exchange(): return lax.all_to_all(value, axes, split_axis=0, concat_axis=0, tiled=True)]
    ppermute x2 -> x4, starting transfers between devices: 6.49 us -> 14.3 us  [the longest x3 9.93 us: local(): lax.ppermute(chosen, 'y', [(s, (s + k) % 4) for s in range(4)])]
    ppermute x2 -> x4, waiting for transfers between devices: 1.93 us -> 6.52 us  [the longest x1 3.83 us: local(): far = lax.ppermute(feats, ('x', 'y'), pairs)]
    unnamed x6 -> x10, local copies, waits for them, and re-layouts: 0.66 us -> 2.06 us
    pallas_call x4 -> x5, Pallas kernels: 5.62 us -> 6.12 us  [call(): pl.pallas_call(body, out_shape=out_shape, in_specs=specs, out_specs=outs,...]
  transfers between devices with their start and end apart: 6 -> 6, of which waited for: 6 -> 4; matrix products, arithmetic and copies ran while one was open for 0% -> 1% of each run, Pallas kernels for 0% -> 0%
where the time goes in v3:
time: 111 us; the launch traced here: 110 us
  blocking collectives  38.4 us (35%)
  starting transfers between devices  34.7 us (31%)
  waiting for transfers between devices  25.9 us (23%)
  Pallas kernels  6.12 us (6%)
  local copies, waits for them, and re-layouts  2.57 us (2%)
  between operations  2.14 us (2%)
    all_to_all x2, blocking collectives, exchange(): return lax.all_to_all(value, axes, split_axis=0, concat_axis=0, tiled=True)  38.4 us
    all_to_all x2, starting transfers between devices, exchange(): return lax.all_to_all(value, axes, split_axis=0, concat_axis=0, tiled=True)  20.4 us
    all_to_all x2, waiting for transfers between devices, exchange(): return lax.all_to_all(value, axes, split_axis=0, concat_axis=0, tiled=True)  19.4 us
    ppermute x3, starting transfers between devices, local(): lax.ppermute(chosen, 'y', [(s, (s + k) % 4) for s in range(4)])  9.93 us
    pallas_call x5, Pallas kernels, call(): pl.pallas_call(body, out_shape=out_shape, in_specs=specs, out_specs=outs,...  6.12 us
    ppermute x1, starting transfers between devices, local(): far = lax.ppermute(feats, ('x', 'y'), pairs)  4.39 us
    ppermute x1, waiting for transfers between devices, local(): far = lax.ppermute(feats, ('x', 'y'), pairs)  3.83 us
    ppermute x3, waiting for transfers between devices, local(): lax.ppermute(chosen, 'y', [(s, (s + k) % 4) for s in range(4)])  2.7 us
  transfers between devices with their start and end apart: 6, of which 4 were waited for; matrix products, arithmetic and copies ran while one was open for 1% of the time, Pallas kernels for 0%

profile of v3, /device:TPU:1, one launch (start us, length us, event | category | flops | bytes accessed | tf_op | source)
XLA Modules:
  0.0 110.1 jit_solution(17128118745942252533)
XLA Ops:
  0.6 0.0 copy-start
  0.6 0.7 copy-done
  1.3 0.0 copy-start.1
  1.3 0.7 copy-done.1
  2.0 0.9 shard_map.86
  2.9 0.0 copy-start.2
  2.9 0.0 copy-start.3
  2.9 13.8 %all-to-all-start = ((bf16[32,56,128]{2,1,0:T(8,128)(2,1)}), bf16[32,56,128]{2,1,0:T(8,128)(2,1)S(1)}, u32[]{:S(2)}, u32[]{:S(2)}) async-start(bf16[32,56,128]{2,1,0:T(8,128)(2,1)} %shard_map.86), calls=%async_computation | async-start | bytes 917504 | tf_op jit(solution)/shard_map/all_to_all | solution.py:204
  16.7 0.0 copy-done.2
  16.8 0.0 copy-done.3
  16.8 0.0 copy-start.4
  16.8 0.6 copy-done.4
  17.5 0.1 tile.10
  17.5 0.1 reshape.161
  17.7 0.1 copy.12
  17.8 0.1 reshape.162
  18.0 4.4 %collective-permute-start = (bf16[4,40,384]{2,1,0:T(8,128)(2,1)S(1)}, bf16[4,40,384]{2,1,0:T(8,128)(2,1)S(1)}, u32[]{:S(2)}, u32[]{:S(2)}) collective-permute-start(bf16[4,40,384]{2,1,0:T(8,128)(2,1)S(1)} %get-tuple-element.14), channel_id=1, source_target_pairs={{0,384},{32,416},{64,192},{96,224},{128,0},{160,32},{192,320},{224... | collective-permute-start | bytes 368648 | tf_op jit(solution)/shard_map/ppermute | solution.py:228
  22.4 3.8 %collective-permute-done = bf16[4,40,384]{2,1,0:T(8,128)(2,1)S(1)} collective-permute-done((bf16[4,40,384]{2,1,0:T(8,128)(2,1)S(1)}, bf16[4,40,384]{2,1,0:T(8,128)(2,1)S(1)}, u32[]{:S(2)}, u32[]{:S(2)}) %collective-permute-start) | collective-permute-done | bytes 122912 | tf_op jit(solution)/shard_map/ppermute | solution.py:228
  26.3 3.2 %collective-permute-start.1 = (bf16[2,40,384]{2,1,0:T(8,128)(2,1)S(1)}, bf16[2,40,384]{2,1,0:T(8,128)(2,1)S(1)}, u32[]{:S(2)}, u32[]{:S(2)}) collective-permute-start(bf16[2,40,384]{2,1,0:T(8,128)(2,1)S(1)} %get-tuple-element.12), channel_id=1, source_target_pairs={{0,32},{32,64},{64,96},{96,0},{1,33},{33,65},{65,97},{97,1},{2,34}... | collective-permute-start | bytes 184328 | tf_op jit(solution)/shard_map/ppermute | solution.py:234
  29.5 3.7 %collective-permute-start.2 = (bf16[2,40,384]{2,1,0:T(8,128)(2,1)S(1)}, bf16[2,40,384]{2,1,0:T(8,128)(2,1)S(1)}, u32[]{:S(2)}, u32[]{:S(2)}) collective-permute-start(bf16[2,40,384]{2,1,0:T(8,128)(2,1)S(1)} %get-tuple-element.13), channel_id=1, source_target_pairs={{0,64},{32,96},{64,0},{96,32},{1,65},{33,97},{65,1},{97,33},{2,66}... | collective-permute-start | bytes 184328 | tf_op jit(solution)/shard_map/ppermute | solution.py:234
  33.3 3.0 %collective-permute-start.3 = (bf16[2,40,384]{2,1,0:T(8,128)(2,1)S(1)}, bf16[2,40,384]{2,1,0:T(8,128)(2,1)S(1)}, u32[]{:S(2)}, u32[]{:S(2)}) collective-permute-start(bf16[2,40,384]{2,1,0:T(8,128)(2,1)S(1)} %get-tuple-element.10), channel_id=1, source_target_pairs={{0,96},{32,0},{64,32},{96,64},{1,97},{33,1},{65,33},{97,65},{2,98}... | collective-permute-start | bytes 184328 | tf_op jit(solution)/shard_map/ppermute | solution.py:234
  36.3 0.1 pad_add_fusion.where_ref
  36.3 0.0 collective-permute-done.1.r1_ref
  36.3 0.4 collective-permute-done.2.r2_ref
  36.7 2.3 %collective-permute-done.3.r3_ref = bf16[2,40,384]{2,1,0:T(8,128)(2,1)S(1)} collective-permute-done((bf16[2,40,384]{2,1,0:T(8,128)(2,1)S(1)}, bf16[2,40,384]{2,1,0:T(8,128)(2,1)S(1)}, u32[]{:S(2)}, u32[]{:S(2)}) %collective-permute-start.3) | collective-permute-done | bytes 61472 | tf_op jit(solution)/shard_map/ppermute | solution.py:234
  39.0 0.0 all-to-all-done.w_ref
  39.0 1.4 %shard_map.87 = (bf16[16,144,128]{2,1,0:T(8,128)(2,1)S(1)}, f32[8,8,128]{2,1,0:T(8,128)S(1)}) custom-call(s32[4]{0:T(128)S(1)} %pad_add_fusion.where_ref, bf16[32,56,128]{2,1,0:T(8,128)(2,1)S(1)} %all-to-all-done.w_ref, bf16[2,40,384]{2,1,0:T(8,128)(2,1)S(1)} %get-tuple-element.11.r0_ref, bf16[2,40,384]{2,1,0:T(8,128)(2,1)S(1)} %collective-permute-done.1.r1_ref, ...), custom_call_target="tpu_custom_call" | custom-call | tf_op jit(solution)/shard_map/pallas_call | solution.py:24
  40.4 28.3 %all_to_all.20.got_ref = bf16[16,144,128]{2,1,0:T(8,128)(2,1)S(1)} all-to-all(bf16[16,144,128]{2,1,0:T(8,128)(2,1)S(1)} %get-tuple-element.6), channel_id=1, replica_groups=mesh['x'=4,'y'=4,'z'=8,'m0'=2,'m1'=2] {'y','m0','m1'}, dimensions={0} | all-to-all | bytes 1179648 | tf_op jit(solution)/shard_map/all_to_all | solution.py:204
  68.7 1.7 %shard_map.88 = (bf16[32,1152]{1,0:T(8,128)(2,1)S(1)}, bf16[8,32,1280]{2,1,0:T(8,128)(2,1)}) custom-call(s32[4]{0:T(128)S(1)} %pad_add_fusion.where_ref, bf16[16,144,128]{2,1,0:T(8,128)(2,1)S(1)} %all_to_all.20.got_ref, f32[8,8,128]{2,1,0:T(8,128)S(1)} %get-tuple-element.7.pair_ref), custom_call_target="tpu_custom_call" | custom-call | tf_op jit(solution)/shard_map/pallas_call | solution.py:24
  70.4 6.5 %all-to-all-start.2 = ((bf16[8,32,1280]{2,1,0:T(8,128)(2,1)}), bf16[8,32,1280]{2,1,0:T(8,128)(2,1)S(1)}, u32[]{:S(2)}, u32[]{:S(2)}) async-start(bf16[8,32,1280]{2,1,0:T(8,128)(2,1)} %get-tuple-element.9), calls=%async_computation.2 | async-start | bytes 1310720 | tf_op jit(solution)/shard_map/all_to_all | solution.py:204
  77.0 0.1 copy.14.pair_ref
  78.4 19.4 %all-to-all-done.2.got_ref = bf16[8,32,1280]{2,1,0:T(8,128)(2,1)S(1)} async-done(((bf16[8,32,1280]{2,1,0:T(8,128)(2,1)}), bf16[8,32,1280]{2,1,0:T(8,128)(2,1)S(1)}, u32[]{:S(2)}, u32[]{:S(2)}) %all-to-all-start.2) | async-done | bytes 655392 | tf_op jit(solution)/shard_map/all_to_all | solution.py:204
  97.8 1.5 %shard_map.89 = bf16[4,32,288]{2,1,0:T(8,128)(2,1)S(1)} custom-call(s32[4]{0:T(128)S(1)} %pad_add_fusion.where_ref, f32[1]{0:T(128)S(6)} %copy.15.scale_ref, f32[1]{0:T(128)S(6)} %copy.16.bias_ref, s32[16,1]{1,0:T(8,128)S(1)} %copy.14.pair_ref, bf16[32,1152]{1,0:T(8,128)(2,1)S(1)} %get-tuple-element.8.own_ref, bf16[8,32,1280]{2,1,0:T(8,128)(2,1)S(1)} %all-to-all-done.2.got_ref), custom_call_target="tpu_custom_call" | custom-call | tf_op jit(solution)/shard_map/pallas_call | solution.py:24
  99.2 10.2 %all_to_all.21.got_ref = bf16[4,32,288]{2,1,0:T(8,128)(2,1)S(1)} all-to-all(bf16[4,32,288]{2,1,0:T(8,128)(2,1)S(1)} %shard_map.89), channel_id=1, replica_groups=mesh['x'=4,'y'=4,'z'=8,'m0'=2,'m1'=2] {'m0','m1'}, dimensions={0} | all-to-all | bytes 147456 | tf_op jit(solution)/shard_map/all_to_all | solution.py:204
  109.4 0.7 shard_map.90
  (7 shorter events, 0.1 us)
Async XLA Ops:
  0.6 0.7 copy-start
  1.3 0.7 copy-start.1
  2.9 13.8 %copy-start.2 = (bf16[16,1536]{1,0:T(8,128)(2,1)S(1)}, bf16[16,1536]{1,0:T(8,128)(2,1)}, u32[]{:S(2)}) copy-start(bf16[16,1536]{1,0:T(8,128)(2,1)} %param.8) | copy-start | bytes 147460
  2.9 13.9 %copy-start.3 = (bf16[16,1536]{1,0:T(8,128)(2,1)S(1)}, bf16[16,1536]{1,0:T(8,128)(2,1)}, u32[]{:S(2)}) copy-start(bf16[16,1536]{1,0:T(8,128)(2,1)} %param.7) | copy-start | bytes 147460
  2.9 36.1 %all-to-all-start = ((bf16[32,56,128]{2,1,0:T(8,128)(2,1)}), bf16[32,56,128]{2,1,0:T(8,128)(2,1)S(1)}, u32[]{:S(2)}, u32[]{:S(2)}) async-start(bf16[32,56,128]{2,1,0:T(8,128)(2,1)} %shard_map.86), calls=%async_computation | async-start | bytes 917504 | tf_op jit(solution)/shard_map/all_to_all | solution.py:204
  16.8 0.7 copy-start.4
  18.0 8.3 %collective-permute-start = (bf16[4,40,384]{2,1,0:T(8,128)(2,1)S(1)}, bf16[4,40,384]{2,1,0:T(8,128)(2,1)S(1)}, u32[]{:S(2)}, u32[]{:S(2)}) collective-permute-start(bf16[4,40,384]{2,1,0:T(8,128)(2,1)S(1)} %get-tuple-element.14), channel_id=1, source_target_pairs={{0,384},{32,416},{64,192},{96,224},{128,0},{160,32},{192,320},{224... | collective-permute-start | bytes 368648 | tf_op jit(solution)/shard_map/ppermute | solution.py:228
  26.3 10.0 %collective-permute-start.1 = (bf16[2,40,384]{2,1,0:T(8,128)(2,1)S(1)}, bf16[2,40,384]{2,1,0:T(8,128)(2,1)S(1)}, u32[]{:S(2)}, u32[]{:S(2)}) collective-permute-start(bf16[2,40,384]{2,1,0:T(8,128)(2,1)S(1)} %get-tuple-element.12), channel_id=1, source_target_pairs={{0,32},{32,64},{64,96},{96,0},{1,33},{33,65},{65,97},{97,1},{2,34}... | collective-permute-start | bytes 184328 | tf_op jit(solution)/shard_map/ppermute | solution.py:234
  29.5 7.2 %collective-permute-start.2 = (bf16[2,40,384]{2,1,0:T(8,128)(2,1)S(1)}, bf16[2,40,384]{2,1,0:T(8,128)(2,1)S(1)}, u32[]{:S(2)}, u32[]{:S(2)}) collective-permute-start(bf16[2,40,384]{2,1,0:T(8,128)(2,1)S(1)} %get-tuple-element.13), channel_id=1, source_target_pairs={{0,64},{32,96},{64,0},{96,32},{1,65},{33,97},{65,1},{97,33},{2,66}... | collective-permute-start | bytes 184328 | tf_op jit(solution)/shard_map/ppermute | solution.py:234
  33.3 5.8 %collective-permute-start.3 = (bf16[2,40,384]{2,1,0:T(8,128)(2,1)S(1)}, bf16[2,40,384]{2,1,0:T(8,128)(2,1)S(1)}, u32[]{:S(2)}, u32[]{:S(2)}) collective-permute-start(bf16[2,40,384]{2,1,0:T(8,128)(2,1)S(1)} %get-tuple-element.10), channel_id=1, source_target_pairs={{0,96},{32,0},{64,32},{96,64},{1,97},{33,1},{65,33},{97,65},{2,98}... | collective-permute-start | bytes 184328 | tf_op jit(solution)/shard_map/ppermute | solution.py:234
  70.4 27.3 %all-to-all-start.2 = ((bf16[8,32,1280]{2,1,0:T(8,128)(2,1)}), bf16[8,32,1280]{2,1,0:T(8,128)(2,1)S(1)}, u32[]{:S(2)}, u32[]{:S(2)}) async-start(bf16[8,32,1280]{2,1,0:T(8,128)(2,1)} %get-tuple-element.9), calls=%async_computation.2 | async-start | bytes 1310720 | tf_op jit(solution)/shard_map/all_to_all | solution.py:204

commit v4 on v3

v4 whole, which is shorter than its diff:
```python
import jax
import jax.numpy as jnp
from jax import lax
from jax.experimental import pallas as pl
from jax.experimental.pallas import tpu as pltpu
from jax.sharding import Mesh
from jax.sharding import PartitionSpec as P


BATCH = ("x", "y", "z")
MP = ("m0", "m1")
bf16 = jnp.bfloat16
f32 = jnp.float32
epsilon = 1e-06
DELTA = (-2, -1, 1, 2)


def call(body, out_shape, scratch, *args, smem=()):
    specs = [
        pl.BlockSpec(memory_space=pltpu.SMEM if k in smem else pltpu.VMEM)
        for k in range(len(args))
    ]
    outs = jax.tree.map(lambda _: pl.BlockSpec(memory_space=pltpu.VMEM), out_shape)
    return pl.pallas_call(
        body, out_shape=out_shape, in_specs=specs, out_specs=outs, scratch_shapes=scratch,
        compiler_params=pltpu.CompilerParams(vmem_limit_bytes=16 << 20),
    )(*args)


def pack(img_ref, txt_ref, out_ref):
    both = jnp.concatenate([img_ref[...].astype(f32), txt_ref[...].astype(f32)], axis=0)
    tail = jnp.concatenate([both[6 * g : 6 * g + 6, 256:288] for g in range(4)], axis=1)
    rows = [both[:, 0:128], both[:, 128:256], tail, jnp.zeros((2, 128), f32)]
    rows = jnp.concatenate(rows, axis=0).astype(bf16)
    for k in range(out_ref.shape[0]):
        out_ref[k] = rows


def project(where_ref, w_ref, r0_ref, r1_ref, r2_ref, r3_ref, out_ref, feat_ref):
    r = lax.broadcasted_iota(jnp.int32, (384, 384), 0)
    c = lax.broadcasted_iota(jnp.int32, (384, 384), 1)
    second = r >= 192
    k = jnp.where(second, r - 192, r)
    source = k + 12 * ((k * 171) >> 11) + jnp.where(second, 12, 0)
    sort = jnp.where(c == source, 1.0, 0.0).astype(bf16)
    k = lax.broadcasted_iota(jnp.int32, (192, 128), 0)
    c = lax.broadcasted_iota(jnp.int32, (192, 128), 1)
    group = (k * 171) >> 11
    inner = k - 12 * group
    low = jnp.where((inner < 6) & (c == 8 * group + inner), 1.0, 0.0).astype(bf16)
    high = jnp.where((inner >= 6) & (c == 8 * group + inner - 6), 1.0, 0.0).astype(bf16)
    weights = [[], []]
    for half in range(2):
        some = w_ref[16 * half : 16 * half + 16]
        main = jnp.concatenate(
            [some[:, 0:24].reshape(384, 128), some[:, 24:48].reshape(384, 128)], axis=1
        )
        tail = some[:, 48:56].reshape(128, 128)
        main = jnp.dot(sort, main, preferred_element_type=f32).astype(bf16)
        low_tail = jnp.dot(low, tail, preferred_element_type=f32)
        high_tail = jnp.dot(high, tail, preferred_element_type=f32)
        for which in range(2):
            at = 64 * which
            tail = low_tail[:, at : at + 32] + high_tail[:, at + 32 : at + 64]
            tail = tail.astype(bf16)
            weights[which].append(
                jnp.concatenate([main[192 * which : 192 * which + 192]] + [tail] * 4, axis=1)
            )
    y = where_ref[3]
    for k, ref in enumerate((r0_ref, r1_ref, r2_ref, r3_ref)):
        feat_ref[(y - k) & 3] = ref[...]
    parts = []
    for which in range(2):
        rows = jnp.concatenate(
            [feat_ref[s, 16 * which : 16 * which + 16, :] for s in range(4)], axis=0
        )
        part = jnp.dot(rows[:, 0:192], weights[which][0], preferred_element_type=f32)
        parts.append(
            part + jnp.dot(rows[:, 192:384], weights[which][1], preferred_element_type=f32)
        )
    for y in range(4):
        rows = jnp.concatenate([part[16 * y : 16 * y + 16] for part in parts], axis=0)
        tail = jnp.concatenate(
            [rows[8 * g : 8 * g + 8, 256 + 32 * g : 288 + 32 * g] for g in range(4)], axis=1
        )
        block = jnp.concatenate([rows[:, 0:128], rows[:, 128:256], tail], axis=0).astype(bf16)
        for m in range(4):
            out_ref[4 * y + m] = block


def embed(got_ref, codes_ref, own_ref):
    total = jnp.zeros((32, 1), f32)
    tiles = []
    tails = []
    for col in range(4):
        pre = got_ref[col].astype(f32)
        for part in range(1, 4):
            pre = pre + got_ref[4 * part + col].astype(f32)
        tiles += [pre[0:32], pre[32:64]]
        last = pre[64:72]
        tails.append(
            jnp.concatenate([last[:, 32 * g : 32 * g + 32] for g in range(4)], axis=0)
        )
    tiles.append(jnp.concatenate(tails, axis=1))
    for pre in tiles:
        total = total + jnp.sum(pre * pre, axis=1, keepdims=True)
    norm = lax.rsqrt(total + epsilon)
    for t, pre in enumerate(tiles):
        own_ref[32 * t : 32 * t + 32, :] = (pre * norm).astype(bf16)
    own_ref[288:296, :] = codes_ref[...].astype(bf16)


def choose(where_ref, own_ref, other_ref, out_ref, two_ref):
    z = where_ref[1]
    m = where_ref[2]
    two_ref[0] = own_ref[...]
    two_ref[1] = other_ref[...]
    middle = (m == 1) | (m == 2)
    for to in range(8):
        other_img = middle | ((m == 0) & (z >= to)) | ((m == 3) & (z < to))
        other_txt = middle | ((m == 0) & (z > to)) | ((m == 3) & (z <= to))
        img = jnp.where(other_img, 1, 0)
        txt = jnp.where(other_txt, 1, 0)
        for t in range(9):
            out_ref[to, 32 * t : 32 * t + 16, :] = two_ref[img, 32 * t : 32 * t + 16, :]
            out_ref[to, 32 * t + 16 : 32 * t + 32, :] = two_ref[
                txt, 32 * t + 16 : 32 * t + 32, :
            ]
        out_ref[to, 288:296, :] = two_ref[img, 288:296, :]


def score(where_ref, scale_ref, bias_ref, pair_ref, own_ref, got_ref, out_ref):
    octet = where_ref[0]
    z = where_ref[1]
    m = where_ref[2]
    scale = jnp.exp(jnp.full((16, 128), scale_ref[0], f32))
    scale_one = scale[:, 0:1]
    offset = bias_ref[0]

    def window(at):
        return jnp.concatenate(
            [
                jnp.concatenate(
                    [got_ref[k, 32 * t + at : 32 * t + at + 16, :] for k in range(8)], axis=0
                )
                for t in range(9)
            ],
            axis=1,
        )

    def mine(at):
        return jnp.concatenate(
            [own_ref[32 * t + at : 32 * t + at + 16, :] for t in range(9)], axis=1
        )

    imgs = window(0)
    txts = window(16)
    codes = got_ref[0, 288:296, :].astype(f32)
    for k in range(1, 8):
        codes = codes + got_ref[k, 288:296, :].astype(f32)
    pair_window = codes[0:1] * 64.0 + codes[1:2]
    lane = lax.broadcasted_iota(jnp.int32, (16, 128), 1)
    row = lax.broadcasted_iota(jnp.int32, (16, 128), 0)
    there = lane >> 4
    behind = jnp.where(there > z, -2, 0)
    ahead = jnp.where(there > z, 0, 2)
    delta = jnp.where(m == 0, behind, jnp.where(m == 3, ahead, jnp.where(m == 1, -1, 1)))
    block = (8 * (octet + delta) + there) & 127
    text_index = block * 16 + (lane & 15)
    match_img = pair_ref[...] == text_index
    own_text = (octet * 8 + z) * 16 + row
    match_txt = pair_window == own_text.astype(f32)

    def grads(own, window, match):
        scores = lax.dot_general(own, window, (((1,), (1,)), ((), ())), preferred_element_type=f32)
        logits = scale * scores + offset
        label = jnp.where(match, 1.0, -1.0)
        coef = (-label / (1.0 + jnp.exp(label * logits))).astype(bf16)
        return scale_one * jnp.dot(coef, window, preferred_element_type=f32)

    image_part = grads(mine(0), txts, match_img)
    text_part = grads(mine(16), imgs, match_txt)
    for to in range(4):
        rows = text_part[4 * to : 4 * to + 4]
        at = 1024 + 32 * to
        pieces = [
            image_part[:, 256 * to : 256 * to + 128],
            image_part[:, 256 * to + 128 : 256 * to + 256],
        ]
        pieces += [rows[:, 128 * t : 128 * t + 128] for t in range(9)]
        pieces.append(
            jnp.concatenate(
                [image_part[4 * g : 4 * g + 4, at : at + 32] for g in range(4)], axis=1
            )
        )
        out_ref[to] = jnp.concatenate(pieces, axis=0).astype(bf16)


def finish(got_ref, image_ref, text_ref):
    total = got_ref[0].astype(f32)
    for k in range(1, 4):
        total = total + got_ref[k].astype(f32)
    image_ref[:, 0:128] = total[0:16]
    image_ref[:, 128:256] = total[16:32]
    image_ref[:, 256:288] = jnp.concatenate(
        [total[68:72, 32 * g : 32 * g + 32] for g in range(4)], axis=0
    )
    pieces = []
    for c in range(4):
        pieces += [total[32 + 8 * c : 36 + 8 * c], total[36 + 8 * c : 40 + 8 * c]]
        pieces.append(total[64:68, 32 * c : 32 * c + 32])
    text_ref[...] = jnp.concatenate(pieces, axis=1)


def exchange(value, axes):
    return lax.all_to_all(value, axes, split_axis=0, concat_axis=0, tiled=True)


def local(img_feat, txt_feat, w_img, w_txt, pair_index, log_scale, bias):
    x, y, z = (lax.axis_index(a) for a in BATCH)
    m = lax.axis_index(MP)
    octet = 4 * x + y
    where = jnp.stack([octet, z, m, y]).astype(jnp.int32)

    sent = call(pack, jax.ShapeDtypeStruct((32, 56, 128), bf16), [], w_img, w_txt)
    weights = exchange(sent, ("x", "z"))

    feats = jnp.concatenate([img_feat, txt_feat], axis=0).reshape(32, 4, 4, 96)
    feats = feats.transpose(2, 0, 1, 3).reshape(4, 32, 384)
    received = [lax.dynamic_index_in_dim(feats, y, 0, keepdims=False)]
    for k in range(1, 4):
        chosen = lax.dynamic_index_in_dim(feats, (y + k) % 4, 0, keepdims=False)
        received.append(
            lax.ppermute(chosen, "y", [(s, (s + k) % 4) for s in range(4)])
        )

    lane = jnp.arange(128, dtype=jnp.int32)
    spread = jnp.tile(pair_index, 8)
    here = (lane // 16) == z
    codes = jnp.stack([jnp.where(here, spread // 64, 0), jnp.where(here, spread % 64, 0)])
    codes = jnp.concatenate([codes.astype(f32), jnp.zeros((6, 128), f32)], axis=0)

    sent = call(
        project,
        jax.ShapeDtypeStruct((16, 72, 128), bf16),
        [pltpu.VMEM((4, 32, 384), bf16)],
        where,
        weights,
        *received,
        smem=(0,),
    )
    got = exchange(sent, ("y",) + MP)
    own = call(embed, jax.ShapeDtypeStruct((296, 128), bf16), [], got, codes)

    pairs = []
    for s in range(512):
        o, rest = divmod(s, 32)
        pairs.append((s, 32 * ((o - DELTA[rest % 4]) % 16) + rest))
    other = lax.ppermute(own, BATCH + MP, pairs)
    sent = call(
        choose,
        jax.ShapeDtypeStruct((8, 296, 128), bf16),
        [pltpu.VMEM((2, 296, 128), bf16)],
        where,
        own,
        other,
        smem=(0,),
    )
    got = exchange(sent, "z")
    sent = call(
        score,
        jax.ShapeDtypeStruct((4, 72, 128), bf16),
        [],
        where,
        log_scale,
        bias,
        pair_index.reshape(16, 1),
        own,
        got,
        smem=(0, 1, 2),
    )
    got = exchange(sent, MP)
    return call(
        finish,
        (jax.ShapeDtypeStruct((16, 288), f32), jax.ShapeDtypeStruct((4, 1152), f32)),
        [],
        got,
    )


def solution(mesh):
    finer = Mesh(mesh.devices.reshape(4, 4, 8, 2, 2), BATCH + MP)
    in_specs = (P(BATCH, None), P(BATCH, None), P(BATCH, MP), P(BATCH, MP), P(BATCH), P(), P())
    out_specs = (P(BATCH, MP), P(BATCH + MP, None))

    return jax.shard_map(local, mesh=finer, in_specs=in_specs, out_specs=out_specs, check_vma=False)
```

time: 111 us -> 104 us (0.937)
  blocking collectives: 38.4 us -> 10.1 us
  waiting for transfers between devices: 25.9 us -> 39.6 us
  starting transfers between devices: 34.7 us -> 41.7 us
    all_to_all x2 -> x1, blocking collectives: 38.4 us -> 10.1 us  [exchange(): return lax.all_to_all(value, axes, split_axis=0, concat_axis=0, tiled=True)]
    all_to_all x2 -> x3, waiting for transfers between devices: 19.4 us -> 30.5 us  [exchange(): return lax.all_to_all(value, axes, split_axis=0, concat_axis=0, tiled=True)]
    all_to_all x2 -> x3, starting transfers between devices: 20.4 us -> 28.9 us  [exchange(): return lax.all_to_all(value, axes, split_axis=0, concat_axis=0, tiled=True)]
    ppermute x1, waiting for transfers between devices: 3.83 us -> 7.39 us  [local(): other = lax.ppermute(own, BATCH + MP, pairs)]
    ppermute x1, starting transfers between devices: 4.39 us -> 2.39 us  [local(): other = lax.ppermute(own, BATCH + MP, pairs)]
    pallas_call x5 -> x6, Pallas kernels: 6.12 us -> 6.67 us  [call(): pl.pallas_call(body, out_shape=out_shape, in_specs=specs, out_specs=outs,...]
  transfers between devices with their start and end apart: 6 -> 7, of which waited for: 4 -> 4; matrix products, arithmetic and copies ran while one was open for 1% -> 1% of each run, Pallas kernels for 0% -> 0%
where the time goes in v4:
time: 104 us; the launch traced here: 103 us
  starting transfers between devices  41.7 us (40%)
  waiting for transfers between devices  39.6 us (38%)
  blocking collectives  10.1 us (10%)
  Pallas kernels  6.67 us (6%)
  local copies, waits for them, and re-layouts  2.68 us (3%)
  between operations  2.15 us (2%)
    all_to_all x3, waiting for transfers between devices, exchange(): return lax.all_to_all(value, axes, split_axis=0, concat_axis=0, tiled=True)  30.5 us
    all_to_all x3, starting transfers between devices, exchange(): return lax.all_to_all(value, axes, split_axis=0, concat_axis=0, tiled=True)  28.9 us
    ppermute x3, starting transfers between devices, local(): lax.ppermute(chosen, 'y', [(s, (s + k) % 4) for s in range(4)])  10.4 us
    all_to_all x1, blocking collectives, exchange(): return lax.all_to_all(value, axes, split_axis=0, concat_axis=0, tiled=True)  10.1 us
    ppermute x1, waiting for transfers between devices, local(): other = lax.ppermute(own, BATCH + MP, pairs)  7.39 us
    pallas_call x6, Pallas kernels, call(): pl.pallas_call(body, out_shape=out_shape, in_specs=specs, out_specs=outs,...  6.67 us
    ppermute x1, starting transfers between devices, local(): other = lax.ppermute(own, BATCH + MP, pairs)  2.39 us
    unnamed x10, local copies, waits for them, and re-layouts  2.15 us
  transfers between devices with their start and end apart: 7, of which 4 were waited for; matrix products, arithmetic and copies ran while one was open for 1% of the time, Pallas kernels for 0%

profile of v4, /device:TPU:1, one launch (start us, length us, event | category | flops | bytes accessed | tf_op | source)
XLA Modules:
  0.0 103.1 jit_solution(6577011787602034739)
XLA Ops:
  0.6 0.0 copy-start
  0.6 0.7 copy-done
  1.3 0.0 copy-start.1
  1.3 0.7 copy-done.1
  2.0 0.9 shard_map.86
  2.9 0.0 copy-start.3
  2.9 13.8 %all-to-all-start = ((bf16[32,56,128]{2,1,0:T(8,128)(2,1)}), bf16[32,56,128]{2,1,0:T(8,128)(2,1)S(1)}, u32[]{:S(2)}, u32[]{:S(2)}) async-start(bf16[32,56,128]{2,1,0:T(8,128)(2,1)} %shard_map.86), calls=%async_computation | async-start | bytes 917504 | tf_op jit(solution)/shard_map/all_to_all | solution.py:216
  16.8 0.0 copy-start.2
  16.8 0.0 copy-done.3
  16.8 0.7 copy-done.2
  17.6 0.1 reshape.161
  17.7 0.1 copy.9
  17.8 0.1 reshape.162
  18.0 3.2 %collective-permute-start = (bf16[32,384]{1,0:T(8,128)(2,1)S(1)}, bf16[32,384]{1,0:T(8,128)(2,1)S(1)}, u32[]{:S(2)}, u32[]{:S(2)}) collective-permute-start(bf16[32,384]{1,0:T(8,128)(2,1)S(1)} %get-tuple-element.4), channel_id=1, source_target_pairs={{0,32},{32,64},{64,96},{96,0},{1,33},{33,65},{65,97},{97,1},{2,34}... | collective-permute-start | bytes 73736 | tf_op jit(solution)/shard_map/ppermute | solution.py:234
  21.2 4.2 %collective-permute-start.1 = (bf16[32,384]{1,0:T(8,128)(2,1)S(1)}, bf16[32,384]{1,0:T(8,128)(2,1)S(1)}, u32[]{:S(2)}, u32[]{:S(2)}) collective-permute-start(bf16[32,384]{1,0:T(8,128)(2,1)S(1)} %get-tuple-element.3), channel_id=1, source_target_pairs={{0,64},{32,96},{64,0},{96,32},{1,65},{33,97},{65,1},{97,33},{2,66}... | collective-permute-start | bytes 73736 | tf_op jit(solution)/shard_map/ppermute | solution.py:234
  25.4 3.0 %collective-permute-start.2 = (bf16[32,384]{1,0:T(8,128)(2,1)S(1)}, bf16[32,384]{1,0:T(8,128)(2,1)S(1)}, u32[]{:S(2)}, u32[]{:S(2)}) collective-permute-start(bf16[32,384]{1,0:T(8,128)(2,1)S(1)} %get-tuple-element.2), channel_id=1, source_target_pairs={{0,96},{32,0},{64,32},{96,64},{1,97},{33,1},{65,33},{97,65},{2,98}... | collective-permute-start | bytes 73736 | tf_op jit(solution)/shard_map/ppermute | solution.py:234
  28.4 0.1 pad_add_fusion.where_ref
  28.5 0.0 collective-permute-done.r1_ref
  28.5 0.0 collective-permute-done.1.r2_ref
  28.5 1.8 %collective-permute-done.2.r3_ref = bf16[32,384]{1,0:T(8,128)(2,1)S(1)} collective-permute-done((bf16[32,384]{1,0:T(8,128)(2,1)S(1)}, bf16[32,384]{1,0:T(8,128)(2,1)S(1)}, u32[]{:S(2)}, u32[]{:S(2)}) %collective-permute-start.2) | collective-permute-done | bytes 24608 | tf_op jit(solution)/shard_map/ppermute | solution.py:234
  30.3 0.0 all-to-all-done.w_ref
  30.3 2.1 %shard_map.87 = bf16[16,72,128]{2,1,0:T(8,128)(2,1)} custom-call(s32[4]{0:T(128)S(1)} %pad_add_fusion.where_ref, bf16[32,56,128]{2,1,0:T(8,128)(2,1)S(1)} %all-to-all-done.w_ref, bf16[32,384]{1,0:T(8,128)(2,1)S(1)} %get-tuple-element.5.r0_ref, bf16[32,384]{1,0:T(8,128)(2,1)S(1)} %collective-permute-done.r1_ref, ...), custom_call_target="tpu_custom_call" | custom-call | tf_op jit(solution)/shard_map/pallas_call | solution.py:24
  32.3 0.0 copy-start.4
  32.3 10.0 %all-to-all-start.1 = ((bf16[16,72,128]{2,1,0:T(8,128)(2,1)}), bf16[16,72,128]{2,1,0:T(8,128)(2,1)S(1)}, u32[]{:S(2)}, u32[]{:S(2)}) async-start(bf16[16,72,128]{2,1,0:T(8,128)(2,1)} %shard_map.87), calls=%async_computation.1 | async-start | bytes 589824 | tf_op jit(solution)/shard_map/all_to_all | solution.py:216
  42.3 0.0 copy-done.4
  42.3 0.1 tile.10
  42.5 12.2 %all-to-all-done.1.got_ref = bf16[16,72,128]{2,1,0:T(8,128)(2,1)S(1)} async-done(((bf16[16,72,128]{2,1,0:T(8,128)(2,1)}), bf16[16,72,128]{2,1,0:T(8,128)(2,1)S(1)}, u32[]{:S(2)}, u32[]{:S(2)}) %all-to-all-start.1) | async-done | bytes 294944 | tf_op jit(solution)/shard_map/all_to_all | solution.py:216
  54.6 0.2 shard_map.88.own_ref
  54.9 2.4 %collective-permute-start.3 = (bf16[296,128]{1,0:T(8,128)(2,1)S(1)}, bf16[296,128]{1,0:T(8,128)(2,1)S(1)}, u32[]{:S(2)}, u32[]{:S(2)}) collective-permute-start(bf16[296,128]{1,0:T(8,128)(2,1)S(1)} %shard_map.88.own_ref), channel_id=1, source_target_pairs={{0,64},{1,33},{2,482},{3,451},{4,68},{5,37},{6,486},{7,455},{8,72}... | collective-permute-start | bytes 227336 | tf_op jit(solution)/shard_map/ppermute | solution.py:259
  57.3 7.4 %collective-permute-done.3.other_ref = bf16[296,128]{1,0:T(8,128)(2,1)S(1)} collective-permute-done((bf16[296,128]{1,0:T(8,128)(2,1)S(1)}, bf16[296,128]{1,0:T(8,128)(2,1)S(1)}, u32[]{:S(2)}, u32[]{:S(2)}) %collective-permute-start.3) | collective-permute-done | bytes 75808 | tf_op jit(solution)/shard_map/ppermute | solution.py:259
  64.7 1.4 %shard_map.89 = bf16[8,296,128]{2,1,0:T(8,128)(2,1)} custom-call(s32[4]{0:T(128)S(1)} %pad_add_fusion.where_ref, bf16[296,128]{1,0:T(8,128)(2,1)S(1)} %shard_map.88.own_ref, bf16[296,128]{1,0:T(8,128)(2,1)S(1)} %collective-permute-done.3.other_ref), custom_call_target="tpu_custom_call" | custom-call | tf_op jit(solution)/shard_map/pallas_call | solution.py:24
  66.1 5.1 %all-to-all-start.2 = ((bf16[8,296,128]{2,1,0:T(8,128)(2,1)}), bf16[8,296,128]{2,1,0:T(8,128)(2,1)S(1)}, u32[]{:S(2)}, u32[]{:S(2)}) async-start(bf16[8,296,128]{2,1,0:T(8,128)(2,1)} %shard_map.89), calls=%async_computation.2 | async-start | bytes 1212416 | tf_op jit(solution)/shard_map/all_to_all | solution.py:216
  71.2 0.1 copy.10.pair_ref
  72.6 18.3 %all-to-all-done.2.got_ref = bf16[8,296,128]{2,1,0:T(8,128)(2,1)S(1)} async-done(((bf16[8,296,128]{2,1,0:T(8,128)(2,1)}), bf16[8,296,128]{2,1,0:T(8,128)(2,1)S(1)}, u32[]{:S(2)}, u32[]{:S(2)}) %all-to-all-start.2) | async-done | bytes 606240 | tf_op jit(solution)/shard_map/all_to_all | solution.py:216
  90.9 1.4 %shard_map.90 = bf16[4,72,128]{2,1,0:T(8,128)(2,1)S(1)} custom-call(s32[4]{0:T(128)S(1)} %pad_add_fusion.where_ref, f32[1]{0:T(128)S(6)} %copy.11.scale_ref, f32[1]{0:T(128)S(6)} %copy.12.bias_ref, s32[16,1]{1,0:T(8,128)S(1)} %copy.10.pair_ref, bf16[296,128]{1,0:T(8,128)(2,1)S(1)} %shard_map.88.own_ref, bf16[8,296,128]{2,1,0:T(8,128)(2,1)S(1)} %all-to-all-done.2.got_ref), custom_call_target="tpu_custom_call" | custom-call | tf_op jit(solution)/shard_map/pallas_call | solution.py:24
  92.2 10.1 %all_to_all.20.got_ref = bf16[4,72,128]{2,1,0:T(8,128)(2,1)S(1)} all-to-all(bf16[4,72,128]{2,1,0:T(8,128)(2,1)S(1)} %shard_map.90), channel_id=1, replica_groups=mesh['x'=4,'y'=4,'z'=8,'m0'=2,'m1'=2] {'m0','m1'}, dimensions={0} | all-to-all | bytes 147456 | tf_op jit(solution)/shard_map/all_to_all | solution.py:216
  102.4 0.7 shard_map.91
  (6 shorter events, 0.1 us)
Async XLA Ops:
  0.6 0.7 copy-start
  1.3 0.7 copy-start.1
  2.9 13.9 %copy-start.3 = (bf16[16,1536]{1,0:T(8,128)(2,1)S(1)}, bf16[16,1536]{1,0:T(8,128)(2,1)}, u32[]{:S(2)}) copy-start(bf16[16,1536]{1,0:T(8,128)(2,1)} %param.7) | copy-start | bytes 147460
  2.9 27.4 %all-to-all-start = ((bf16[32,56,128]{2,1,0:T(8,128)(2,1)}), bf16[32,56,128]{2,1,0:T(8,128)(2,1)S(1)}, u32[]{:S(2)}, u32[]{:S(2)}) async-start(bf16[32,56,128]{2,1,0:T(8,128)(2,1)} %shard_map.86), calls=%async_computation | async-start | bytes 917504 | tf_op jit(solution)/shard_map/all_to_all | solution.py:216
  16.8 0.8 copy-start.2
  18.0 10.5 %collective-permute-start = (bf16[32,384]{1,0:T(8,128)(2,1)S(1)}, bf16[32,384]{1,0:T(8,128)(2,1)S(1)}, u32[]{:S(2)}, u32[]{:S(2)}) collective-permute-start(bf16[32,384]{1,0:T(8,128)(2,1)S(1)} %get-tuple-element.4), channel_id=1, source_target_pairs={{0,32},{32,64},{64,96},{96,0},{1,33},{33,65},{65,97},{97,1},{2,34}... | collective-permute-start | bytes 73736 | tf_op jit(solution)/shard_map/ppermute | solution.py:234
  21.2 7.3 %collective-permute-start.1 = (bf16[32,384]{1,0:T(8,128)(2,1)S(1)}, bf16[32,384]{1,0:T(8,128)(2,1)S(1)}, u32[]{:S(2)}, u32[]{:S(2)}) collective-permute-start(bf16[32,384]{1,0:T(8,128)(2,1)S(1)} %get-tuple-element.3), channel_id=1, source_target_pairs={{0,64},{32,96},{64,0},{96,32},{1,65},{33,97},{65,1},{97,33},{2,66}... | collective-permute-start | bytes 73736 | tf_op jit(solution)/shard_map/ppermute | solution.py:234
  25.4 4.9 %collective-permute-start.2 = (bf16[32,384]{1,0:T(8,128)(2,1)S(1)}, bf16[32,384]{1,0:T(8,128)(2,1)S(1)}, u32[]{:S(2)}, u32[]{:S(2)}) collective-permute-start(bf16[32,384]{1,0:T(8,128)(2,1)S(1)} %get-tuple-element.2), channel_id=1, source_target_pairs={{0,96},{32,0},{64,32},{96,64},{1,97},{33,1},{65,33},{97,65},{2,98}... | collective-permute-start | bytes 73736 | tf_op jit(solution)/shard_map/ppermute | solution.py:234
  32.3 10.0 %copy-start.4 = (s32[16]{0:T(128)S(1)}, s32[16]{0:T(128)}, u32[]{:S(2)}) copy-start(s32[16]{0:T(128)} %param.11) | copy-start | bytes 196
  32.3 22.3 %all-to-all-start.1 = ((bf16[16,72,128]{2,1,0:T(8,128)(2,1)}), bf16[16,72,128]{2,1,0:T(8,128)(2,1)S(1)}, u32[]{:S(2)}, u32[]{:S(2)}) async-start(bf16[16,72,128]{2,1,0:T(8,128)(2,1)} %shard_map.87), calls=%async_computation.1 | async-start | bytes 589824 | tf_op jit(solution)/shard_map/all_to_all | solution.py:216
  54.9 9.8 %collective-permute-start.3 = (bf16[296,128]{1,0:T(8,128)(2,1)S(1)}, bf16[296,128]{1,0:T(8,128)(2,1)S(1)}, u32[]{:S(2)}, u32[]{:S(2)}) collective-permute-start(bf16[296,128]{1,0:T(8,128)(2,1)S(1)} %shard_map.88.own_ref), channel_id=1, source_target_pairs={{0,64},{1,33},{2,482},{3,451},{4,68},{5,37},{6,486},{7,455},{8,72}... | collective-permute-start | bytes 227336 | tf_op jit(solution)/shard_map/ppermute | solution.py:259
  66.1 24.7 %all-to-all-start.2 = ((bf16[8,296,128]{2,1,0:T(8,128)(2,1)}), bf16[8,296,128]{2,1,0:T(8,128)(2,1)S(1)}, u32[]{:S(2)}, u32[]{:S(2)}) async-start(bf16[8,296,128]{2,1,0:T(8,128)(2,1)} %shard_map.89), calls=%async_computation.2 | async-start | bytes 1212416 | tf_op jit(solution)/shard_map/all_to_all | solution.py:216

commit v5 on v4

--- a/solution.py
+++ b/solution.py
@@ -15,11 +15,11 @@
 DELTA = (-2, -1, 1, 2)
 
 
-def call(body, out_shape, scratch, *args, smem=()):
-    specs = [
-        pl.BlockSpec(memory_space=pltpu.SMEM if k in smem else pltpu.VMEM)
-        for k in range(len(args))
+def call(body, out_shape, scratch, *args, smem=(), hbm=()):
+    spaces = [
+        pltpu.SMEM if k in smem else pltpu.HBM if k in hbm else pltpu.VMEM for k in range(len(args))
     ]
+    specs = [pl.BlockSpec(memory_space=space) for space in spaces]
     outs = jax.tree.map(lambda _: pl.BlockSpec(memory_space=pltpu.VMEM), out_shape)
     return pl.pallas_call(
         body, out_shape=out_shape, in_specs=specs, out_specs=outs, scratch_shapes=scratch,
@@ -27,8 +27,16 @@
     )(*args)
 
 
-def pack(img_ref, txt_ref, out_ref):
-    both = jnp.concatenate([img_ref[...].astype(f32), txt_ref[...].astype(f32)], axis=0)
+def pack(img_ref, txt_ref, out_ref, img, txt, sems):
+    copies = [
+        pltpu.make_async_copy(img_ref, img, sems.at[0]),
+        pltpu.make_async_copy(txt_ref, txt, sems.at[1]),
+    ]
+    for copy in copies:
+        copy.start()
+    for copy in copies:
+        copy.wait()
+    both = jnp.concatenate([img[...].astype(f32), txt[...].astype(f32)], axis=0)
     tail = jnp.concatenate([both[6 * g : 6 * g + 6, 256:288] for g in range(4)], axis=1)
     rows = [both[:, 0:128], both[:, 128:256], tail, jnp.zeros((2, 128), f32)]
     rows = jnp.concatenate(rows, axis=0).astype(bf16)
@@ -36,19 +44,41 @@
         out_ref[k] = rows
 
 
-def project(where_ref, w_ref, r0_ref, r1_ref, r2_ref, r3_ref, out_ref, feat_ref):
+def setup(where_ref, pair_ref, scale_ref, bias_ref, sort_ref, split_ref, pairs_ref, consts_ref):
     r = lax.broadcasted_iota(jnp.int32, (384, 384), 0)
     c = lax.broadcasted_iota(jnp.int32, (384, 384), 1)
     second = r >= 192
     k = jnp.where(second, r - 192, r)
     source = k + 12 * ((k * 171) >> 11) + jnp.where(second, 12, 0)
-    sort = jnp.where(c == source, 1.0, 0.0).astype(bf16)
+    sort_ref[...] = jnp.where(c == source, 1.0, 0.0).astype(bf16)
     k = lax.broadcasted_iota(jnp.int32, (192, 128), 0)
     c = lax.broadcasted_iota(jnp.int32, (192, 128), 1)
     group = (k * 171) >> 11
     inner = k - 12 * group
-    low = jnp.where((inner < 6) & (c == 8 * group + inner), 1.0, 0.0).astype(bf16)
-    high = jnp.where((inner >= 6) & (c == 8 * group + inner - 6), 1.0, 0.0).astype(bf16)
+    low = (inner < 6) & (c == 8 * group + inner)
+    high = (inner >= 6) & (c == 8 * group + inner - 6)
+    split_ref[0:192, :] = jnp.where(low, 1.0, 0.0).astype(bf16)
+    split_ref[192:384, :] = jnp.where(high, 1.0, 0.0).astype(bf16)
+    row = lax.broadcasted_iota(jnp.int32, (16, 128), 0)
+    lane = lax.broadcasted_iota(jnp.int32, (8, 128), 1)
+    down = jnp.zeros((16, 128), jnp.int32)
+    across = jnp.zeros((8, 128), jnp.int32)
+    for k in range(16):
+        down = jnp.where(row == k, pair_ref[k], down)
+        across = jnp.where(lane == 16 * where_ref[1] + k, pair_ref[k], across)
+    pairs_ref[...] = down
+    row = lax.broadcasted_iota(jnp.int32, (8, 128), 0)
+    consts_ref[0:8, :] = jnp.where(row == 0, across >> 6, across & 63).astype(f32)
+    consts_ref[8:16, :] = jnp.full((8, 128), scale_ref[0], f32)
+    consts_ref[16:24, :] = jnp.full((8, 128), bias_ref[0], f32)
+
+
+def project(
+    where_ref, sort_ref, split_ref, w_ref, r0_ref, r1_ref, r2_ref, r3_ref, out_ref, feat_ref
+):
+    sort = sort_ref[...]
+    low = split_ref[0:192, :]
+    high = split_ref[192:384, :]
     weights = [[], []]
     for half in range(2):
         some = w_ref[16 * half : 16 * half + 16]
@@ -88,7 +118,7 @@
             out_ref[4 * y + m] = block
 
 
-def embed(got_ref, codes_ref, own_ref):
+def embed(got_ref, consts_ref, own_ref):
     total = jnp.zeros((32, 1), f32)
     tiles = []
     tails = []
@@ -107,7 +137,7 @@
     norm = lax.rsqrt(total + epsilon)
     for t, pre in enumerate(tiles):
         own_ref[32 * t : 32 * t + 32, :] = (pre * norm).astype(bf16)
-    own_ref[288:296, :] = codes_ref[...].astype(bf16)
+    own_ref[288:296, :] = consts_ref[0:8, :].astype(bf16)
 
 
 def choose(where_ref, own_ref, other_ref, out_ref, two_ref):
@@ -129,13 +159,13 @@
         out_ref[to, 288:296, :] = two_ref[img, 288:296, :]
 
 
-def score(where_ref, scale_ref, bias_ref, pair_ref, own_ref, got_ref, out_ref):
+def score(where_ref, consts_ref, pair_ref, own_ref, got_ref, out_ref):
     octet = where_ref[0]
     z = where_ref[1]
     m = where_ref[2]
-    scale = jnp.exp(jnp.full((16, 128), scale_ref[0], f32))
+    scale = jnp.exp(consts_ref[8:9, :])
     scale_one = scale[:, 0:1]
-    offset = bias_ref[0]
+    offset = consts_ref[16:17, :]
 
     def window(at):
         return jnp.concatenate(
@@ -222,7 +252,14 @@
     octet = 4 * x + y
     where = jnp.stack([octet, z, m, y]).astype(jnp.int32)
 
-    sent = call(pack, jax.ShapeDtypeStruct((32, 56, 128), bf16), [], w_img, w_txt)
+    sent = call(
+        pack,
+        jax.ShapeDtypeStruct((32, 56, 128), bf16),
+        [pltpu.VMEM((12, 288), bf16), pltpu.VMEM((12, 288), bf16), pltpu.SemaphoreType.DMA((2,))],
+        w_img,
+        w_txt,
+        hbm=(0, 1),
+    )
     weights = exchange(sent, ("x", "z"))
 
     feats = jnp.concatenate([img_feat, txt_feat], axis=0).reshape(32, 4, 4, 96)
@@ -234,29 +271,41 @@
             lax.ppermute(chosen, "y", [(s, (s + k) % 4) for s in range(4)])
         )
 
-    lane = jnp.arange(128, dtype=jnp.int32)
-    spread = jnp.tile(pair_index, 8)
-    here = (lane // 16) == z
-    codes = jnp.stack([jnp.where(here, spread // 64, 0), jnp.where(here, spread % 64, 0)])
-    codes = jnp.concatenate([codes.astype(f32), jnp.zeros((6, 128), f32)], axis=0)
+    sort, split, pairs, consts = call(
+        setup,
+        (
+            jax.ShapeDtypeStruct((384, 384), bf16),
+            jax.ShapeDtypeStruct((384, 128), bf16),
+            jax.ShapeDtypeStruct((16, 128), jnp.int32),
+            jax.ShapeDtypeStruct((24, 128), f32),
+        ),
+        [],
+        where,
+        pair_index,
+        log_scale,
+        bias,
+        smem=(0, 1, 2, 3),
+    )
 
     sent = call(
         project,
         jax.ShapeDtypeStruct((16, 72, 128), bf16),
         [pltpu.VMEM((4, 32, 384), bf16)],
         where,
+        sort,
+        split,
         weights,
         *received,
         smem=(0,),
     )
     got = exchange(sent, ("y",) + MP)
-    own = call(embed, jax.ShapeDtypeStruct((296, 128), bf16), [], got, codes)
-
-    pairs = []
+    own = call(embed, jax.ShapeDtypeStruct((296, 128), bf16), [], got, consts)
+
+    moves = []
     for s in range(512):
         o, rest = divmod(s, 32)
-        pairs.append((s, 32 * ((o - DELTA[rest % 4]) % 16) + rest))
-    other = lax.ppermute(own, BATCH + MP, pairs)
+        moves.append((s, 32 * ((o - DELTA[rest % 4]) % 16) + rest))
+    other = lax.ppermute(own, BATCH + MP, moves)
     sent = call(
         choose,
         jax.ShapeDtypeStruct((8, 296, 128), bf16),
@@ -272,12 +321,11 @@
         jax.ShapeDtypeStruct((4, 72, 128), bf16),
         [],
         where,
-        log_scale,
-        bias,
-        pair_index.reshape(16, 1),
+        consts,
+        pairs,
         own,
         got,
-        smem=(0, 1, 2),
+        smem=(0,),
     )
     got = exchange(sent, MP)
     return call(

time: 104 us -> 102 us (0.981)
  blocking collectives: 10.1 us -> 56.3 us
  waiting for transfers between devices: 39.6 us -> 7.4 us
  starting transfers between devices: 41.7 us -> 26.6 us
    all_to_all x1 -> x3, blocking collectives: 10.1 us -> 56.3 us  [exchange(): return lax.all_to_all(value, axes, split_axis=0, concat_axis=0, tiled=True)]
    all_to_all x3 -> x1, waiting for transfers between devices: 30.5 us -> 0.01 us  [exchange(): return lax.all_to_all(value, axes, split_axis=0, concat_axis=0, tiled=True)]
    all_to_all x3 -> x1, starting transfers between devices: 28.9 us -> 13.8 us  [exchange(): return lax.all_to_all(value, axes, split_axis=0, concat_axis=0, tiled=True)]
    ppermute x3, waiting for transfers between devices: 1.79 us -> 0.01 us  [local(): lax.ppermute(chosen, 'y', [(s, (s + k) % 4) for s in range(4)])]
    pallas_call x6 -> x7, Pallas kernels: 6.67 us -> 5.88 us  [call(): pl.pallas_call(body, out_shape=out_shape, in_specs=specs, out_specs=outs,...]
  transfers between devices with their start and end apart: 7 -> 5, of which waited for: 4 -> 1; matrix products, arithmetic and copies ran while one was open for 1% -> 0% of each run, Pallas kernels for 0% -> 1%
where the time goes in v5:
time: 102 us; the launch traced here: 101 us
  blocking collectives  56.3 us (55%)
  starting transfers between devices  26.6 us (26%)
  waiting for transfers between devices  7.4 us (7%)
  Pallas kernels  5.88 us (6%)
  local copies, waits for them, and re-layouts  2.51 us (2%)
  between operations  2.21 us (2%)
    all_to_all x3, blocking collectives, exchange(): return lax.all_to_all(value, axes, split_axis=0, concat_axis=0, tiled=True)  56.3 us
    all_to_all x1, starting transfers between devices, exchange(): return lax.all_to_all(value, axes, split_axis=0, concat_axis=0, tiled=True)  13.8 us
    ppermute x3, starting transfers between devices, local(): lax.ppermute(chosen, 'y', [(s, (s + k) % 4) for s in range(4)])  10.4 us
    ppermute x1, waiting for transfers between devices, local(): other = lax.ppermute(own, BATCH + MP, moves)  7.39 us
    pallas_call x7, Pallas kernels, call(): pl.pallas_call(body, out_shape=out_shape, in_specs=specs, out_specs=outs,...  5.88 us
    ppermute x1, starting transfers between devices, local(): other = lax.ppermute(own, BATCH + MP, moves)  2.39 us
    unnamed x10, local copies, waits for them, and re-layouts  2.16 us
  transfers between devices with their start and end apart: 5, of which 1 were waited for; matrix products, arithmetic and copies ran while one was open for 0% of the time, Pallas kernels for 1%

profile of v5, /device:TPU:1, one launch (start us, length us, event | category | flops | bytes accessed | tf_op | source)
XLA Modules:
  0.0 101.0 jit_solution(8348719894091848581)
XLA Ops:
  0.6 0.0 copy-start
  0.6 0.7 copy-done
  1.3 0.0 copy-start.1
  1.3 0.7 copy-done.1
  2.0 0.9 shard_map.87
  3.0 0.0 copy-start.4
  3.0 13.8 %all-to-all-start = ((bf16[32,56,128]{2,1,0:T(8,128)(2,1)}), bf16[32,56,128]{2,1,0:T(8,128)(2,1)S(1)}, u32[]{:S(2)}, u32[]{:S(2)}) async-start(bf16[32,56,128]{2,1,0:T(8,128)(2,1)} %shard_map.87), calls=%async_computation | async-start | bytes 917504 | tf_op jit(solution)/shard_map/all_to_all | solution.py:246
  16.8 0.0 copy-start.3
  16.9 0.0 copy-done.4
  16.9 0.7 copy-done.3
  17.6 0.1 reshape.10
  17.8 0.1 copy.9
  17.8 0.1 reshape.11
  18.0 3.2 %collective-permute-start = (bf16[32,384]{1,0:T(8,128)(2,1)S(1)}, bf16[32,384]{1,0:T(8,128)(2,1)S(1)}, u32[]{:S(2)}, u32[]{:S(2)}) collective-permute-start(bf16[32,384]{1,0:T(8,128)(2,1)S(1)} %get-tuple-element.12), channel_id=1, source_target_pairs={{0,32},{32,64},{64,96},{96,0},{1,33},{33,65},{65,97},{97,1},{2,34}... | collective-permute-start | bytes 73736 | tf_op jit(solution)/shard_map/ppermute | solution.py:271
  21.2 4.2 %collective-permute-start.1 = (bf16[32,384]{1,0:T(8,128)(2,1)S(1)}, bf16[32,384]{1,0:T(8,128)(2,1)S(1)}, u32[]{:S(2)}, u32[]{:S(2)}) collective-permute-start(bf16[32,384]{1,0:T(8,128)(2,1)S(1)} %get-tuple-element.11), channel_id=1, source_target_pairs={{0,64},{32,96},{64,0},{96,32},{1,65},{33,97},{65,1},{97,33},{2,66}... | collective-permute-start | bytes 73736 | tf_op jit(solution)/shard_map/ppermute | solution.py:271
  25.5 3.0 %collective-permute-start.2 = (bf16[32,384]{1,0:T(8,128)(2,1)S(1)}, bf16[32,384]{1,0:T(8,128)(2,1)S(1)}, u32[]{:S(2)}, u32[]{:S(2)}) collective-permute-start(bf16[32,384]{1,0:T(8,128)(2,1)S(1)} %get-tuple-element.10), channel_id=1, source_target_pairs={{0,96},{32,0},{64,32},{96,64},{1,97},{33,1},{65,33},{97,65},{2,98}... | collective-permute-start | bytes 73736 | tf_op jit(solution)/shard_map/ppermute | solution.py:271
  28.5 0.1 pad_add_fusion.where_ref
  29.2 0.0 copy-start.2
  29.9 0.0 copy-done.2
  29.9 0.7 shard_map.86
  30.6 0.0 collective-permute-done.r1_ref
  30.6 0.0 collective-permute-done.1.r2_ref
  30.6 0.0 collective-permute-done.2.r3_ref
  30.6 0.0 all-to-all-done.w_ref
  30.6 1.3 %shard_map.88 = bf16[16,72,128]{2,1,0:T(8,128)(2,1)S(1)} custom-call(s32[4]{0:T(128)S(1)} %pad_add_fusion.where_ref, bf16[384,384]{1,0:T(8,128)(2,1)S(1)} %get-tuple-element.8.sort_ref, bf16[384,128]{1,0:T(8,128)(2,1)S(1)} %get-tuple-element.9.split_ref, bf16[32,56,128]{2,1,0:T(8,128)(2,1)S(1)} %all-to-all-done.w_ref, ...), custom_call_target="tpu_custom_call" | custom-call | tf_op jit(solution)/shard_map/pallas_call | solution.py:24
  32.0 21.7 %all_to_all.20.got_ref = bf16[16,72,128]{2,1,0:T(8,128)(2,1)S(1)} all-to-all(bf16[16,72,128]{2,1,0:T(8,128)(2,1)S(1)} %shard_map.88), channel_id=1, replica_groups=mesh['x'=4,'y'=4,'z'=8,'m0'=2,'m1'=2] {'y','m0','m1'}, dimensions={0} | all-to-all | bytes 589824 | tf_op jit(solution)/shard_map/all_to_all | solution.py:246
  53.7 0.2 shard_map.89.own_ref
  53.9 2.4 %collective-permute-start.3 = (bf16[296,128]{1,0:T(8,128)(2,1)S(1)}, bf16[296,128]{1,0:T(8,128)(2,1)S(1)}, u32[]{:S(2)}, u32[]{:S(2)}) collective-permute-start(bf16[296,128]{1,0:T(8,128)(2,1)S(1)} %shard_map.89.own_ref), channel_id=1, source_target_pairs={{0,64},{1,33},{2,482},{3,451},{4,68},{5,37},{6,486},{7,455},{8,72}... | collective-permute-start | bytes 227336 | tf_op jit(solution)/shard_map/ppermute | solution.py:308
  56.3 7.4 %collective-permute-done.3.other_ref = bf16[296,128]{1,0:T(8,128)(2,1)S(1)} collective-permute-done((bf16[296,128]{1,0:T(8,128)(2,1)S(1)}, bf16[296,128]{1,0:T(8,128)(2,1)S(1)}, u32[]{:S(2)}, u32[]{:S(2)}) %collective-permute-start.3) | collective-permute-done | bytes 75808 | tf_op jit(solution)/shard_map/ppermute | solution.py:308
  63.7 0.6 shard_map.90
  64.3 22.7 %all_to_all.21.got_ref = bf16[8,296,128]{2,1,0:T(8,128)(2,1)S(1)} all-to-all(bf16[8,296,128]{2,1,0:T(8,128)(2,1)S(1)} %shard_map.90), channel_id=1, replica_groups=mesh['x'=4,'y'=4,'z'=8,'m0'=2,'m1'=2] {'z'}, dimensions={0} | all-to-all | bytes 1212416 | tf_op jit(solution)/shard_map/all_to_all | solution.py:246
  87.0 1.4 %shard_map.91 = bf16[4,72,128]{2,1,0:T(8,128)(2,1)S(1)} custom-call(s32[4]{0:T(128)S(1)} %pad_add_fusion.where_ref, f32[24,128]{1,0:T(8,128)S(1)} %get-tuple-element.6.consts_ref, s32[16,128]{1,0:T(8,128)S(1)} %get-tuple-element.7.pair_ref, bf16[296,128]{1,0:T(8,128)(2,1)S(1)} %shard_map.89.own_ref, bf16[8,296,128]{2,1,0:T(8,128)(2,1)S(1)} %all_to_all.21.got_ref), custom_call_target="tpu_custom_call" | custom-call | tf_op jit(solution)/shard_map/pallas_call | solution.py:24
  88.4 11.9 %all_to_all.22.got_ref = bf16[4,72,128]{2,1,0:T(8,128)(2,1)S(1)} all-to-all(bf16[4,72,128]{2,1,0:T(8,128)(2,1)S(1)} %shard_map.91), channel_id=1, replica_groups=mesh['x'=4,'y'=4,'z'=8,'m0'=2,'m1'=2] {'m0','m1'}, dimensions={0} | all-to-all | bytes 147456 | tf_op jit(solution)/shard_map/all_to_all | solution.py:246
  100.4 0.7 shard_map.92
  (2 shorter events, 0.0 us)
Async XLA Ops:
  0.6 0.7 copy-start
  1.3 0.7 copy-start.1
  3.0 13.9 %copy-start.4 = (bf16[16,1536]{1,0:T(8,128)(2,1)S(1)}, bf16[16,1536]{1,0:T(8,128)(2,1)}, u32[]{:S(2)}) copy-start(bf16[16,1536]{1,0:T(8,128)(2,1)} %param.7) | copy-start | bytes 147460
  3.0 27.7 %all-to-all-start = ((bf16[32,56,128]{2,1,0:T(8,128)(2,1)}), bf16[32,56,128]{2,1,0:T(8,128)(2,1)S(1)}, u32[]{:S(2)}, u32[]{:S(2)}) async-start(bf16[32,56,128]{2,1,0:T(8,128)(2,1)} %shard_map.87), calls=%async_computation | async-start | bytes 917504 | tf_op jit(solution)/shard_map/all_to_all | solution.py:246
  16.8 0.8 copy-start.3
  18.0 12.6 %collective-permute-start = (bf16[32,384]{1,0:T(8,128)(2,1)S(1)}, bf16[32,384]{1,0:T(8,128)(2,1)S(1)}, u32[]{:S(2)}, u32[]{:S(2)}) collective-permute-start(bf16[32,384]{1,0:T(8,128)(2,1)S(1)} %get-tuple-element.12), channel_id=1, source_target_pairs={{0,32},{32,64},{64,96},{96,0},{1,33},{33,65},{65,97},{97,1},{2,34}... | collective-permute-start | bytes 73736 | tf_op jit(solution)/shard_map/ppermute | solution.py:271
  21.2 9.4 %collective-permute-start.1 = (bf16[32,384]{1,0:T(8,128)(2,1)S(1)}, bf16[32,384]{1,0:T(8,128)(2,1)S(1)}, u32[]{:S(2)}, u32[]{:S(2)}) collective-permute-start(bf16[32,384]{1,0:T(8,128)(2,1)S(1)} %get-tuple-element.11), channel_id=1, source_target_pairs={{0,64},{32,96},{64,0},{96,32},{1,65},{33,97},{65,1},{97,33},{2,66}... | collective-permute-start | bytes 73736 | tf_op jit(solution)/shard_map/ppermute | solution.py:271
  25.5 5.1 %collective-permute-start.2 = (bf16[32,384]{1,0:T(8,128)(2,1)S(1)}, bf16[32,384]{1,0:T(8,128)(2,1)S(1)}, u32[]{:S(2)}, u32[]{:S(2)}) collective-permute-start(bf16[32,384]{1,0:T(8,128)(2,1)S(1)} %get-tuple-element.10), channel_id=1, source_target_pairs={{0,96},{32,0},{64,32},{96,64},{1,97},{33,1},{65,33},{97,65},{2,98}... | collective-permute-start | bytes 73736 | tf_op jit(solution)/shard_map/ppermute | solution.py:271
  29.2 0.7 copy-start.2
  53.9 9.8 %collective-permute-start.3 = (bf16[296,128]{1,0:T(8,128)(2,1)S(1)}, bf16[296,128]{1,0:T(8,128)(2,1)S(1)}, u32[]{:S(2)}, u32[]{:S(2)}) collective-permute-start(bf16[296,128]{1,0:T(8,128)(2,1)S(1)} %shard_map.89.own_ref), channel_id=1, source_target_pairs={{0,64},{1,33},{2,482},{3,451},{4,68},{5,37},{6,486},{7,455},{8,72}... | collective-permute-start | bytes 227336 | tf_op jit(solution)/shard_map/ppermute | solution.py:308

commit v6 on v5

--- a/solution.py
+++ b/solution.py
@@ -15,7 +15,7 @@
 DELTA = (-2, -1, 1, 2)
 
 
-def call(body, out_shape, scratch, *args, smem=(), hbm=()):
+def call(body, out_shape, scratch, *args, smem=(), hbm=(), vmem=16):
     spaces = [
         pltpu.SMEM if k in smem else pltpu.HBM if k in hbm else pltpu.VMEM for k in range(len(args))
     ]
@@ -23,7 +23,7 @@
     outs = jax.tree.map(lambda _: pl.BlockSpec(memory_space=pltpu.VMEM), out_shape)
     return pl.pallas_call(
         body, out_shape=out_shape, in_specs=specs, out_specs=outs, scratch_shapes=scratch,
-        compiler_params=pltpu.CompilerParams(vmem_limit_bytes=16 << 20),
+        compiler_params=pltpu.CompilerParams(vmem_limit_bytes=vmem << 20),
     )(*args)
 
 
@@ -114,8 +114,16 @@
             [rows[8 * g : 8 * g + 8, 256 + 32 * g : 288 + 32 * g] for g in range(4)], axis=1
         )
         block = jnp.concatenate([rows[:, 0:128], rows[:, 128:256], tail], axis=0).astype(bf16)
-        for m in range(4):
-            out_ref[4 * y + m] = block
+        for m in range(2):
+            out_ref[2 * y + m] = block
+
+
+def combine(got_ref, out_ref):
+    for m in range(2):
+        pre = got_ref[m].astype(f32)
+        for part in range(1, 4):
+            pre = pre + got_ref[2 * part + m].astype(f32)
+        out_ref[m] = pre
 
 
 def embed(got_ref, consts_ref, own_ref):
@@ -123,9 +131,7 @@
     tiles = []
     tails = []
     for col in range(4):
-        pre = got_ref[col].astype(f32)
-        for part in range(1, 4):
-            pre = pre + got_ref[4 * part + col].astype(f32)
+        pre = got_ref[2 * (col % 2) + col // 2]
         tiles += [pre[0:32], pre[32:64]]
         last = pre[64:72]
         tails.append(
@@ -259,6 +265,7 @@
         w_img,
         w_txt,
         hbm=(0, 1),
+        vmem=60,
     )
     weights = exchange(sent, ("x", "z"))
 
@@ -289,7 +296,7 @@
 
     sent = call(
         project,
-        jax.ShapeDtypeStruct((16, 72, 128), bf16),
+        jax.ShapeDtypeStruct((8, 72, 128), bf16),
         [pltpu.VMEM((4, 32, 384), bf16)],
         where,
         sort,
@@ -298,7 +305,9 @@
         *received,
         smem=(0,),
     )
-    got = exchange(sent, ("y",) + MP)
+    got = exchange(sent, ("y", "m0"))
+    half = call(combine, jax.ShapeDtypeStruct((2, 72, 128), f32), [], got)
+    got = lax.all_gather(half, "m1", axis=0, tiled=True)
     own = call(embed, jax.ShapeDtypeStruct((296, 128), bf16), [], got, consts)
 
     moves = []

time: 102 us -> 97.6 us (0.957)
  blocking collectives: 56.3 us -> 53.6 us
  waiting for transfers between devices: 7.4 us -> 5.79 us
  local copies, waits for them, and re-layouts: 2.51 us -> 1.11 us
    all_to_all x3, blocking collectives: 56.3 us -> 47.3 us  [exchange(): return lax.all_to_all(value, axes, split_axis=0, concat_axis=0, tiled=True)]
    all_gather x0 -> x1, blocking collectives: none -> 6.25 us  [local(): got = lax.all_gather(half, 'm1', axis=0, tiled=True)]
    ppermute x1, waiting for transfers between devices: 7.39 us -> 5.78 us  [local(): other = lax.ppermute(own, BATCH + MP, moves)]
    unnamed x10 -> x6, local copies, waits for them, and re-layouts: 2.16 us -> 0.75 us
    pallas_call x7 -> x8, Pallas kernels: 5.88 us -> 6.59 us  [call(): pl.pallas_call(body, out_shape=out_shape, in_specs=specs, out_specs=outs,...]
where the time goes in v6:
time: 97.6 us; the launch traced here: 97 us
  blocking collectives  53.6 us (55%)
  starting transfers between devices  27.6 us (28%)
  Pallas kernels  6.59 us (7%)
  waiting for transfers between devices  5.79 us (6%)
  between operations  2.21 us (2%)
  local copies, waits for them, and re-layouts  1.11 us (1%)
    all_to_all x3, blocking collectives, exchange(): return lax.all_to_all(value, axes, split_axis=0, concat_axis=0, tiled=True)  47.3 us
    all_to_all x1, starting transfers between devices, exchange(): return lax.all_to_all(value, axes, split_axis=0, concat_axis=0, tiled=True)  13.8 us
    ppermute x3, starting transfers between devices, local(): lax.ppermute(chosen, 'y', [(s, (s + k) % 4) for s in range(4)])  10.4 us
    pallas_call x8, Pallas kernels, call(): pl.pallas_call(body, out_shape=out_shape, in_specs=specs, out_specs=outs,...  6.59 us
    all_gather x1, blocking collectives, local(): got = lax.all_gather(half, 'm1', axis=0, tiled=True)  6.25 us
    ppermute x1, waiting for transfers between devices, local(): other = lax.ppermute(own, BATCH + MP, moves)  5.78 us
    ppermute x1, starting transfers between devices, local(): other = lax.ppermute(own, BATCH + MP, moves)  3.34 us
  transfers between devices with their start and end apart: 5, of which 1 were waited for; matrix products, arithmetic and copies ran while one was open for 0% of the time, Pallas kernels for 1%

profile of v6, /device:TPU:1, one launch (start us, length us, event | category | flops | bytes accessed | tf_op | source)
XLA Modules:
  0.0 97.0 jit_solution(1569508974163457713)
XLA Ops:
  0.6 1.6 %shard_map.87 = bf16[32,56,128]{2,1,0:T(8,128)(2,1)} custom-call(bf16[12,288]{1,0:T(8,128)(2,1)} %img_ref.1, bf16[12,288]{1,0:T(8,128)(2,1)} %txt_ref.1), custom_call_target="tpu_custom_call" | custom-call | tf_op jit(solution)/shard_map/pallas_call | solution.py:24
  2.2 0.0 copy-start.2
  2.2 13.8 %all-to-all-start = ((bf16[32,56,128]{2,1,0:T(8,128)(2,1)}), bf16[32,56,128]{2,1,0:T(8,128)(2,1)S(1)}, u32[]{:S(2)}, u32[]{:S(2)}) async-start(bf16[32,56,128]{2,1,0:T(8,128)(2,1)} %shard_map.87), calls=%async_computation | async-start | bytes 917504 | tf_op jit(solution)/shard_map/all_to_all | solution.py:252
  16.1 0.0 copy-start.1
  16.2 0.0 copy-done.2
  16.2 0.7 copy-done.1
  16.9 0.1 reshape.10
  17.1 0.1 copy.10
  17.1 0.1 reshape.11
  17.3 3.2 %collective-permute-start = (bf16[32,384]{1,0:T(8,128)(2,1)S(1)}, bf16[32,384]{1,0:T(8,128)(2,1)S(1)}, u32[]{:S(2)}, u32[]{:S(2)}) collective-permute-start(bf16[32,384]{1,0:T(8,128)(2,1)S(1)} %get-tuple-element.12), channel_id=1, source_target_pairs={{0,32},{32,64},{64,96},{96,0},{1,33},{33,65},{65,97},{97,1},{2,34}... | collective-permute-start | bytes 73736 | tf_op jit(solution)/shard_map/ppermute | solution.py:278
  20.5 4.2 %collective-permute-start.1 = (bf16[32,384]{1,0:T(8,128)(2,1)S(1)}, bf16[32,384]{1,0:T(8,128)(2,1)S(1)}, u32[]{:S(2)}, u32[]{:S(2)}) collective-permute-start(bf16[32,384]{1,0:T(8,128)(2,1)S(1)} %get-tuple-element.11), channel_id=1, source_target_pairs={{0,64},{32,96},{64,0},{96,32},{1,65},{33,97},{65,1},{97,33},{2,66}... | collective-permute-start | bytes 73736 | tf_op jit(solution)/shard_map/ppermute | solution.py:278
  24.7 3.0 %collective-permute-start.2 = (bf16[32,384]{1,0:T(8,128)(2,1)S(1)}, bf16[32,384]{1,0:T(8,128)(2,1)S(1)}, u32[]{:S(2)}, u32[]{:S(2)}) collective-permute-start(bf16[32,384]{1,0:T(8,128)(2,1)S(1)} %get-tuple-element.10), channel_id=1, source_target_pairs={{0,96},{32,0},{64,32},{96,64},{1,97},{33,1},{65,33},{97,65},{2,98}... | collective-permute-start | bytes 73736 | tf_op jit(solution)/shard_map/ppermute | solution.py:278
  27.7 0.1 pad_add_fusion.where_ref
  28.5 0.0 copy-start
  29.1 0.0 copy-done
  29.2 0.7 shard_map.86
  29.9 0.0 collective-permute-done.r1_ref
  29.9 0.0 collective-permute-done.1.r2_ref
  29.9 0.0 collective-permute-done.2.r3_ref
  29.9 0.0 all-to-all-done.w_ref
  29.9 1.3 %shard_map.88 = bf16[8,72,128]{2,1,0:T(8,128)(2,1)S(1)} custom-call(s32[4]{0:T(128)S(1)} %pad_add_fusion.where_ref, bf16[384,384]{1,0:T(8,128)(2,1)S(1)} %get-tuple-element.8.sort_ref, bf16[384,128]{1,0:T(8,128)(2,1)S(1)} %get-tuple-element.9.split_ref, bf16[32,56,128]{2,1,0:T(8,128)(2,1)S(1)} %all-to-all-done.w_ref, ...), custom_call_target="tpu_custom_call" | custom-call | tf_op jit(solution)/shard_map/pallas_call | solution.py:24
  31.3 12.6 %all_to_all.20.got_ref = bf16[8,72,128]{2,1,0:T(8,128)(2,1)S(1)} all-to-all(bf16[8,72,128]{2,1,0:T(8,128)(2,1)S(1)} %shard_map.88), channel_id=1, replica_groups=mesh['x'=4,'y'=4,'z'=8,'m0'=2,'m1'=2] {'y','m0'}, dimensions={0} | all-to-all | bytes 294912 | tf_op jit(solution)/shard_map/all_to_all | solution.py:252
  43.8 6.2 %all_gather.3.got_ref = f32[4,72,128]{2,1,0:T(8,128)S(1)} all-gather(f32[2,72,128]{2,1,0:T(8,128)S(1)} %shard_map.89), channel_id=1, replica_groups=mesh['x'=4,'y'=4,'z'=8,'m0'=2,'m1'=2] {'m1'}, dimensions={0}, use_global_device_ids=true | all-gather | bytes 221184 | tf_op jit(solution)/shard_map/all_gather | solution.py:310
  50.1 0.2 shard_map.90.own_ref
  50.3 3.3 %collective-permute-start.3 = (bf16[296,128]{1,0:T(8,128)(2,1)S(1)}, bf16[296,128]{1,0:T(8,128)(2,1)S(1)}, u32[]{:S(2)}, u32[]{:S(2)}) collective-permute-start(bf16[296,128]{1,0:T(8,128)(2,1)S(1)} %shard_map.90.own_ref), channel_id=1, source_target_pairs={{0,64},{1,33},{2,482},{3,451},{4,68},{5,37},{6,486},{7,455},{8,72}... | collective-permute-start | bytes 227336 | tf_op jit(solution)/shard_map/ppermute | solution.py:317
  53.7 5.8 %collective-permute-done.3.other_ref = bf16[296,128]{1,0:T(8,128)(2,1)S(1)} collective-permute-done((bf16[296,128]{1,0:T(8,128)(2,1)S(1)}, bf16[296,128]{1,0:T(8,128)(2,1)S(1)}, u32[]{:S(2)}, u32[]{:S(2)}) %collective-permute-start.3) | collective-permute-done | bytes 75808 | tf_op jit(solution)/shard_map/ppermute | solution.py:317
  59.4 0.6 shard_map.91
  60.1 21.1 %all_to_all.21.got_ref = bf16[8,296,128]{2,1,0:T(8,128)(2,1)S(1)} all-to-all(bf16[8,296,128]{2,1,0:T(8,128)(2,1)S(1)} %shard_map.91), channel_id=1, replica_groups=mesh['x'=4,'y'=4,'z'=8,'m0'=2,'m1'=2] {'z'}, dimensions={0} | all-to-all | bytes 1212416 | tf_op jit(solution)/shard_map/all_to_all | solution.py:252
  81.1 1.4 %shard_map.92 = bf16[4,72,128]{2,1,0:T(8,128)(2,1)S(1)} custom-call(s32[4]{0:T(128)S(1)} %pad_add_fusion.where_ref, f32[24,128]{1,0:T(8,128)S(1)} %get-tuple-element.6.consts_ref, s32[16,128]{1,0:T(8,128)S(1)} %get-tuple-element.7.pair_ref, bf16[296,128]{1,0:T(8,128)(2,1)S(1)} %shard_map.90.own_ref, bf16[8,296,128]{2,1,0:T(8,128)(2,1)S(1)} %all_to_all.21.got_ref), custom_call_target="tpu_custom_call" | custom-call | tf_op jit(solution)/shard_map/pallas_call | solution.py:24
  82.5 13.7 %all_to_all.22.got_ref = bf16[4,72,128]{2,1,0:T(8,128)(2,1)S(1)} all-to-all(bf16[4,72,128]{2,1,0:T(8,128)(2,1)S(1)} %shard_map.92), channel_id=1, replica_groups=mesh['x'=4,'y'=4,'z'=8,'m0'=2,'m1'=2] {'m0','m1'}, dimensions={0} | all-to-all | bytes 147456 | tf_op jit(solution)/shard_map/all_to_all | solution.py:252
  96.3 0.7 shard_map.93
  (3 shorter events, 0.1 us)
Async XLA Ops:
  2.2 13.9 %copy-start.2 = (bf16[16,1536]{1,0:T(8,128)(2,1)S(1)}, bf16[16,1536]{1,0:T(8,128)(2,1)}, u32[]{:S(2)}) copy-start(bf16[16,1536]{1,0:T(8,128)(2,1)} %param.7) | copy-start | bytes 147460
  2.2 27.7 %all-to-all-start = ((bf16[32,56,128]{2,1,0:T(8,128)(2,1)}), bf16[32,56,128]{2,1,0:T(8,128)(2,1)S(1)}, u32[]{:S(2)}, u32[]{:S(2)}) async-start(bf16[32,56,128]{2,1,0:T(8,128)(2,1)} %shard_map.87), calls=%async_computation | async-start | bytes 917504 | tf_op jit(solution)/shard_map/all_to_all | solution.py:252
  16.1 0.8 copy-start.1
  17.3 12.6 %collective-permute-start = (bf16[32,384]{1,0:T(8,128)(2,1)S(1)}, bf16[32,384]{1,0:T(8,128)(2,1)S(1)}, u32[]{:S(2)}, u32[]{:S(2)}) collective-permute-start(bf16[32,384]{1,0:T(8,128)(2,1)S(1)} %get-tuple-element.12), channel_id=1, source_target_pairs={{0,32},{32,64},{64,96},{96,0},{1,33},{33,65},{65,97},{97,1},{2,34}... | collective-permute-start | bytes 73736 | tf_op jit(solution)/shard_map/ppermute | solution.py:278
  20.5 9.4 %collective-permute-start.1 = (bf16[32,384]{1,0:T(8,128)(2,1)S(1)}, bf16[32,384]{1,0:T(8,128)(2,1)S(1)}, u32[]{:S(2)}, u32[]{:S(2)}) collective-permute-start(bf16[32,384]{1,0:T(8,128)(2,1)S(1)} %get-tuple-element.11), channel_id=1, source_target_pairs={{0,64},{32,96},{64,0},{96,32},{1,65},{33,97},{65,1},{97,33},{2,66}... | collective-permute-start | bytes 73736 | tf_op jit(solution)/shard_map/ppermute | solution.py:278
  24.7 5.1 %collective-permute-start.2 = (bf16[32,384]{1,0:T(8,128)(2,1)S(1)}, bf16[32,384]{1,0:T(8,128)(2,1)S(1)}, u32[]{:S(2)}, u32[]{:S(2)}) collective-permute-start(bf16[32,384]{1,0:T(8,128)(2,1)S(1)} %get-tuple-element.10), channel_id=1, source_target_pairs={{0,96},{32,0},{64,32},{96,64},{1,97},{33,1},{65,33},{97,65},{2,98}... | collective-permute-start | bytes 73736 | tf_op jit(solution)/shard_map/ppermute | solution.py:278
  28.5 0.7 copy-start
  50.3 9.1 %collective-permute-start.3 = (bf16[296,128]{1,0:T(8,128)(2,1)S(1)}, bf16[296,128]{1,0:T(8,128)(2,1)S(1)}, u32[]{:S(2)}, u32[]{:S(2)}) collective-permute-start(bf16[296,128]{1,0:T(8,128)(2,1)S(1)} %shard_map.90.own_ref), channel_id=1, source_target_pairs={{0,64},{1,33},{2,482},{3,451},{4,68},{5,37},{6,486},{7,455},{8,72}... | collective-permute-start | bytes 227336 | tf_op jit(solution)/shard_map/ppermute | solution.py:317

commit v7 on v6

--- a/solution.py
+++ b/solution.py
@@ -12,7 +12,7 @@
 bf16 = jnp.bfloat16
 f32 = jnp.float32
 epsilon = 1e-06
-DELTA = (-2, -1, 1, 2)
+DELTA = (-1, -2, 1, 2)
 
 
 def call(body, out_shape, scratch, *args, smem=(), hbm=(), vmem=16):
@@ -27,24 +27,45 @@
     )(*args)
 
 
-def pack(img_ref, txt_ref, out_ref, img, txt, sems):
-    copies = [
-        pltpu.make_async_copy(img_ref, img, sems.at[0]),
-        pltpu.make_async_copy(txt_ref, txt, sems.at[1]),
-    ]
+def pack(
+    where_ref, w_img_ref, w_txt_ref, img_ref, txt_ref, pair_ref,
+    out_ref, c0_ref, c1_ref, c2_ref, c3_ref, info_ref,
+    w_img, w_txt, img, txt, pair, feats, sems,
+):
+    moves = ((w_img_ref, w_img), (w_txt_ref, w_txt), (img_ref, img), (txt_ref, txt))
+    moves += ((pair_ref, pair),)
+    copies = [pltpu.make_async_copy(a, b, sems.at[k]) for k, (a, b) in enumerate(moves)]
     for copy in copies:
         copy.start()
     for copy in copies:
         copy.wait()
-    both = jnp.concatenate([img[...].astype(f32), txt[...].astype(f32)], axis=0)
+    both = jnp.concatenate([w_img[...].astype(f32), w_txt[...].astype(f32)], axis=0)
     tail = jnp.concatenate([both[6 * g : 6 * g + 6, 256:288] for g in range(4)], axis=1)
     rows = [both[:, 0:128], both[:, 128:256], tail, jnp.zeros((2, 128), f32)]
     rows = jnp.concatenate(rows, axis=0).astype(bf16)
     for k in range(out_ref.shape[0]):
         out_ref[k] = rows
-
-
-def setup(where_ref, pair_ref, scale_ref, bias_ref, sort_ref, split_ref, pairs_ref, consts_ref):
+    for y in range(4):
+        for which, feat in enumerate((img, txt)):
+            for k in range(4):
+                at = 384 * k + 96 * y
+                feats[y, 16 * which : 16 * which + 16, 96 * k : 96 * k + 96] = feat[
+                    :, at : at + 96
+                ]
+    for k, ref in enumerate((c0_ref, c1_ref, c2_ref, c3_ref)):
+        ref[...] = feats[(where_ref[3] + k) & 3]
+    row = lax.broadcasted_iota(jnp.int32, (16, 128), 0)
+    lane = lax.broadcasted_iota(jnp.int32, (8, 128), 1) & 15
+    down = jnp.zeros((16, 128), jnp.int32)
+    across = jnp.zeros((8, 128), jnp.int32)
+    for k in range(16):
+        down = jnp.where(row == k, pair[k], down)
+        across = jnp.where(lane == k, pair[k], across)
+    info_ref[0:16, :] = down.astype(f32)
+    info_ref[16:24, :] = across.astype(f32)
+
+
+def setup(where_ref, info_ref, scalars_ref, sort_ref, split_ref, pairs_ref, consts_ref):
     r = lax.broadcasted_iota(jnp.int32, (384, 384), 0)
     c = lax.broadcasted_iota(jnp.int32, (384, 384), 1)
     second = r >= 192
@@ -59,18 +80,13 @@
     high = (inner >= 6) & (c == 8 * group + inner - 6)
     split_ref[0:192, :] = jnp.where(low, 1.0, 0.0).astype(bf16)
     split_ref[192:384, :] = jnp.where(high, 1.0, 0.0).astype(bf16)
-    row = lax.broadcasted_iota(jnp.int32, (16, 128), 0)
+    pairs_ref[...] = info_ref[0:16, :].astype(jnp.int32)
+    row = lax.broadcasted_iota(jnp.int32, (8, 128), 0)
     lane = lax.broadcasted_iota(jnp.int32, (8, 128), 1)
-    down = jnp.zeros((16, 128), jnp.int32)
-    across = jnp.zeros((8, 128), jnp.int32)
-    for k in range(16):
-        down = jnp.where(row == k, pair_ref[k], down)
-        across = jnp.where(lane == 16 * where_ref[1] + k, pair_ref[k], across)
-    pairs_ref[...] = down
-    row = lax.broadcasted_iota(jnp.int32, (8, 128), 0)
+    across = info_ref[16:24, :].astype(jnp.int32)
+    across = jnp.where((lane >> 4) == where_ref[1], across, 0)
     consts_ref[0:8, :] = jnp.where(row == 0, across >> 6, across & 63).astype(f32)
-    consts_ref[8:16, :] = jnp.full((8, 128), scale_ref[0], f32)
-    consts_ref[16:24, :] = jnp.full((8, 128), bias_ref[0], f32)
+    consts_ref[8:24, :] = scalars_ref[...]
 
 
 def project(
@@ -151,10 +167,10 @@
     m = where_ref[2]
     two_ref[0] = own_ref[...]
     two_ref[1] = other_ref[...]
-    middle = (m == 1) | (m == 2)
+    near = (m == 0) | (m == 2)
     for to in range(8):
-        other_img = middle | ((m == 0) & (z >= to)) | ((m == 3) & (z < to))
-        other_txt = middle | ((m == 0) & (z > to)) | ((m == 3) & (z <= to))
+        other_img = near | ((m == 1) & (z >= to)) | ((m == 3) & (z < to))
+        other_txt = near | ((m == 1) & (z > to)) | ((m == 3) & (z <= to))
         img = jnp.where(other_img, 1, 0)
         txt = jnp.where(other_txt, 1, 0)
         for t in range(9):
@@ -169,7 +185,7 @@
     octet = where_ref[0]
     z = where_ref[1]
     m = where_ref[2]
-    scale = jnp.exp(consts_ref[8:9, :])
+    scale = consts_ref[8:9, :]
     scale_one = scale[:, 0:1]
     offset = consts_ref[16:17, :]
 
@@ -200,7 +216,7 @@
     there = lane >> 4
     behind = jnp.where(there > z, -2, 0)
     ahead = jnp.where(there > z, 0, 2)
-    delta = jnp.where(m == 0, behind, jnp.where(m == 3, ahead, jnp.where(m == 1, -1, 1)))
+    delta = jnp.where(m == 1, behind, jnp.where(m == 3, ahead, m - 1))
     block = (8 * (octet + delta) + there) & 127
     text_index = block * 16 + (lane & 15)
     match_img = pair_ref[...] == text_index
@@ -258,26 +274,35 @@
     octet = 4 * x + y
     where = jnp.stack([octet, z, m, y]).astype(jnp.int32)
 
-    sent = call(
+    sent, *chosen, info = call(
         pack,
-        jax.ShapeDtypeStruct((32, 56, 128), bf16),
-        [pltpu.VMEM((12, 288), bf16), pltpu.VMEM((12, 288), bf16), pltpu.SemaphoreType.DMA((2,))],
+        (jax.ShapeDtypeStruct((32, 56, 128), bf16),)
+        + (jax.ShapeDtypeStruct((32, 384), bf16),) * 4
+        + (jax.ShapeDtypeStruct((24, 128), f32),),
+        [pltpu.VMEM((12, 288), bf16)] * 2
+        + [pltpu.VMEM((16, 1536), bf16)] * 2
+        + [pltpu.SMEM((16,), jnp.int32)]
+        + [pltpu.VMEM((4, 32, 384), bf16), pltpu.SemaphoreType.DMA((5,))],
+        where,
         w_img,
         w_txt,
-        hbm=(0, 1),
+        img_feat,
+        txt_feat,
+        pair_index,
+        smem=(0,),
+        hbm=(1, 2, 3, 4, 5),
         vmem=60,
     )
     weights = exchange(sent, ("x", "z"))
 
-    feats = jnp.concatenate([img_feat, txt_feat], axis=0).reshape(32, 4, 4, 96)
-    feats = feats.transpose(2, 0, 1, 3).reshape(4, 32, 384)
-    received = [lax.dynamic_index_in_dim(feats, y, 0, keepdims=False)]
+    received = [chosen[0]]
     for k in range(1, 4):
-        chosen = lax.dynamic_index_in_dim(feats, (y + k) % 4, 0, keepdims=False)
         received.append(
-            lax.ppermute(chosen, "y", [(s, (s + k) % 4) for s in range(4)])
-        )
-
+            lax.ppermute(chosen[k], "y", [(s, (s + k) % 4) for s in range(4)])
+        )
+
+    row = lax.broadcasted_iota(jnp.int32, (16, 128), 0)
+    scalars = jnp.where(row < 8, jnp.exp(log_scale[0]), bias[0])
     sort, split, pairs, consts = call(
         setup,
         (
@@ -288,10 +313,9 @@
         ),
         [],
         where,
-        pair_index,
-        log_scale,
-        bias,
-        smem=(0, 1, 2, 3),
+        info,
+        scalars,
+        smem=(0,),
     )
 
     sent = call(

time: 97.6 us -> 97.2 us (level)
  local copies, waits for them, and re-layouts: 1.11 us -> 0.1 us
    ppermute x1, waiting for transfers between devices: 5.78 us -> 4.58 us  [local(): other = lax.ppermute(own, BATCH + MP, moves)]
  transfers between devices with their start and end apart: 5 -> 5, of which waited for: 1 -> 2; matrix products, arithmetic and copies ran while one was open for 0% -> 0% of each run, Pallas kernels for 1% -> 1%
where the time goes in v7:
time: 97.2 us; the launch traced here: 96.5 us
  blocking collectives  53.5 us (55%)
  starting transfers between devices  27.8 us (29%)
  Pallas kernels  7.42 us (8%)
  waiting for transfers between devices  4.94 us (5%)
  between operations  2.17 us (2%)
    all_to_all x3, blocking collectives, exchange(): return lax.all_to_all(value, axes, split_axis=0, concat_axis=0, tiled=True)  47.2 us
    all_to_all x1, starting transfers between devices, exchange(): return lax.all_to_all(value, axes, split_axis=0, concat_axis=0, tiled=True)  13.8 us
    ppermute x3, starting transfers between devices, local(): lax.ppermute(chosen[k], 'y', [(s, (s + k) % 4) for s in range(4)])  10.4 us
    pallas_call x8, Pallas kernels, call(): pl.pallas_call(body, out_shape=out_shape, in_specs=specs, out_specs=outs,...  7.42 us
    all_gather x1, blocking collectives, local(): got = lax.all_gather(half, 'm1', axis=0, tiled=True)  6.25 us
    ppermute x1, waiting for transfers between devices, local(): other = lax.ppermute(own, BATCH + MP, moves)  4.58 us
    ppermute x1, starting transfers between devices, local(): other = lax.ppermute(own, BATCH + MP, moves)  3.54 us
  transfers between devices with their start and end apart: 5, of which 2 were waited for; matrix products, arithmetic and copies ran while one was open for 0% of the time, Pallas kernels for 1%

profile of v7, /device:TPU:1, one launch (start us, length us, event | category | flops | bytes accessed | tf_op | source)
XLA Modules:
  0.0 96.5 jit_solution(10279483283638007942)
XLA Ops:
  0.6 0.7 pad_add_fusion.where_ref
  1.3 2.4 %shard_map.86 = (bf16[32,56,128]{2,1,0:T(8,128)(2,1)}, bf16[32,384]{1,0:T(8,128)(2,1)}, bf16[32,384]{1,0:T(8,128)(2,1)}, bf16[32,384]{1,0:T(8,128)(2,1)}, bf16[32,384]{1,0:T(8,128)(2,1)}, /*index=5*/f32[24,128]{1,0:T(8,128)}) custom-call(s32[4]{0:T(128)} %pad_add_fusion.where_ref, bf16[12,288]{1,0:T(8,128)(2,1)} %w_img_ref.1, bf16[12,288]{1,0:T(8,128)(2,1)} %w_txt_ref.1, ...), custom_call_target="tpu_custom_call" | custom-call | tf_op jit(solution)/shard_map/pallas_call | solution.py:24
  3.7 0.0 copy-start.5
  3.8 0.0 copy-start.4
  3.8 0.0 copy-start.3
  3.8 13.8 %all-to-all-start = ((bf16[32,56,128]{2,1,0:T(8,128)(2,1)}), bf16[32,56,128]{2,1,0:T(8,128)(2,1)S(1)}, u32[]{:S(2)}, u32[]{:S(2)}) async-start(bf16[32,56,128]{2,1,0:T(8,128)(2,1)} %get-tuple-element.17), calls=%async_computation | async-start | bytes 917504 | tf_op jit(solution)/shard_map/all_to_all | solution.py:268
  17.6 0.0 copy-done.5
  17.6 3.2 %collective-permute-start = (bf16[32,384]{1,0:T(8,128)(2,1)S(1)}, bf16[32,384]{1,0:T(8,128)(2,1)S(1)}, u32[]{:S(2)}, u32[]{:S(2)}) collective-permute-start(bf16[32,384]{1,0:T(8,128)(2,1)S(1)} %copy-done.5), channel_id=1, source_target_pairs={{0,32},{32,64},{64,96},{96,0},{1,33},{33,65},{65,97},{97,1},{2,34}... | collective-permute-start | bytes 73736 | tf_op jit(solution)/shard_map/ppermute | solution.py:301
  20.8 0.0 copy-start.1
  20.9 0.0 copy-done.4
  20.9 0.0 copy-start.2
  20.9 4.2 %collective-permute-start.1 = (bf16[32,384]{1,0:T(8,128)(2,1)S(1)}, bf16[32,384]{1,0:T(8,128)(2,1)S(1)}, u32[]{:S(2)}, u32[]{:S(2)}) collective-permute-start(bf16[32,384]{1,0:T(8,128)(2,1)S(1)} %copy-done.4), channel_id=1, source_target_pairs={{0,64},{32,96},{64,0},{96,32},{1,65},{33,97},{65,1},{97,33},{2,66}... | collective-permute-start | bytes 73736 | tf_op jit(solution)/shard_map/ppermute | solution.py:301
  25.1 0.0 copy-done.3
  25.1 0.0 copy-start
  25.1 3.0 %collective-permute-start.2 = (bf16[32,384]{1,0:T(8,128)(2,1)S(1)}, bf16[32,384]{1,0:T(8,128)(2,1)S(1)}, u32[]{:S(2)}, u32[]{:S(2)}) collective-permute-start(bf16[32,384]{1,0:T(8,128)(2,1)S(1)} %copy-done.3), channel_id=1, source_target_pairs={{0,96},{32,0},{64,32},{96,64},{1,97},{33,1},{65,33},{97,65},{2,98}... | collective-permute-start | bytes 73736 | tf_op jit(solution)/shard_map/ppermute | solution.py:301
  29.5 0.1 iota.7.scalars_ref
  29.5 0.0 copy-done.1
  29.5 0.0 copy-done.2
  29.5 0.7 shard_map.87
  30.2 0.0 collective-permute-done.r1_ref
  30.2 0.0 collective-permute-done.1.r2_ref
  30.3 0.0 collective-permute-done.2.r3_ref
  30.3 0.4 all-to-all-done.w_ref
  30.6 0.0 copy-done
  30.6 1.3 %shard_map.88 = bf16[8,72,128]{2,1,0:T(8,128)(2,1)S(1)} custom-call(s32[4]{0:T(128)S(1)} %copy-done.1, bf16[384,384]{1,0:T(8,128)(2,1)S(1)} %get-tuple-element.15.sort_ref, bf16[384,128]{1,0:T(8,128)(2,1)S(1)} %get-tuple-element.16.split_ref, bf16[32,56,128]{2,1,0:T(8,128)(2,1)S(1)} %all-to-all-done.w_ref, bf16[32,384]{1,0:T(8,128)(2,1)S(1)} %copy-done, ...), custom_call_target="tpu_custom_call" | custom-call | tf_op jit(solution)/shard_map/pallas_call | solution.py:24
  32.0 13.4 %all_to_all.20.got_ref = bf16[8,72,128]{2,1,0:T(8,128)(2,1)S(1)} all-to-all(bf16[8,72,128]{2,1,0:T(8,128)(2,1)S(1)} %shard_map.88), channel_id=1, replica_groups=mesh['x'=4,'y'=4,'z'=8,'m0'=2,'m1'=2] {'y','m0'}, dimensions={0} | all-to-all | bytes 294912 | tf_op jit(solution)/shard_map/all_to_all | solution.py:268
  45.4 6.2 %all_gather.3.got_ref = f32[4,72,128]{2,1,0:T(8,128)S(1)} all-gather(f32[2,72,128]{2,1,0:T(8,128)S(1)} %shard_map.89), channel_id=1, replica_groups=mesh['x'=4,'y'=4,'z'=8,'m0'=2,'m1'=2] {'m1'}, dimensions={0}, use_global_device_ids=true | all-gather | bytes 221184 | tf_op jit(solution)/shard_map/all_gather | solution.py:334
  51.6 0.2 shard_map.90.own_ref
  51.9 3.5 %collective-permute-start.3 = (bf16[296,128]{1,0:T(8,128)(2,1)S(1)}, bf16[296,128]{1,0:T(8,128)(2,1)S(1)}, u32[]{:S(2)}, u32[]{:S(2)}) collective-permute-start(bf16[296,128]{1,0:T(8,128)(2,1)S(1)} %shard_map.90.own_ref), channel_id=1, source_target_pairs={{0,32},{1,65},{2,482},{3,451},{4,36},{5,69},{6,486},{7,455},{8,40}... | collective-permute-start | bytes 227336 | tf_op jit(solution)/shard_map/ppermute | solution.py:341
  55.4 4.6 %collective-permute-done.3.other_ref = bf16[296,128]{1,0:T(8,128)(2,1)S(1)} collective-permute-done((bf16[296,128]{1,0:T(8,128)(2,1)S(1)}, bf16[296,128]{1,0:T(8,128)(2,1)S(1)}, u32[]{:S(2)}, u32[]{:S(2)}) %collective-permute-start.3) | collective-permute-done | bytes 75808 | tf_op jit(solution)/shard_map/ppermute | solution.py:341
  60.0 0.6 shard_map.91
  60.6 20.1 %all_to_all.21.got_ref = bf16[8,296,128]{2,1,0:T(8,128)(2,1)S(1)} all-to-all(bf16[8,296,128]{2,1,0:T(8,128)(2,1)S(1)} %shard_map.91), channel_id=1, replica_groups=mesh['x'=4,'y'=4,'z'=8,'m0'=2,'m1'=2] {'z'}, dimensions={0} | all-to-all | bytes 1212416 | tf_op jit(solution)/shard_map/all_to_all | solution.py:268
  80.8 1.4 %shard_map.92 = bf16[4,72,128]{2,1,0:T(8,128)(2,1)S(1)} custom-call(s32[4]{0:T(128)S(1)} %copy-done.1, f32[24,128]{1,0:T(8,128)S(1)} %get-tuple-element.13.consts_ref, s32[16,128]{1,0:T(8,128)S(1)} %get-tuple-element.14.pair_ref, bf16[296,128]{1,0:T(8,128)(2,1)S(1)} %shard_map.90.own_ref, bf16[8,296,128]{2,1,0:T(8,128)(2,1)S(1)} %all_to_all.21.got_ref), custom_call_target="tpu_custom_call" | custom-call | tf_op jit(solution)/shard_map/pallas_call | solution.py:24
  82.2 13.7 %all_to_all.22.got_ref = bf16[4,72,128]{2,1,0:T(8,128)(2,1)S(1)} all-to-all(bf16[4,72,128]{2,1,0:T(8,128)(2,1)S(1)} %shard_map.92), channel_id=1, replica_groups=mesh['x'=4,'y'=4,'z'=8,'m0'=2,'m1'=2] {'m0','m1'}, dimensions={0} | all-to-all | bytes 147456 | tf_op jit(solution)/shard_map/all_to_all | solution.py:268
  95.8 0.7 shard_map.93
  (2 shorter events, 0.0 us)
Async XLA Ops:
  3.7 13.9 %copy-start.5 = (bf16[32,384]{1,0:T(8,128)(2,1)S(1)}, bf16[32,384]{1,0:T(8,128)(2,1)}, u32[]{:S(2)}) copy-start(bf16[32,384]{1,0:T(8,128)(2,1)} %get-tuple-element.19) | copy-start | bytes 73732
  3.8 17.1 %copy-start.4 = (bf16[32,384]{1,0:T(8,128)(2,1)S(1)}, bf16[32,384]{1,0:T(8,128)(2,1)}, u32[]{:S(2)}) copy-start(bf16[32,384]{1,0:T(8,128)(2,1)} %get-tuple-element.20) | copy-start | bytes 73732
  3.8 21.3 %copy-start.3 = (bf16[32,384]{1,0:T(8,128)(2,1)S(1)}, bf16[32,384]{1,0:T(8,128)(2,1)}, u32[]{:S(2)}) copy-start(bf16[32,384]{1,0:T(8,128)(2,1)} %get-tuple-element.21) | copy-start | bytes 73732
  3.8 26.9 %all-to-all-start = ((bf16[32,56,128]{2,1,0:T(8,128)(2,1)}), bf16[32,56,128]{2,1,0:T(8,128)(2,1)S(1)}, u32[]{:S(2)}, u32[]{:S(2)}) async-start(bf16[32,56,128]{2,1,0:T(8,128)(2,1)} %get-tuple-element.17), calls=%async_computation | async-start | bytes 917504 | tf_op jit(solution)/shard_map/all_to_all | solution.py:268
  17.6 12.6 %collective-permute-start = (bf16[32,384]{1,0:T(8,128)(2,1)S(1)}, bf16[32,384]{1,0:T(8,128)(2,1)S(1)}, u32[]{:S(2)}, u32[]{:S(2)}) collective-permute-start(bf16[32,384]{1,0:T(8,128)(2,1)S(1)} %copy-done.5), channel_id=1, source_target_pairs={{0,32},{32,64},{64,96},{96,0},{1,33},{33,65},{65,97},{97,1},{2,34}... | collective-permute-start | bytes 73736 | tf_op jit(solution)/shard_map/ppermute | solution.py:301
  20.8 8.7 %copy-start.1 = (s32[4]{0:T(128)S(1)}, s32[4]{0:T(128)}, u32[]{:S(2)}) copy-start(s32[4]{0:T(128)} %pad_add_fusion.where_ref) | copy-start | bytes 52
  20.9 8.7 %copy-start.2 = (f32[24,128]{1,0:T(8,128)S(1)}, f32[24,128]{1,0:T(8,128)}, u32[]{:S(2)}) copy-start(f32[24,128]{1,0:T(8,128)} %get-tuple-element.12.info_ref) | copy-start | bytes 36868
  20.9 9.4 %collective-permute-start.1 = (bf16[32,384]{1,0:T(8,128)(2,1)S(1)}, bf16[32,384]{1,0:T(8,128)(2,1)S(1)}, u32[]{:S(2)}, u32[]{:S(2)}) collective-permute-start(bf16[32,384]{1,0:T(8,128)(2,1)S(1)} %copy-done.4), channel_id=1, source_target_pairs={{0,64},{32,96},{64,0},{96,32},{1,65},{33,97},{65,1},{97,33},{2,66}... | collective-permute-start | bytes 73736 | tf_op jit(solution)/shard_map/ppermute | solution.py:301
  25.1 5.5 %copy-start = (bf16[32,384]{1,0:T(8,128)(2,1)S(1)}, bf16[32,384]{1,0:T(8,128)(2,1)}, u32[]{:S(2)}) copy-start(bf16[32,384]{1,0:T(8,128)(2,1)} %get-tuple-element.18.r0_ref) | copy-start | bytes 73732
  25.1 5.1 %collective-permute-start.2 = (bf16[32,384]{1,0:T(8,128)(2,1)S(1)}, bf16[32,384]{1,0:T(8,128)(2,1)S(1)}, u32[]{:S(2)}, u32[]{:S(2)}) collective-permute-start(bf16[32,384]{1,0:T(8,128)(2,1)S(1)} %copy-done.3), channel_id=1, source_target_pairs={{0,96},{32,0},{64,32},{96,64},{1,97},{33,1},{65,33},{97,65},{2,98}... | collective-permute-start | bytes 73736 | tf_op jit(solution)/shard_map/ppermute | solution.py:301
  51.9 8.1 %collective-permute-start.3 = (bf16[296,128]{1,0:T(8,128)(2,1)S(1)}, bf16[296,128]{1,0:T(8,128)(2,1)S(1)}, u32[]{:S(2)}, u32[]{:S(2)}) collective-permute-start(bf16[296,128]{1,0:T(8,128)(2,1)S(1)} %shard_map.90.own_ref), channel_id=1, source_target_pairs={{0,32},{1,65},{2,482},{3,451},{4,36},{5,69},{6,486},{7,455},{8,40}... | collective-permute-start | bytes 227336 | tf_op jit(solution)/shard_map/ppermute | solution.py:341

commit v8 on v6

--- a/solution.py
+++ b/solution.py
@@ -7,12 +7,15 @@
 from jax.sharding import PartitionSpec as P
 
 
-BATCH = ("x", "y", "z")
+X = ("x1", "x0")
+Z = ("z2", "z1", "z0")
+BATCH = X + ("y",) + Z
+SPREAD = ("z0", "x0", "z1", "x1", "z2")
 MP = ("m0", "m1")
 bf16 = jnp.bfloat16
 f32 = jnp.float32
 epsilon = 1e-06
-DELTA = (-2, -1, 1, 2)
+DELTA = (-1, -2, 1, 2)
 
 
 def call(body, out_shape, scratch, *args, smem=(), hbm=(), vmem=16):
@@ -44,7 +47,7 @@
         out_ref[k] = rows
 
 
-def setup(where_ref, pair_ref, scale_ref, bias_ref, sort_ref, split_ref, pairs_ref, consts_ref):
+def setup(where_ref, pair_ref, sort_ref, split_ref, pairs_ref, codes_ref):
     r = lax.broadcasted_iota(jnp.int32, (384, 384), 0)
     c = lax.broadcasted_iota(jnp.int32, (384, 384), 1)
     second = r >= 192
@@ -68,9 +71,7 @@
         across = jnp.where(lane == 16 * where_ref[1] + k, pair_ref[k], across)
     pairs_ref[...] = down
     row = lax.broadcasted_iota(jnp.int32, (8, 128), 0)
-    consts_ref[0:8, :] = jnp.where(row == 0, across >> 6, across & 63).astype(f32)
-    consts_ref[8:16, :] = jnp.full((8, 128), scale_ref[0], f32)
-    consts_ref[16:24, :] = jnp.full((8, 128), bias_ref[0], f32)
+    codes_ref[...] = jnp.where(row == 0, across >> 6, across & 63).astype(f32)
 
 
 def project(
@@ -81,7 +82,11 @@
     high = split_ref[192:384, :]
     weights = [[], []]
     for half in range(2):
-        some = w_ref[16 * half : 16 * half + 16]
+        places = []
+        for q in range(16 * half, 16 * half + 16):
+            x1, x0, z2, z1, z0 = (q >> 4) & 1, (q >> 3) & 1, (q >> 2) & 1, (q >> 1) & 1, q & 1
+            places.append(16 * z0 + 8 * x0 + 4 * z1 + 2 * x1 + z2)
+        some = jnp.stack([w_ref[place] for place in places], axis=0)
         main = jnp.concatenate(
             [some[:, 0:24].reshape(384, 128), some[:, 24:48].reshape(384, 128)], axis=1
         )
@@ -126,7 +131,7 @@
         out_ref[m] = pre
 
 
-def embed(got_ref, consts_ref, own_ref):
+def embed(got_ref, codes_ref, own_ref):
     total = jnp.zeros((32, 1), f32)
     tiles = []
     tails = []
@@ -143,7 +148,7 @@
     norm = lax.rsqrt(total + epsilon)
     for t, pre in enumerate(tiles):
         own_ref[32 * t : 32 * t + 32, :] = (pre * norm).astype(bf16)
-    own_ref[288:296, :] = consts_ref[0:8, :].astype(bf16)
+    own_ref[288:296, :] = codes_ref[...].astype(bf16)
 
 
 def choose(where_ref, own_ref, other_ref, out_ref, two_ref):
@@ -151,10 +156,10 @@
     m = where_ref[2]
     two_ref[0] = own_ref[...]
     two_ref[1] = other_ref[...]
-    middle = (m == 1) | (m == 2)
+    near = (m == 0) | (m == 2)
     for to in range(8):
-        other_img = middle | ((m == 0) & (z >= to)) | ((m == 3) & (z < to))
-        other_txt = middle | ((m == 0) & (z > to)) | ((m == 3) & (z <= to))
+        other_img = near | ((m == 1) & (z >= to)) | ((m == 3) & (z < to))
+        other_txt = near | ((m == 1) & (z > to)) | ((m == 3) & (z <= to))
         img = jnp.where(other_img, 1, 0)
         txt = jnp.where(other_txt, 1, 0)
         for t in range(9):
@@ -165,13 +170,13 @@
         out_ref[to, 288:296, :] = two_ref[img, 288:296, :]
 
 
-def score(where_ref, consts_ref, pair_ref, own_ref, got_ref, out_ref):
+def score(where_ref, scalars_ref, pair_ref, own_ref, got_ref, out_ref):
     octet = where_ref[0]
     z = where_ref[1]
     m = where_ref[2]
-    scale = jnp.exp(consts_ref[8:9, :])
+    scale = scalars_ref[0:1, :]
     scale_one = scale[:, 0:1]
-    offset = consts_ref[16:17, :]
+    offset = scalars_ref[8:9, :]
 
     def window(at):
         return jnp.concatenate(
@@ -200,7 +205,7 @@
     there = lane >> 4
     behind = jnp.where(there > z, -2, 0)
     ahead = jnp.where(there > z, 0, 2)
-    delta = jnp.where(m == 0, behind, jnp.where(m == 3, ahead, jnp.where(m == 1, -1, 1)))
+    delta = jnp.where(m == 1, behind, jnp.where(m == 3, ahead, m - 1))
     block = (8 * (octet + delta) + there) & 127
     text_index = block * 16 + (lane & 15)
     match_img = pair_ref[...] == text_index
@@ -253,7 +258,7 @@
 
 
 def local(img_feat, txt_feat, w_img, w_txt, pair_index, log_scale, bias):
-    x, y, z = (lax.axis_index(a) for a in BATCH)
+    x, y, z = (lax.axis_index(a) for a in (X, "y", Z))
     m = lax.axis_index(MP)
     octet = 4 * x + y
     where = jnp.stack([octet, z, m, y]).astype(jnp.int32)
@@ -267,7 +272,7 @@
         hbm=(0, 1),
         vmem=60,
     )
-    weights = exchange(sent, ("x", "z"))
+    weights = exchange(sent, SPREAD)
 
     feats = jnp.concatenate([img_feat, txt_feat], axis=0).reshape(32, 4, 4, 96)
     feats = feats.transpose(2, 0, 1, 3).reshape(4, 32, 384)
@@ -278,20 +283,18 @@
             lax.ppermute(chosen, "y", [(s, (s + k) % 4) for s in range(4)])
         )
 
-    sort, split, pairs, consts = call(
+    sort, split, pairs, codes = call(
         setup,
         (
             jax.ShapeDtypeStruct((384, 384), bf16),
             jax.ShapeDtypeStruct((384, 128), bf16),
             jax.ShapeDtypeStruct((16, 128), jnp.int32),
-            jax.ShapeDtypeStruct((24, 128), f32),
+            jax.ShapeDtypeStruct((8, 128), f32),
         ),
         [],
         where,
         pair_index,
-        log_scale,
-        bias,
-        smem=(0, 1, 2, 3),
+        smem=(0, 1),
     )
 
     sent = call(
@@ -308,13 +311,16 @@
     got = exchange(sent, ("y", "m0"))
     half = call(combine, jax.ShapeDtypeStruct((2, 72, 128), f32), [], got)
     got = lax.all_gather(half, "m1", axis=0, tiled=True)
-    own = call(embed, jax.ShapeDtypeStruct((296, 128), bf16), [], got, consts)
+    own = call(embed, jax.ShapeDtypeStruct((296, 128), bf16), [], got, codes)
 
     moves = []
     for s in range(512):
         o, rest = divmod(s, 32)
         moves.append((s, 32 * ((o - DELTA[rest % 4]) % 16) + rest))
+    own, log_scale, bias = lax.optimization_barrier((own, log_scale, bias))
     other = lax.ppermute(own, BATCH + MP, moves)
+    row = lax.broadcasted_iota(jnp.int32, (16, 128), 0)
+    scalars = jnp.where(row < 8, jnp.exp(log_scale[0]), bias[0])
     sent = call(
         choose,
         jax.ShapeDtypeStruct((8, 296, 128), bf16),
@@ -324,13 +330,13 @@
         other,
         smem=(0,),
     )
-    got = exchange(sent, "z")
+    got = exchange(sent, Z)
     sent = call(
         score,
         jax.ShapeDtypeStruct((4, 72, 128), bf16),
         [],
         where,
-        consts,
+        scalars,
         pairs,
         own,
         got,
@@ -346,7 +352,7 @@
 
 
 def solution(mesh):
-    finer = Mesh(mesh.devices.reshape(4, 4, 8, 2, 2), BATCH + MP)
+    finer = Mesh(mesh.devices.reshape(2, 2, 4, 2, 2, 2, 2, 2), BATCH + MP)
     in_specs = (P(BATCH, None), P(BATCH, None), P(BATCH, MP), P(BATCH, MP), P(BATCH), P(), P())
     out_specs = (P(BATCH, MP), P(BATCH + MP, None))
 

time: 97.6 us -> 98.2 us (level)
  blocking collectives: 53.6 us -> 32.5 us
  waiting for transfers between devices: 5.79 us -> 22.3 us
  starting transfers between devices: 27.6 us -> 31.3 us
    all_to_all x3 -> x2, blocking collectives: 47.3 us -> 26.1 us  [exchange(): return lax.all_to_all(value, axes, split_axis=0, concat_axis=0, tiled=True)]
    all_to_all x1 -> x2, waiting for transfers between devices: 0.01 us -> 17.2 us  [exchange(): return lax.all_to_all(value, axes, split_axis=0, concat_axis=0, tiled=True)]
    all_to_all x1 -> x2, starting transfers between devices: 13.8 us -> 17.4 us  [exchange(): return lax.all_to_all(value, axes, split_axis=0, concat_axis=0, tiled=True)]
    ppermute x1, waiting for transfers between devices: 5.78 us -> 4.58 us  [local(): other = lax.ppermute(own, BATCH + MP, moves)]
  transfers between devices with their start and end apart: 5 -> 6, of which waited for: 1 -> 4; matrix products, arithmetic and copies ran while one was open for 0% -> 0% of each run, Pallas kernels for 1% -> 1%
where the time goes in v8:
time: 98.2 us; the launch traced here: 97.5 us
  blocking collectives  32.5 us (33%)
  starting transfers between devices  31.3 us (32%)
  waiting for transfers between devices  22.3 us (23%)
  Pallas kernels  7.42 us (8%)
  between operations  2.22 us (2%)
  local copies, waits for them, and re-layouts  1.74 us (2%)
    all_to_all x2, blocking collectives, exchange(): return lax.all_to_all(value, axes, split_axis=0, concat_axis=0, tiled=True)  26.1 us
    all_to_all x2, starting transfers between devices, exchange(): return lax.all_to_all(value, axes, split_axis=0, concat_axis=0, tiled=True)  17.4 us
    all_to_all x2, waiting for transfers between devices, exchange(): return lax.all_to_all(value, axes, split_axis=0, concat_axis=0, tiled=True)  17.2 us
    ppermute x3, starting transfers between devices, local(): lax.ppermute(chosen, 'y', [(s, (s + k) % 4) for s in range(4)])  10.4 us
    pallas_call x8, Pallas kernels, call(): pl.pallas_call(body, out_shape=out_shape, in_specs=specs, out_specs=outs,...  7.42 us
    all_gather x1, blocking collectives, local(): got = lax.all_gather(half, 'm1', axis=0, tiled=True)  6.36 us
    ppermute x1, waiting for transfers between devices, local(): other = lax.ppermute(own, BATCH + MP, moves)  4.58 us
    ppermute x1, starting transfers between devices, local(): other = lax.ppermute(own, BATCH + MP, moves)  3.54 us
  transfers between devices with their start and end apart: 6, of which 4 were waited for; matrix products, arithmetic and copies ran while one was open for 0% of the time, Pallas kernels for 1%

profile of v8, /device:TPU:1, one launch (start us, length us, event | category | flops | bytes accessed | tf_op | source)
XLA Modules:
  0.0 97.5 jit_solution(9095555465828412590)
XLA Ops:
  0.6 1.6 %shard_map.87 = bf16[32,56,128]{2,1,0:T(8,128)(2,1)} custom-call(bf16[12,288]{1,0:T(8,128)(2,1)} %img_ref.1, bf16[12,288]{1,0:T(8,128)(2,1)} %txt_ref.1), custom_call_target="tpu_custom_call" | custom-call | tf_op jit(solution)/shard_map/pallas_call | solution.py:27
  2.2 0.0 copy-start.2
  2.3 13.8 %all-to-all-start = ((bf16[32,56,128]{2,1,0:T(8,128)(2,1)}), bf16[32,56,128]{2,1,0:T(8,128)(2,1)S(1)}, u32[]{:S(2)}, u32[]{:S(2)}) async-start(bf16[32,56,128]{2,1,0:T(8,128)(2,1)} %shard_map.87), calls=%async_computation | async-start | bytes 917504 | tf_op jit(solution)/shard_map/all_to_all | solution.py:257
  16.1 0.0 copy-start.1
  16.2 0.0 copy-done.2
  16.2 0.7 copy-done.1
  16.9 0.1 reshape.11
  17.1 0.1 copy.10
  17.1 0.1 reshape.12
  17.3 3.2 %collective-permute-start = (bf16[32,384]{1,0:T(8,128)(2,1)S(1)}, bf16[32,384]{1,0:T(8,128)(2,1)S(1)}, u32[]{:S(2)}, u32[]{:S(2)}) collective-permute-start(bf16[32,384]{1,0:T(8,128)(2,1)S(1)} %get-tuple-element.18), channel_id=1, source_target_pairs={{0,32},{32,64},{64,96},{96,0},{1,33},{33,65},{65,97},{97,1},{2,34}... | collective-permute-start | bytes 73736 | tf_op jit(solution)/shard_map/ppermute | solution.py:283
  20.5 4.2 %collective-permute-start.1 = (bf16[32,384]{1,0:T(8,128)(2,1)S(1)}, bf16[32,384]{1,0:T(8,128)(2,1)S(1)}, u32[]{:S(2)}, u32[]{:S(2)}) collective-permute-start(bf16[32,384]{1,0:T(8,128)(2,1)S(1)} %get-tuple-element.17), channel_id=1, source_target_pairs={{0,64},{32,96},{64,0},{96,32},{1,65},{33,97},{65,1},{97,33},{2,66}... | collective-permute-start | bytes 73736 | tf_op jit(solution)/shard_map/ppermute | solution.py:283
  24.8 3.0 %collective-permute-start.2 = (bf16[32,384]{1,0:T(8,128)(2,1)S(1)}, bf16[32,384]{1,0:T(8,128)(2,1)S(1)}, u32[]{:S(2)}, u32[]{:S(2)}) collective-permute-start(bf16[32,384]{1,0:T(8,128)(2,1)S(1)} %get-tuple-element.16), channel_id=1, source_target_pairs={{0,96},{32,0},{64,32},{96,64},{1,97},{33,1},{65,33},{97,65},{2,98}... | collective-permute-start | bytes 73736 | tf_op jit(solution)/shard_map/ppermute | solution.py:283
  27.8 0.0 copy-start
  27.8 0.1 pad_add_fusion.where_ref
  27.9 0.6 copy-done
  28.4 0.7 shard_map.86
  29.1 0.0 collective-permute-done.r1_ref
  29.1 0.0 collective-permute-done.1.r2_ref
  29.2 0.5 collective-permute-done.2.r3_ref
  29.6 1.6 %all-to-all-done.w_ref = bf16[32,56,128]{2,1,0:T(8,128)(2,1)S(1)} async-done(((bf16[32,56,128]{2,1,0:T(8,128)(2,1)}), bf16[32,56,128]{2,1,0:T(8,128)(2,1)S(1)}, u32[]{:S(2)}, u32[]{:S(2)}) %all-to-all-start) | async-done | bytes 458784 | tf_op jit(solution)/shard_map/all_to_all | solution.py:257
  31.2 1.3 %shard_map.88 = bf16[8,72,128]{2,1,0:T(8,128)(2,1)S(1)} custom-call(s32[4]{0:T(128)S(1)} %pad_add_fusion.where_ref, bf16[384,384]{1,0:T(8,128)(2,1)S(1)} %get-tuple-element.9.sort_ref, bf16[384,128]{1,0:T(8,128)(2,1)S(1)} %get-tuple-element.10.split_ref, bf16[32,56,128]{2,1,0:T(8,128)(2,1)S(1)} %all-to-all-done.w_ref, ...), custom_call_target="tpu_custom_call" | custom-call | tf_op jit(solution)/shard_map/pallas_call | solution.py:27
  32.6 13.4 %all_to_all.20.got_ref = bf16[8,72,128]{2,1,0:T(8,128)(2,1)S(1)} all-to-all(bf16[8,72,128]{2,1,0:T(8,128)(2,1)S(1)} %shard_map.88), channel_id=1, replica_groups=mesh['x1'=2,'x0'=2,'y'=4,'z2'=2,'z1'=2,'z0'=2,'m0'=2,'m1'=2] {'y','m0'}, dimensions={0} | all-to-all | bytes 294912 | tf_op jit(solution)/shard_map/all_to_all | solution.py:257
  46.0 6.4 %all_gather.3.got_ref = f32[4,72,128]{2,1,0:T(8,128)S(1)} all-gather(f32[2,72,128]{2,1,0:T(8,128)S(1)} %shard_map.89), channel_id=1, replica_groups=mesh['x1'=2,'x0'=2,'y'=4,'z2'=2,'z1'=2,'z0'=2,'m0'=2,'m1'=2] {'m1'}, dimensions={0}, use_global_device_ids=true | all-gather | bytes 221184 | tf_op jit(solution)/shard_map/all_gather | solution.py:313
  52.3 0.2 shard_map.90.own_ref
  52.6 3.5 %collective-permute-start.3 = (bf16[296,128]{1,0:T(8,128)(2,1)S(1)}, bf16[296,128]{1,0:T(8,128)(2,1)S(1)}, u32[]{:S(2)}, u32[]{:S(2)}) collective-permute-start(bf16[296,128]{1,0:T(8,128)(2,1)S(1)} %shard_map.90.own_ref), channel_id=1, source_target_pairs={{0,32},{1,65},{2,482},{3,451},{4,36},{5,69},{6,486},{7,455},{8,40}... | collective-permute-start | bytes 227336 | tf_op jit(solution)/shard_map/ppermute | solution.py:321
  56.1 4.6 %collective-permute-done.3.other_ref = bf16[296,128]{1,0:T(8,128)(2,1)S(1)} collective-permute-done((bf16[296,128]{1,0:T(8,128)(2,1)S(1)}, bf16[296,128]{1,0:T(8,128)(2,1)S(1)}, u32[]{:S(2)}, u32[]{:S(2)}) %collective-permute-start.3) | collective-permute-done | bytes 75808 | tf_op jit(solution)/shard_map/ppermute | solution.py:321
  60.7 1.4 %shard_map.91 = bf16[8,296,128]{2,1,0:T(8,128)(2,1)} custom-call(s32[4]{0:T(128)S(1)} %pad_add_fusion.where_ref, bf16[296,128]{1,0:T(8,128)(2,1)S(1)} %shard_map.90.own_ref, bf16[296,128]{1,0:T(8,128)(2,1)S(1)} %collective-permute-done.3.other_ref), custom_call_target="tpu_custom_call" | custom-call | tf_op jit(solution)/shard_map/pallas_call | solution.py:27
  62.1 3.5 %all-to-all-start.2 = ((bf16[8,296,128]{2,1,0:T(8,128)(2,1)}), bf16[8,296,128]{2,1,0:T(8,128)(2,1)S(1)}, u32[]{:S(2)}, u32[]{:S(2)}) async-start(bf16[8,296,128]{2,1,0:T(8,128)(2,1)} %shard_map.91), calls=%async_computation.2 | async-start | bytes 1212416 | tf_op jit(solution)/shard_map/all_to_all | solution.py:257
  67.0 15.6 %all-to-all-done.2.got_ref = bf16[8,296,128]{2,1,0:T(8,128)(2,1)S(1)} async-done(((bf16[8,296,128]{2,1,0:T(8,128)(2,1)}), bf16[8,296,128]{2,1,0:T(8,128)(2,1)S(1)}, u32[]{:S(2)}, u32[]{:S(2)}) %all-to-all-start.2) | async-done | bytes 606240 | tf_op jit(solution)/shard_map/all_to_all | solution.py:257
  82.6 0.1 iota.7.scalars_ref
  82.7 1.4 %shard_map.92 = bf16[4,72,128]{2,1,0:T(8,128)(2,1)S(1)} custom-call(s32[4]{0:T(128)S(1)} %pad_add_fusion.where_ref, f32[16,128]{1,0:T(8,128)S(1)} %iota.7.scalars_ref, s32[16,128]{1,0:T(8,128)S(1)} %get-tuple-element.14.pair_ref, bf16[296,128]{1,0:T(8,128)(2,1)S(1)} %shard_map.90.own_ref, bf16[8,296,128]{2,1,0:T(8,128)(2,1)S(1)} %all-to-all-done.2.got_ref), custom_call_target="tpu_custom_call" | custom-call | tf_op jit(solution)/shard_map/pallas_call | solution.py:27
  84.1 12.7 %all_to_all.21.got_ref = bf16[4,72,128]{2,1,0:T(8,128)(2,1)S(1)} all-to-all(bf16[4,72,128]{2,1,0:T(8,128)(2,1)S(1)} %shard_map.92), channel_id=1, replica_groups=mesh['x1'=2,'x0'=2,'y'=4,'z2'=2,'z1'=2,'z0'=2,'m0'=2,'m1'=2] {'m0','m1'}, dimensions={0} | all-to-all | bytes 147456 | tf_op jit(solution)/shard_map/all_to_all | solution.py:257
  96.9 0.7 shard_map.93
  (4 shorter events, 0.1 us)
Async XLA Ops:
  2.2 13.9 %copy-start.2 = (bf16[16,1536]{1,0:T(8,128)(2,1)S(1)}, bf16[16,1536]{1,0:T(8,128)(2,1)}, u32[]{:S(2)}) copy-start(bf16[16,1536]{1,0:T(8,128)(2,1)} %param.7) | copy-start | bytes 147460
  2.3 29.0 %all-to-all-start = ((bf16[32,56,128]{2,1,0:T(8,128)(2,1)}), bf16[32,56,128]{2,1,0:T(8,128)(2,1)S(1)}, u32[]{:S(2)}, u32[]{:S(2)}) async-start(bf16[32,56,128]{2,1,0:T(8,128)(2,1)} %shard_map.87), calls=%async_computation | async-start | bytes 917504 | tf_op jit(solution)/shard_map/all_to_all | solution.py:257
  16.1 0.8 copy-start.1
  17.3 11.8 %collective-permute-start = (bf16[32,384]{1,0:T(8,128)(2,1)S(1)}, bf16[32,384]{1,0:T(8,128)(2,1)S(1)}, u32[]{:S(2)}, u32[]{:S(2)}) collective-permute-start(bf16[32,384]{1,0:T(8,128)(2,1)S(1)} %get-tuple-element.18), channel_id=1, source_target_pairs={{0,32},{32,64},{64,96},{96,0},{1,33},{33,65},{65,97},{97,1},{2,34}... | collective-permute-start | bytes 73736 | tf_op jit(solution)/shard_map/ppermute | solution.py:283
  20.5 8.6 %collective-permute-start.1 = (bf16[32,384]{1,0:T(8,128)(2,1)S(1)}, bf16[32,384]{1,0:T(8,128)(2,1)S(1)}, u32[]{:S(2)}, u32[]{:S(2)}) collective-permute-start(bf16[32,384]{1,0:T(8,128)(2,1)S(1)} %get-tuple-element.17), channel_id=1, source_target_pairs={{0,64},{32,96},{64,0},{96,32},{1,65},{33,97},{65,1},{97,33},{2,66}... | collective-permute-start | bytes 73736 | tf_op jit(solution)/shard_map/ppermute | solution.py:283
  24.8 4.9 %collective-permute-start.2 = (bf16[32,384]{1,0:T(8,128)(2,1)S(1)}, bf16[32,384]{1,0:T(8,128)(2,1)S(1)}, u32[]{:S(2)}, u32[]{:S(2)}) collective-permute-start(bf16[32,384]{1,0:T(8,128)(2,1)S(1)} %get-tuple-element.16), channel_id=1, source_target_pairs={{0,96},{32,0},{64,32},{96,64},{1,97},{33,1},{65,33},{97,65},{2,98}... | collective-permute-start | bytes 73736 | tf_op jit(solution)/shard_map/ppermute | solution.py:283
  27.8 0.7 copy-start
  52.6 8.1 %collective-permute-start.3 = (bf16[296,128]{1,0:T(8,128)(2,1)S(1)}, bf16[296,128]{1,0:T(8,128)(2,1)S(1)}, u32[]{:S(2)}, u32[]{:S(2)}) collective-permute-start(bf16[296,128]{1,0:T(8,128)(2,1)S(1)} %shard_map.90.own_ref), channel_id=1, source_target_pairs={{0,32},{1,65},{2,482},{3,451},{4,36},{5,69},{6,486},{7,455},{8,40}... | collective-permute-start | bytes 227336 | tf_op jit(solution)/shard_map/ppermute | solution.py:321
  62.1 20.5 %all-to-all-start.2 = ((bf16[8,296,128]{2,1,0:T(8,128)(2,1)}), bf16[8,296,128]{2,1,0:T(8,128)(2,1)S(1)}, u32[]{:S(2)}, u32[]{:S(2)}) async-start(bf16[8,296,128]{2,1,0:T(8,128)(2,1)} %shard_map.91), calls=%async_computation.2 | async-start | bytes 1212416 | tf_op jit(solution)/shard_map/all_to_all | solution.py:257

commit v9 on v8

--- a/solution.py
+++ b/solution.py
@@ -18,36 +18,63 @@
 DELTA = (-1, -2, 1, 2)
 
 
-def call(body, out_shape, scratch, *args, smem=(), hbm=(), vmem=16):
+def call(body, out_shape, scratch, *args, smem=(), hbm=(), out=pltpu.VMEM, vmem=16):
     spaces = [
         pltpu.SMEM if k in smem else pltpu.HBM if k in hbm else pltpu.VMEM for k in range(len(args))
     ]
     specs = [pl.BlockSpec(memory_space=space) for space in spaces]
-    outs = jax.tree.map(lambda _: pl.BlockSpec(memory_space=pltpu.VMEM), out_shape)
+    outs = jax.tree.map(lambda _: pl.BlockSpec(memory_space=out), out_shape)
     return pl.pallas_call(
         body, out_shape=out_shape, in_specs=specs, out_specs=outs, scratch_shapes=scratch,
         compiler_params=pltpu.CompilerParams(vmem_limit_bytes=vmem << 20),
     )(*args)
 
 
-def pack(img_ref, txt_ref, out_ref, img, txt, sems):
-    copies = [
-        pltpu.make_async_copy(img_ref, img, sems.at[0]),
-        pltpu.make_async_copy(txt_ref, txt, sems.at[1]),
+def pack(
+    w_img_ref, w_txt_ref, img_ref, txt_ref, out_ref, c0_ref, c1_ref, c2_ref, c3_ref,
+    w_img, w_txt, img, txt, rows, feats, in_sems, out_sems,
+):
+    moves = ((w_img_ref, w_img), (w_txt_ref, w_txt), (img_ref, img), (txt_ref, txt))
+    reads = [pltpu.make_async_copy(a, b, in_sems.at[k]) for k, (a, b) in enumerate(moves)]
+    for copy in reads:
+        copy.start()
+    for copy in reads[:2]:
+        copy.wait()
+    both = jnp.concatenate([w_img[...].astype(f32), w_txt[...].astype(f32)], axis=0)
+    tail = jnp.concatenate([both[6 * g : 6 * g + 6, 256:288] for g in range(4)], axis=1)
+    block = [both[:, 0:128], both[:, 128:256], tail, jnp.zeros((2, 128), f32)]
+    block = jnp.concatenate(block, axis=0).astype(bf16)
+    for k in range(8):
+        rows[k] = block
+    writes = [
+        pltpu.make_async_copy(rows, out_ref.at[8 * k : 8 * k + 8], out_sems.at[k])
+        for k in range(4)
     ]
-    for copy in copies:
+    for copy in writes:
         copy.start()
-    for copy in copies:
+    for copy in reads[2:]:
         copy.wait()
-    both = jnp.concatenate([img[...].astype(f32), txt[...].astype(f32)], axis=0)
-    tail = jnp.concatenate([both[6 * g : 6 * g + 6, 256:288] for g in range(4)], axis=1)
-    rows = [both[:, 0:128], both[:, 128:256], tail, jnp.zeros((2, 128), f32)]
-    rows = jnp.concatenate(rows, axis=0).astype(bf16)
-    for k in range(out_ref.shape[0]):
-        out_ref[k] = rows
-
-
-def setup(where_ref, pair_ref, sort_ref, split_ref, pairs_ref, codes_ref):
+    for y in range(4):
+        for which, feat in enumerate((img, txt)):
+            for k in range(4):
+                at = 384 * k + 96 * y
+                feats[y, 16 * which : 16 * which + 16, 96 * k : 96 * k + 96] = feat[
+                    :, at : at + 96
+                ]
+    here = lax.axis_index("y")
+    more = [
+        pltpu.make_async_copy(feats.at[(here + k) & 3], ref, out_sems.at[4 + k])
+        for k, ref in enumerate((c0_ref, c1_ref, c2_ref, c3_ref))
+    ]
+    for copy in more:
+        copy.start()
+    for copy in writes + more:
+        copy.wait()
+
+
+def setup(
+    where_ref, pair_ref, scale_ref, bias_ref, sort_ref, split_ref, pairs_ref, codes_ref, scalars_ref
+):
     r = lax.broadcasted_iota(jnp.int32, (384, 384), 0)
     c = lax.broadcasted_iota(jnp.int32, (384, 384), 1)
     second = r >= 192
@@ -72,6 +99,8 @@
     pairs_ref[...] = down
     row = lax.broadcasted_iota(jnp.int32, (8, 128), 0)
     codes_ref[...] = jnp.where(row == 0, across >> 6, across & 63).astype(f32)
+    scalars_ref[0:8, :] = jnp.exp(jnp.full((8, 128), scale_ref[0], f32))
+    scalars_ref[8:16, :] = jnp.full((8, 128), bias_ref[0], f32)
 
 
 def project(
@@ -263,38 +292,45 @@
     octet = 4 * x + y
     where = jnp.stack([octet, z, m, y]).astype(jnp.int32)
 
-    sent = call(
+    sent, *chosen = call(
         pack,
-        jax.ShapeDtypeStruct((32, 56, 128), bf16),
-        [pltpu.VMEM((12, 288), bf16), pltpu.VMEM((12, 288), bf16), pltpu.SemaphoreType.DMA((2,))],
+        (jax.ShapeDtypeStruct((32, 56, 128), bf16),)
+        + (jax.ShapeDtypeStruct((32, 384), bf16),) * 4,
+        [pltpu.VMEM((12, 288), bf16)] * 2
+        + [pltpu.VMEM((16, 1536), bf16)] * 2
+        + [pltpu.VMEM((8, 56, 128), bf16), pltpu.VMEM((4, 32, 384), bf16)]
+        + [pltpu.SemaphoreType.DMA((4,)), pltpu.SemaphoreType.DMA((8,))],
         w_img,
         w_txt,
-        hbm=(0, 1),
+        img_feat,
+        txt_feat,
+        hbm=(0, 1, 2, 3),
+        out=pltpu.HBM,
         vmem=60,
     )
     weights = exchange(sent, SPREAD)
 
-    feats = jnp.concatenate([img_feat, txt_feat], axis=0).reshape(32, 4, 4, 96)
-    feats = feats.transpose(2, 0, 1, 3).reshape(4, 32, 384)
-    received = [lax.dynamic_index_in_dim(feats, y, 0, keepdims=False)]
+    received = [chosen[0]]
     for k in range(1, 4):
-        chosen = lax.dynamic_index_in_dim(feats, (y + k) % 4, 0, keepdims=False)
         received.append(
-            lax.ppermute(chosen, "y", [(s, (s + k) % 4) for s in range(4)])
-        )
-
-    sort, split, pairs, codes = call(
+            lax.ppermute(chosen[k], "y", [(s, (s + k) % 4) for s in range(4)])
+        )
+
+    sort, split, pairs, codes, scalars = call(
         setup,
         (
             jax.ShapeDtypeStruct((384, 384), bf16),
             jax.ShapeDtypeStruct((384, 128), bf16),
             jax.ShapeDtypeStruct((16, 128), jnp.int32),
             jax.ShapeDtypeStruct((8, 128), f32),
+            jax.ShapeDtypeStruct((16, 128), f32),
         ),
         [],
         where,
         pair_index,
-        smem=(0, 1),
+        log_scale,
+        bias,
+        smem=(0, 1, 2, 3),
     )
 
     sent = call(
@@ -317,10 +353,7 @@
     for s in range(512):
         o, rest = divmod(s, 32)
         moves.append((s, 32 * ((o - DELTA[rest % 4]) % 16) + rest))
-    own, log_scale, bias = lax.optimization_barrier((own, log_scale, bias))
     other = lax.ppermute(own, BATCH + MP, moves)
-    row = lax.broadcasted_iota(jnp.int32, (16, 128), 0)
-    scalars = jnp.where(row < 8, jnp.exp(log_scale[0]), bias[0])
     sent = call(
         choose,
         jax.ShapeDtypeStruct((8, 296, 128), bf16),

time: 98.2 us -> 96.3 us (0.981)
  blocking collectives: 32.5 us -> 51.9 us
  waiting for transfers between devices: 22.3 us -> 7.07 us
  starting transfers between devices: 31.3 us -> 27.8 us
  local copies, waits for them, and re-layouts: 1.74 us -> 0.03 us
    all_to_all x2 -> x3, blocking collectives: 26.1 us -> 45.5 us  [exchange(): return lax.all_to_all(value, axes, split_axis=0, concat_axis=0, tiled=True)]
    all_to_all x2 -> x1, waiting for transfers between devices: 17.2 us -> 2.49 us  [exchange(): return lax.all_to_all(value, axes, split_axis=0, concat_axis=0, tiled=True)]
    all_to_all x2 -> x1, starting transfers between devices: 17.4 us -> 13.8 us  [exchange(): return lax.all_to_all(value, axes, split_axis=0, concat_axis=0, tiled=True)]
    unnamed x6 -> x10, local copies, waits for them, and re-layouts: 1.32 us -> 0.03 us
  transfers between devices with their start and end apart: 6 -> 5, of which waited for: 4 -> 2; matrix products, arithmetic and copies ran while one was open for 0% -> 0% of each run, Pallas kernels for 1% -> 1%
where the time goes in v9:
time: 96.3 us; the launch traced here: 95.7 us
  blocking collectives  51.9 us (54%)
  starting transfers between devices  27.8 us (29%)
  waiting for transfers between devices  7.07 us (7%)
  Pallas kernels  6.69 us (7%)
  between operations  2.15 us (2%)
    all_to_all x3, blocking collectives, exchange(): return lax.all_to_all(value, axes, split_axis=0, concat_axis=0, tiled=True)  45.5 us
    all_to_all x1, starting transfers between devices, exchange(): return lax.all_to_all(value, axes, split_axis=0, concat_axis=0, tiled=True)  13.8 us
    ppermute x3, starting transfers between devices, local(): lax.ppermute(chosen[k], 'y', [(s, (s + k) % 4) for s in range(4)])  10.4 us
    pallas_call x8, Pallas kernels, call(): pl.pallas_call(body, out_shape=out_shape, in_specs=specs, out_specs=outs,...  6.69 us
    all_gather x1, blocking collectives, local(): got = lax.all_gather(half, 'm1', axis=0, tiled=True)  6.37 us
    ppermute x1, waiting for transfers between devices, local(): other = lax.ppermute(own, BATCH + MP, moves)  4.58 us
    ppermute x1, starting transfers between devices, local(): other = lax.ppermute(own, BATCH + MP, moves)  3.54 us
    all_to_all x1, waiting for transfers between devices, exchange(): return lax.all_to_all(value, axes, split_axis=0, concat_axis=0, tiled=True)  2.49 us
  transfers between devices with their start and end apart: 5, of which 2 were waited for; matrix products, arithmetic and copies ran while one was open for 0% of the time, Pallas kernels for 1%

profile of v9, /device:TPU:1, one launch (start us, length us, event | category | flops | bytes accessed | tf_op | source)
XLA Modules:
  0.0 95.7 jit_solution(6715209671982825865)
XLA Ops:
  0.6 1.7 %shard_map.87 = (bf16[32,56,128]{2,1,0:T(8,128)(2,1)}, bf16[32,384]{1,0:T(8,128)(2,1)}, bf16[32,384]{1,0:T(8,128)(2,1)}, bf16[32,384]{1,0:T(8,128)(2,1)}, bf16[32,384]{1,0:T(8,128)(2,1)}) custom-call(bf16[12,288]{1,0:T(8,128)(2,1)} %w_img_ref.1, bf16[12,288]{1,0:T(8,128)(2,1)} %w_txt_ref.1, bf16[16,1536]{1,0:T(8,128)(2,1)} %img_ref.1, bf16[16,1536]{1,0:T(8,128)(2,1)} %txt_ref.1), custom_call_target="tpu_custom_call" | custom-call | tf_op jit(solution)/shard_map/pallas_call | solution.py:27
  2.3 0.0 copy-start.4
  2.4 0.0 copy-start.3
  2.4 0.0 copy-start.2
  2.4 13.8 %all-to-all-start = ((bf16[32,56,128]{2,1,0:T(8,128)(2,1)}), bf16[32,56,128]{2,1,0:T(8,128)(2,1)S(1)}, u32[]{:S(2)}, u32[]{:S(2)}) async-start(bf16[32,56,128]{2,1,0:T(8,128)(2,1)} %get-tuple-element.16), calls=%async_computation | async-start | bytes 917504 | tf_op jit(solution)/shard_map/all_to_all | solution.py:286
  16.2 0.0 copy-done.4
  16.2 3.2 %collective-permute-start = (bf16[32,384]{1,0:T(8,128)(2,1)S(1)}, bf16[32,384]{1,0:T(8,128)(2,1)S(1)}, u32[]{:S(2)}, u32[]{:S(2)}) collective-permute-start(bf16[32,384]{1,0:T(8,128)(2,1)S(1)} %copy-done.4), channel_id=1, source_target_pairs={{0,32},{32,64},{64,96},{96,0},{1,33},{33,65},{65,97},{97,1},{2,34}... | collective-permute-start | bytes 73736 | tf_op jit(solution)/shard_map/ppermute | solution.py:316
  19.4 0.0 copy-done.3
  19.5 4.2 %collective-permute-start.1 = (bf16[32,384]{1,0:T(8,128)(2,1)S(1)}, bf16[32,384]{1,0:T(8,128)(2,1)S(1)}, u32[]{:S(2)}, u32[]{:S(2)}) collective-permute-start(bf16[32,384]{1,0:T(8,128)(2,1)S(1)} %copy-done.3), channel_id=1, source_target_pairs={{0,64},{32,96},{64,0},{96,32},{1,65},{33,97},{65,1},{97,33},{2,66}... | collective-permute-start | bytes 73736 | tf_op jit(solution)/shard_map/ppermute | solution.py:316
  23.7 0.0 copy-done.2
  23.7 3.0 %collective-permute-start.2 = (bf16[32,384]{1,0:T(8,128)(2,1)S(1)}, bf16[32,384]{1,0:T(8,128)(2,1)S(1)}, u32[]{:S(2)}, u32[]{:S(2)}) collective-permute-start(bf16[32,384]{1,0:T(8,128)(2,1)S(1)} %copy-done.2), channel_id=1, source_target_pairs={{0,96},{32,0},{64,32},{96,64},{1,97},{33,1},{65,33},{97,65},{2,98}... | collective-permute-start | bytes 73736 | tf_op jit(solution)/shard_map/ppermute | solution.py:316
  26.7 0.0 copy-start
  26.7 0.1 pad_add_fusion.where_ref
  27.4 0.0 copy-start.1
  28.1 0.0 copy-done.1
  28.1 0.7 shard_map.86
  28.8 0.0 collective-permute-done.r1_ref
  28.8 0.0 collective-permute-done.1.r2_ref
  28.9 0.0 collective-permute-done.2.r3_ref
  28.9 2.5 %all-to-all-done.w_ref = bf16[32,56,128]{2,1,0:T(8,128)(2,1)S(1)} async-done(((bf16[32,56,128]{2,1,0:T(8,128)(2,1)}), bf16[32,56,128]{2,1,0:T(8,128)(2,1)S(1)}, u32[]{:S(2)}, u32[]{:S(2)}) %all-to-all-start) | async-done | bytes 458784 | tf_op jit(solution)/shard_map/all_to_all | solution.py:286
  31.4 0.0 copy-done
  31.4 1.3 %shard_map.88 = bf16[8,72,128]{2,1,0:T(8,128)(2,1)S(1)} custom-call(s32[4]{0:T(128)S(1)} %pad_add_fusion.where_ref, bf16[384,384]{1,0:T(8,128)(2,1)S(1)} %get-tuple-element.14.sort_ref, bf16[384,128]{1,0:T(8,128)(2,1)S(1)} %get-tuple-element.15.split_ref, bf16[32,56,128]{2,1,0:T(8,128)(2,1)S(1)} %all-to-all-done.w_ref, bf16[32,384]{1,0:T(8,128)(2,1)S(1)} %copy-done, ...), custom_call_target="tpu_custom_call" | custom-call | tf_op jit(solution)/shard_map/pallas_call | solution.py:27
  32.7 13.4 %all_to_all.20.got_ref = bf16[8,72,128]{2,1,0:T(8,128)(2,1)S(1)} all-to-all(bf16[8,72,128]{2,1,0:T(8,128)(2,1)S(1)} %shard_map.88), channel_id=1, replica_groups=mesh['x1'=2,'x0'=2,'y'=4,'z2'=2,'z1'=2,'z0'=2,'m0'=2,'m1'=2] {'y','m0'}, dimensions={0} | all-to-all | bytes 294912 | tf_op jit(solution)/shard_map/all_to_all | solution.py:286
  46.1 6.4 %all_gather.3.got_ref = f32[4,72,128]{2,1,0:T(8,128)S(1)} all-gather(f32[2,72,128]{2,1,0:T(8,128)S(1)} %shard_map.89), channel_id=1, replica_groups=mesh['x1'=2,'x0'=2,'y'=4,'z2'=2,'z1'=2,'z0'=2,'m0'=2,'m1'=2] {'m1'}, dimensions={0}, use_global_device_ids=true | all-gather | bytes 221184 | tf_op jit(solution)/shard_map/all_gather | solution.py:349
  52.5 0.2 shard_map.90.own_ref
  52.7 3.5 %collective-permute-start.3 = (bf16[296,128]{1,0:T(8,128)(2,1)S(1)}, bf16[296,128]{1,0:T(8,128)(2,1)S(1)}, u32[]{:S(2)}, u32[]{:S(2)}) collective-permute-start(bf16[296,128]{1,0:T(8,128)(2,1)S(1)} %shard_map.90.own_ref), channel_id=1, source_target_pairs={{0,32},{1,65},{2,482},{3,451},{4,36},{5,69},{6,486},{7,455},{8,40}... | collective-permute-start | bytes 227336 | tf_op jit(solution)/shard_map/ppermute | solution.py:356
  56.3 4.6 %collective-permute-done.3.other_ref = bf16[296,128]{1,0:T(8,128)(2,1)S(1)} collective-permute-done((bf16[296,128]{1,0:T(8,128)(2,1)S(1)}, bf16[296,128]{1,0:T(8,128)(2,1)S(1)}, u32[]{:S(2)}, u32[]{:S(2)}) %collective-permute-start.3) | collective-permute-done | bytes 75808 | tf_op jit(solution)/shard_map/ppermute | solution.py:356
  60.8 0.6 shard_map.91
  61.4 18.5 %all_to_all.21.got_ref = bf16[8,296,128]{2,1,0:T(8,128)(2,1)S(1)} all-to-all(bf16[8,296,128]{2,1,0:T(8,128)(2,1)S(1)} %shard_map.91), channel_id=1, replica_groups=mesh['x1'=2,'x0'=2,'y'=4,'z2'=2,'z1'=2,'z0'=2,'m0'=2,'m1'=2] {'z2','z1',..., dimensions={0} | all-to-all | bytes 1212416 | tf_op jit(solution)/shard_map/all_to_all | solution.py:286
  80.0 1.4 %shard_map.92 = bf16[4,72,128]{2,1,0:T(8,128)(2,1)S(1)} custom-call(s32[4]{0:T(128)S(1)} %pad_add_fusion.where_ref, f32[16,128]{1,0:T(8,128)S(1)} %get-tuple-element.12.scalars_ref, s32[16,128]{1,0:T(8,128)S(1)} %get-tuple-element.13.pair_ref, bf16[296,128]{1,0:T(8,128)(2,1)S(1)} %shard_map.90.own_ref, bf16[8,296,128]{2,1,0:T(8,128)(2,1)S(1)} %all_to_all.21.got_ref), custom_call_target="tpu_custom_call" | custom-call | tf_op jit(solution)/shard_map/pallas_call | solution.py:27
  81.4 13.6 %all_to_all.22.got_ref = bf16[4,72,128]{2,1,0:T(8,128)(2,1)S(1)} all-to-all(bf16[4,72,128]{2,1,0:T(8,128)(2,1)S(1)} %shard_map.92), channel_id=1, replica_groups=mesh['x1'=2,'x0'=2,'y'=4,'z2'=2,'z1'=2,'z0'=2,'m0'=2,'m1'=2] {'m0','m1'}, dimensions={0} | all-to-all | bytes 147456 | tf_op jit(solution)/shard_map/all_to_all | solution.py:286
  95.0 0.7 shard_map.93
  (1 shorter events, 0.0 us)
Async XLA Ops:
  2.3 13.9 %copy-start.4 = (bf16[32,384]{1,0:T(8,128)(2,1)S(1)}, bf16[32,384]{1,0:T(8,128)(2,1)}, u32[]{:S(2)}) copy-start(bf16[32,384]{1,0:T(8,128)(2,1)} %get-tuple-element.18) | copy-start | bytes 73732
  2.4 17.1 %copy-start.3 = (bf16[32,384]{1,0:T(8,128)(2,1)S(1)}, bf16[32,384]{1,0:T(8,128)(2,1)}, u32[]{:S(2)}) copy-start(bf16[32,384]{1,0:T(8,128)(2,1)} %get-tuple-element.19) | copy-start | bytes 73732
  2.4 21.3 %copy-start.2 = (bf16[32,384]{1,0:T(8,128)(2,1)S(1)}, bf16[32,384]{1,0:T(8,128)(2,1)}, u32[]{:S(2)}) copy-start(bf16[32,384]{1,0:T(8,128)(2,1)} %get-tuple-element.20) | copy-start | bytes 73732
  2.4 29.0 %all-to-all-start = ((bf16[32,56,128]{2,1,0:T(8,128)(2,1)}), bf16[32,56,128]{2,1,0:T(8,128)(2,1)S(1)}, u32[]{:S(2)}, u32[]{:S(2)}) async-start(bf16[32,56,128]{2,1,0:T(8,128)(2,1)} %get-tuple-element.16), calls=%async_computation | async-start | bytes 917504 | tf_op jit(solution)/shard_map/all_to_all | solution.py:286
  16.2 12.6 %collective-permute-start = (bf16[32,384]{1,0:T(8,128)(2,1)S(1)}, bf16[32,384]{1,0:T(8,128)(2,1)S(1)}, u32[]{:S(2)}, u32[]{:S(2)}) collective-permute-start(bf16[32,384]{1,0:T(8,128)(2,1)S(1)} %copy-done.4), channel_id=1, source_target_pairs={{0,32},{32,64},{64,96},{96,0},{1,33},{33,65},{65,97},{97,1},{2,34}... | collective-permute-start | bytes 73736 | tf_op jit(solution)/shard_map/ppermute | solution.py:316
  19.5 9.4 %collective-permute-start.1 = (bf16[32,384]{1,0:T(8,128)(2,1)S(1)}, bf16[32,384]{1,0:T(8,128)(2,1)S(1)}, u32[]{:S(2)}, u32[]{:S(2)}) collective-permute-start(bf16[32,384]{1,0:T(8,128)(2,1)S(1)} %copy-done.3), channel_id=1, source_target_pairs={{0,64},{32,96},{64,0},{96,32},{1,65},{33,97},{65,1},{97,33},{2,66}... | collective-permute-start | bytes 73736 | tf_op jit(solution)/shard_map/ppermute | solution.py:316
  23.7 5.2 %collective-permute-start.2 = (bf16[32,384]{1,0:T(8,128)(2,1)S(1)}, bf16[32,384]{1,0:T(8,128)(2,1)S(1)}, u32[]{:S(2)}, u32[]{:S(2)}) collective-permute-start(bf16[32,384]{1,0:T(8,128)(2,1)S(1)} %copy-done.2), channel_id=1, source_target_pairs={{0,96},{32,0},{64,32},{96,64},{1,97},{33,1},{65,33},{97,65},{2,98}... | collective-permute-start | bytes 73736 | tf_op jit(solution)/shard_map/ppermute | solution.py:316
  26.7 4.7 %copy-start = (bf16[32,384]{1,0:T(8,128)(2,1)S(1)}, bf16[32,384]{1,0:T(8,128)(2,1)}, u32[]{:S(2)}) copy-start(bf16[32,384]{1,0:T(8,128)(2,1)} %get-tuple-element.17.r0_ref) | copy-start | bytes 73732
  27.4 0.7 copy-start.1
  52.7 8.1 %collective-permute-start.3 = (bf16[296,128]{1,0:T(8,128)(2,1)S(1)}, bf16[296,128]{1,0:T(8,128)(2,1)S(1)}, u32[]{:S(2)}, u32[]{:S(2)}) collective-permute-start(bf16[296,128]{1,0:T(8,128)(2,1)S(1)} %shard_map.90.own_ref), channel_id=1, source_target_pairs={{0,32},{1,65},{2,482},{3,451},{4,36},{5,69},{6,486},{7,455},{8,40}... | collective-permute-start | bytes 227336 | tf_op jit(solution)/shard_map/ppermute | solution.py:356

commit v10 on v9

--- a/solution.py
+++ b/solution.py
@@ -10,12 +10,20 @@
 X = ("x1", "x0")
 Z = ("z2", "z1", "z0")
 BATCH = X + ("y",) + Z
-SPREAD = ("z0", "x0", "z1", "x1", "z2")
+SPREAD = ("z2", "z1", "z0", "x1", "x0")
+Z_ORDER = ("z1", "z0", "z2")
 MP = ("m0", "m1")
 bf16 = jnp.bfloat16
 f32 = jnp.float32
 epsilon = 1e-06
 DELTA = (-1, -2, 1, 2)
+
+
+def place_in(order, **values):
+    place = 0
+    for axis in order:
+        place = 2 * place + ((values[axis[0]] >> int(axis[1])) & 1)
+    return place
 
 
 def call(body, out_shape, scratch, *args, smem=(), hbm=(), out=pltpu.VMEM, vmem=16):
@@ -111,10 +119,9 @@
     high = split_ref[192:384, :]
     weights = [[], []]
     for half in range(2):
-        places = []
-        for q in range(16 * half, 16 * half + 16):
-            x1, x0, z2, z1, z0 = (q >> 4) & 1, (q >> 3) & 1, (q >> 2) & 1, (q >> 1) & 1, q & 1
-            places.append(16 * z0 + 8 * x0 + 4 * z1 + 2 * x1 + z2)
+        places = [
+            place_in(SPREAD, x=q >> 3, z=q & 7) for q in range(16 * half, 16 * half + 16)
+        ]
         some = jnp.stack([w_ref[place] for place in places], axis=0)
         main = jnp.concatenate(
             [some[:, 0:24].reshape(384, 128), some[:, 24:48].reshape(384, 128)], axis=1
@@ -154,9 +161,8 @@
 
 def combine(got_ref, out_ref):
     for m in range(2):
-        pre = got_ref[m].astype(f32)
-        for part in range(1, 4):
-            pre = pre + got_ref[2 * part + m].astype(f32)
+        pieces = [got_ref[2 * y + m].astype(f32) for y in range(4)]
+        pre = pieces[0] + pieces[1] + pieces[2] + pieces[3]
         out_ref[m] = pre
 
 
@@ -191,12 +197,13 @@
         other_txt = near | ((m == 1) & (z > to)) | ((m == 3) & (z <= to))
         img = jnp.where(other_img, 1, 0)
         txt = jnp.where(other_txt, 1, 0)
+        at = place_in(Z_ORDER, z=to)
         for t in range(9):
-            out_ref[to, 32 * t : 32 * t + 16, :] = two_ref[img, 32 * t : 32 * t + 16, :]
-            out_ref[to, 32 * t + 16 : 32 * t + 32, :] = two_ref[
+            out_ref[at, 32 * t : 32 * t + 16, :] = two_ref[img, 32 * t : 32 * t + 16, :]
+            out_ref[at, 32 * t + 16 : 32 * t + 32, :] = two_ref[
                 txt, 32 * t + 16 : 32 * t + 32, :
             ]
-        out_ref[to, 288:296, :] = two_ref[img, 288:296, :]
+        out_ref[at, 288:296, :] = two_ref[img, 288:296, :]
 
 
 def score(where_ref, scalars_ref, pair_ref, own_ref, got_ref, out_ref):
@@ -207,11 +214,13 @@
     scale_one = scale[:, 0:1]
     offset = scalars_ref[8:9, :]
 
+    order = [place_in(Z_ORDER, z=k) for k in range(8)]
+
     def window(at):
         return jnp.concatenate(
             [
                 jnp.concatenate(
-                    [got_ref[k, 32 * t + at : 32 * t + at + 16, :] for k in range(8)], axis=0
+                    [got_ref[k, 32 * t + at : 32 * t + at + 16, :] for k in order], axis=0
                 )
                 for t in range(9)
             ],
@@ -363,7 +372,7 @@
         other,
         smem=(0,),
     )
-    got = exchange(sent, Z)
+    got = exchange(sent, Z_ORDER)
     sent = call(
         score,
         jax.ShapeDtypeStruct((4, 72, 128), bf16),

time: 96.3 us -> 94 us (0.976)
  blocking collectives: 51.9 us -> 50.3 us
    all_to_all x3, blocking collectives: 45.5 us -> 44.3 us  [exchange(): return lax.all_to_all(value, axes, split_axis=0, concat_axis=0, tiled=True)]
where the time goes in v10:
time: 94 us; the launch traced here: 93.4 us
  blocking collectives  50.3 us (54%)
  starting transfers between devices  27.8 us (30%)
  Pallas kernels  6.71 us (7%)
  waiting for transfers between devices  6.4 us (7%)
  between operations  2.15 us (2%)
    all_to_all x3, blocking collectives, exchange(): return lax.all_to_all(value, axes, split_axis=0, concat_axis=0, tiled=True)  44.3 us
    all_to_all x1, starting transfers between devices, exchange(): return lax.all_to_all(value, axes, split_axis=0, concat_axis=0, tiled=True)  13.8 us
    ppermute x3, starting transfers between devices, local(): lax.ppermute(chosen[k], 'y', [(s, (s + k) % 4) for s in range(4)])  10.4 us
    pallas_call x8, Pallas kernels, call(): pl.pallas_call(body, out_shape=out_shape, in_specs=specs, out_specs=outs,...  6.71 us
    all_gather x1, blocking collectives, local(): got = lax.all_gather(half, 'm1', axis=0, tiled=True)  5.98 us
    ppermute x1, waiting for transfers between devices, local(): other = lax.ppermute(own, BATCH + MP, moves)  4.58 us
    ppermute x1, starting transfers between devices, local(): other = lax.ppermute(own, BATCH + MP, moves)  3.54 us
  transfers between devices with their start and end apart: 5, of which 2 were waited for; matrix products, arithmetic and copies ran while one was open for 0% of the time, Pallas kernels for 1%

profile of v10, /device:TPU:1, one launch (start us, length us, event | category | flops | bytes accessed | tf_op | source)
XLA Modules:
  0.0 93.4 jit_solution(13975180217298959264)
XLA Ops:
  0.6 1.7 %shard_map.87 = (bf16[32,56,128]{2,1,0:T(8,128)(2,1)}, bf16[32,384]{1,0:T(8,128)(2,1)}, bf16[32,384]{1,0:T(8,128)(2,1)}, bf16[32,384]{1,0:T(8,128)(2,1)}, bf16[32,384]{1,0:T(8,128)(2,1)}) custom-call(bf16[12,288]{1,0:T(8,128)(2,1)} %w_img_ref.1, bf16[12,288]{1,0:T(8,128)(2,1)} %w_txt_ref.1, bf16[16,1536]{1,0:T(8,128)(2,1)} %img_ref.1, bf16[16,1536]{1,0:T(8,128)(2,1)} %txt_ref.1), custom_call_target="tpu_custom_call" | custom-call | tf_op jit(solution)/shard_map/pallas_call | solution.py:35
  2.3 0.0 copy-start.4
  2.4 0.0 copy-start.3
  2.4 0.0 copy-start.2
  2.4 13.8 %all-to-all-start = ((bf16[32,56,128]{2,1,0:T(8,128)(2,1)}), bf16[32,56,128]{2,1,0:T(8,128)(2,1)S(1)}, u32[]{:S(2)}, u32[]{:S(2)}) async-start(bf16[32,56,128]{2,1,0:T(8,128)(2,1)} %get-tuple-element.16), calls=%async_computation | async-start | bytes 917504 | tf_op jit(solution)/shard_map/all_to_all | solution.py:295
  16.2 0.0 copy-done.4
  16.2 3.2 %collective-permute-start = (bf16[32,384]{1,0:T(8,128)(2,1)S(1)}, bf16[32,384]{1,0:T(8,128)(2,1)S(1)}, u32[]{:S(2)}, u32[]{:S(2)}) collective-permute-start(bf16[32,384]{1,0:T(8,128)(2,1)S(1)} %copy-done.4), channel_id=1, source_target_pairs={{0,32},{32,64},{64,96},{96,0},{1,33},{33,65},{65,97},{97,1},{2,34}... | collective-permute-start | bytes 73736 | tf_op jit(solution)/shard_map/ppermute | solution.py:325
  19.4 0.0 copy-done.3
  19.5 4.2 %collective-permute-start.1 = (bf16[32,384]{1,0:T(8,128)(2,1)S(1)}, bf16[32,384]{1,0:T(8,128)(2,1)S(1)}, u32[]{:S(2)}, u32[]{:S(2)}) collective-permute-start(bf16[32,384]{1,0:T(8,128)(2,1)S(1)} %copy-done.3), channel_id=1, source_target_pairs={{0,64},{32,96},{64,0},{96,32},{1,65},{33,97},{65,1},{97,33},{2,66}... | collective-permute-start | bytes 73736 | tf_op jit(solution)/shard_map/ppermute | solution.py:325
  23.7 0.0 copy-done.2
  23.7 3.0 %collective-permute-start.2 = (bf16[32,384]{1,0:T(8,128)(2,1)S(1)}, bf16[32,384]{1,0:T(8,128)(2,1)S(1)}, u32[]{:S(2)}, u32[]{:S(2)}) collective-permute-start(bf16[32,384]{1,0:T(8,128)(2,1)S(1)} %copy-done.2), channel_id=1, source_target_pairs={{0,96},{32,0},{64,32},{96,64},{1,97},{33,1},{65,33},{97,65},{2,98}... | collective-permute-start | bytes 73736 | tf_op jit(solution)/shard_map/ppermute | solution.py:325
  26.7 0.0 copy-start
  26.7 0.1 pad_add_fusion.where_ref
  27.4 0.0 copy-start.1
  28.1 0.0 copy-done.1
  28.1 0.7 shard_map.86
  28.8 0.0 collective-permute-done.r1_ref
  28.8 0.0 collective-permute-done.1.r2_ref
  28.9 0.0 collective-permute-done.2.r3_ref
  28.9 1.8 %all-to-all-done.w_ref = bf16[32,56,128]{2,1,0:T(8,128)(2,1)S(1)} async-done(((bf16[32,56,128]{2,1,0:T(8,128)(2,1)}), bf16[32,56,128]{2,1,0:T(8,128)(2,1)S(1)}, u32[]{:S(2)}, u32[]{:S(2)}) %all-to-all-start) | async-done | bytes 458784 | tf_op jit(solution)/shard_map/all_to_all | solution.py:295
  30.7 0.0 copy-done
  30.7 1.3 %shard_map.88 = bf16[8,72,128]{2,1,0:T(8,128)(2,1)S(1)} custom-call(s32[4]{0:T(128)S(1)} %pad_add_fusion.where_ref, bf16[384,384]{1,0:T(8,128)(2,1)S(1)} %get-tuple-element.14.sort_ref, bf16[384,128]{1,0:T(8,128)(2,1)S(1)} %get-tuple-element.15.split_ref, bf16[32,56,128]{2,1,0:T(8,128)(2,1)S(1)} %all-to-all-done.w_ref, bf16[32,384]{1,0:T(8,128)(2,1)S(1)} %copy-done, ...), custom_call_target="tpu_custom_call" | custom-call | tf_op jit(solution)/shard_map/pallas_call | solution.py:35
  32.0 13.4 %all_to_all.20.got_ref = bf16[8,72,128]{2,1,0:T(8,128)(2,1)S(1)} all-to-all(bf16[8,72,128]{2,1,0:T(8,128)(2,1)S(1)} %shard_map.88), channel_id=1, replica_groups=mesh['x1'=2,'x0'=2,'y'=4,'z2'=2,'z1'=2,'z0'=2,'m0'=2,'m1'=2] {'y','m0'}, dimensions={0} | all-to-all | bytes 294912 | tf_op jit(solution)/shard_map/all_to_all | solution.py:295
  45.4 6.0 %all_gather.3.got_ref = f32[4,72,128]{2,1,0:T(8,128)S(1)} all-gather(f32[2,72,128]{2,1,0:T(8,128)S(1)} %shard_map.89), channel_id=1, replica_groups=mesh['x1'=2,'x0'=2,'y'=4,'z2'=2,'z1'=2,'z0'=2,'m0'=2,'m1'=2] {'m1'}, dimensions={0}, use_global_device_ids=true | all-gather | bytes 221184 | tf_op jit(solution)/shard_map/all_gather | solution.py:358
  51.4 0.2 shard_map.90.own_ref
  51.7 3.5 %collective-permute-start.3 = (bf16[296,128]{1,0:T(8,128)(2,1)S(1)}, bf16[296,128]{1,0:T(8,128)(2,1)S(1)}, u32[]{:S(2)}, u32[]{:S(2)}) collective-permute-start(bf16[296,128]{1,0:T(8,128)(2,1)S(1)} %shard_map.90.own_ref), channel_id=1, source_target_pairs={{0,32},{1,65},{2,482},{3,451},{4,36},{5,69},{6,486},{7,455},{8,40}... | collective-permute-start | bytes 227336 | tf_op jit(solution)/shard_map/ppermute | solution.py:365
  55.2 4.6 %collective-permute-done.3.other_ref = bf16[296,128]{1,0:T(8,128)(2,1)S(1)} collective-permute-done((bf16[296,128]{1,0:T(8,128)(2,1)S(1)}, bf16[296,128]{1,0:T(8,128)(2,1)S(1)}, u32[]{:S(2)}, u32[]{:S(2)}) %collective-permute-start.3) | collective-permute-done | bytes 75808 | tf_op jit(solution)/shard_map/ppermute | solution.py:365
  59.8 0.6 shard_map.91
  60.4 16.1 %all_to_all.21.got_ref = bf16[8,296,128]{2,1,0:T(8,128)(2,1)S(1)} all-to-all(bf16[8,296,128]{2,1,0:T(8,128)(2,1)S(1)} %shard_map.91), channel_id=1, replica_groups=mesh['x1'=2,'x0'=2,'y'=4,'z2'=2,'z1'=2,'z0'=2,'m0'=2,'m1'=2] {'z1','z0',..., dimensions={0} | all-to-all | bytes 1212416 | tf_op jit(solution)/shard_map/all_to_all | solution.py:295
  76.5 1.4 %shard_map.92 = bf16[4,72,128]{2,1,0:T(8,128)(2,1)S(1)} custom-call(s32[4]{0:T(128)S(1)} %pad_add_fusion.where_ref, f32[16,128]{1,0:T(8,128)S(1)} %get-tuple-element.12.scalars_ref, s32[16,128]{1,0:T(8,128)S(1)} %get-tuple-element.13.pair_ref, bf16[296,128]{1,0:T(8,128)(2,1)S(1)} %shard_map.90.own_ref, bf16[8,296,128]{2,1,0:T(8,128)(2,1)S(1)} %all_to_all.21.got_ref), custom_call_target="tpu_custom_call" | custom-call | tf_op jit(solution)/shard_map/pallas_call | solution.py:35
  77.9 14.9 %all_to_all.22.got_ref = bf16[4,72,128]{2,1,0:T(8,128)(2,1)S(1)} all-to-all(bf16[4,72,128]{2,1,0:T(8,128)(2,1)S(1)} %shard_map.92), channel_id=1, replica_groups=mesh['x1'=2,'x0'=2,'y'=4,'z2'=2,'z1'=2,'z0'=2,'m0'=2,'m1'=2] {'m0','m1'}, dimensions={0} | all-to-all | bytes 147456 | tf_op jit(solution)/shard_map/all_to_all | solution.py:295
  92.7 0.7 shard_map.93
  (1 shorter events, 0.0 us)
Async XLA Ops:
  2.3 13.9 %copy-start.4 = (bf16[32,384]{1,0:T(8,128)(2,1)S(1)}, bf16[32,384]{1,0:T(8,128)(2,1)}, u32[]{:S(2)}) copy-start(bf16[32,384]{1,0:T(8,128)(2,1)} %get-tuple-element.18) | copy-start | bytes 73732
  2.4 17.1 %copy-start.3 = (bf16[32,384]{1,0:T(8,128)(2,1)S(1)}, bf16[32,384]{1,0:T(8,128)(2,1)}, u32[]{:S(2)}) copy-start(bf16[32,384]{1,0:T(8,128)(2,1)} %get-tuple-element.19) | copy-start | bytes 73732
  2.4 21.3 %copy-start.2 = (bf16[32,384]{1,0:T(8,128)(2,1)S(1)}, bf16[32,384]{1,0:T(8,128)(2,1)}, u32[]{:S(2)}) copy-start(bf16[32,384]{1,0:T(8,128)(2,1)} %get-tuple-element.20) | copy-start | bytes 73732
  2.4 28.3 %all-to-all-start = ((bf16[32,56,128]{2,1,0:T(8,128)(2,1)}), bf16[32,56,128]{2,1,0:T(8,128)(2,1)S(1)}, u32[]{:S(2)}, u32[]{:S(2)}) async-start(bf16[32,56,128]{2,1,0:T(8,128)(2,1)} %get-tuple-element.16), calls=%async_computation | async-start | bytes 917504 | tf_op jit(solution)/shard_map/all_to_all | solution.py:295
  16.2 12.6 %collective-permute-start = (bf16[32,384]{1,0:T(8,128)(2,1)S(1)}, bf16[32,384]{1,0:T(8,128)(2,1)S(1)}, u32[]{:S(2)}, u32[]{:S(2)}) collective-permute-start(bf16[32,384]{1,0:T(8,128)(2,1)S(1)} %copy-done.4), channel_id=1, source_target_pairs={{0,32},{32,64},{64,96},{96,0},{1,33},{33,65},{65,97},{97,1},{2,34}... | collective-permute-start | bytes 73736 | tf_op jit(solution)/shard_map/ppermute | solution.py:325
  19.5 9.4 %collective-permute-start.1 = (bf16[32,384]{1,0:T(8,128)(2,1)S(1)}, bf16[32,384]{1,0:T(8,128)(2,1)S(1)}, u32[]{:S(2)}, u32[]{:S(2)}) collective-permute-start(bf16[32,384]{1,0:T(8,128)(2,1)S(1)} %copy-done.3), channel_id=1, source_target_pairs={{0,64},{32,96},{64,0},{96,32},{1,65},{33,97},{65,1},{97,33},{2,66}... | collective-permute-start | bytes 73736 | tf_op jit(solution)/shard_map/ppermute | solution.py:325
  23.7 5.2 %collective-permute-start.2 = (bf16[32,384]{1,0:T(8,128)(2,1)S(1)}, bf16[32,384]{1,0:T(8,128)(2,1)S(1)}, u32[]{:S(2)}, u32[]{:S(2)}) collective-permute-start(bf16[32,384]{1,0:T(8,128)(2,1)S(1)} %copy-done.2), channel_id=1, source_target_pairs={{0,96},{32,0},{64,32},{96,64},{1,97},{33,1},{65,33},{97,65},{2,98}... | collective-permute-start | bytes 73736 | tf_op jit(solution)/shard_map/ppermute | solution.py:325
  26.7 4.0 %copy-start = (bf16[32,384]{1,0:T(8,128)(2,1)S(1)}, bf16[32,384]{1,0:T(8,128)(2,1)}, u32[]{:S(2)}) copy-start(bf16[32,384]{1,0:T(8,128)(2,1)} %get-tuple-element.17.r0_ref) | copy-start | bytes 73732
  27.4 0.7 copy-start.1
  51.7 8.1 %collective-permute-start.3 = (bf16[296,128]{1,0:T(8,128)(2,1)S(1)}, bf16[296,128]{1,0:T(8,128)(2,1)S(1)}, u32[]{:S(2)}, u32[]{:S(2)}) collective-permute-start(bf16[296,128]{1,0:T(8,128)(2,1)S(1)} %shard_map.90.own_ref), channel_id=1, source_target_pairs={{0,32},{1,65},{2,482},{3,451},{4,36},{5,69},{6,486},{7,455},{8,40}... | collective-permute-start | bytes 227336 | tf_op jit(solution)/shard_map/ppermute | solution.py:365

commit v11 on v10

--- a/solution.py
+++ b/solution.py
@@ -250,15 +250,19 @@
     own_text = (octet * 8 + z) * 16 + row
     match_txt = pair_window == own_text.astype(f32)
 
-    def grads(own, window, match):
-        scores = lax.dot_general(own, window, (((1,), (1,)), ((), ())), preferred_element_type=f32)
-        logits = scale * scores + offset
+    sides = ((mine(0), txts, match_img), (mine(16), imgs, match_txt))
+    scores = [
+        lax.dot_general(own, window, (((1,), (1,)), ((), ())), preferred_element_type=f32)
+        for own, window, _ in sides
+    ]
+    coefs = []
+    for score, (_, _, match) in zip(scores, sides):
         label = jnp.where(match, 1.0, -1.0)
-        coef = (-label / (1.0 + jnp.exp(label * logits))).astype(bf16)
-        return scale_one * jnp.dot(coef, window, preferred_element_type=f32)
-
-    image_part = grads(mine(0), txts, match_img)
-    text_part = grads(mine(16), imgs, match_txt)
+        coefs.append((-label / (1.0 + jnp.exp(label * (scale * score + offset)))).astype(bf16))
+    image_part, text_part = (
+        scale_one * jnp.dot(coef, window, preferred_element_type=f32)
+        for coef, (_, window, _) in zip(coefs, sides)
+    )
     for to in range(4):
         rows = text_part[4 * to : 4 * to + 4]
         at = 1024 + 32 * to

time: 94 us -> 93.7 us (level)
  no operation moved by 1% of the time
where the time goes in v11:
time: 93.7 us; the launch traced here: 93.1 us
  blocking collectives  50.3 us (54%)
  starting transfers between devices  27.8 us (30%)
  waiting for transfers between devices  6.4 us (7%)
  Pallas kernels  6.37 us (7%)
  between operations  2.14 us (2%)
    all_to_all x3, blocking collectives, exchange(): return lax.all_to_all(value, axes, split_axis=0, concat_axis=0, tiled=True)  44.3 us
    all_to_all x1, starting transfers between devices, exchange(): return lax.all_to_all(value, axes, split_axis=0, concat_axis=0, tiled=True)  13.8 us
    ppermute x3, starting transfers between devices, local(): lax.ppermute(chosen[k], 'y', [(s, (s + k) % 4) for s in range(4)])  10.4 us
    pallas_call x8, Pallas kernels, call(): pl.pallas_call(body, out_shape=out_shape, in_specs=specs, out_specs=outs,...  6.37 us
    all_gather x1, blocking collectives, local(): got = lax.all_gather(half, 'm1', axis=0, tiled=True)  5.98 us
    ppermute x1, waiting for transfers between devices, local(): other = lax.ppermute(own, BATCH + MP, moves)  4.58 us
    ppermute x1, starting transfers between devices, local(): other = lax.ppermute(own, BATCH + MP, moves)  3.54 us
  transfers between devices with their start and end apart: 5, of which 2 were waited for; matrix products, arithmetic and copies ran while one was open for 0% of the time, Pallas kernels for 1%

profile of v11, /device:TPU:1, one launch (start us, length us, event | category | flops | bytes accessed | tf_op | source)
XLA Modules:
  0.0 93.1 jit_solution(11827315395156813186)
XLA Ops:
  0.6 1.7 %shard_map.87 = (bf16[32,56,128]{2,1,0:T(8,128)(2,1)}, bf16[32,384]{1,0:T(8,128)(2,1)}, bf16[32,384]{1,0:T(8,128)(2,1)}, bf16[32,384]{1,0:T(8,128)(2,1)}, bf16[32,384]{1,0:T(8,128)(2,1)}) custom-call(bf16[12,288]{1,0:T(8,128)(2,1)} %w_img_ref.1, bf16[12,288]{1,0:T(8,128)(2,1)} %w_txt_ref.1, bf16[16,1536]{1,0:T(8,128)(2,1)} %img_ref.1, bf16[16,1536]{1,0:T(8,128)(2,1)} %txt_ref.1), custom_call_target="tpu_custom_call" | custom-call | tf_op jit(solution)/shard_map/pallas_call | solution.py:35
  2.3 0.0 copy-start.4
  2.4 0.0 copy-start.3
  2.4 0.0 copy-start.2
  2.4 13.8 %all-to-all-start = ((bf16[32,56,128]{2,1,0:T(8,128)(2,1)}), bf16[32,56,128]{2,1,0:T(8,128)(2,1)S(1)}, u32[]{:S(2)}, u32[]{:S(2)}) async-start(bf16[32,56,128]{2,1,0:T(8,128)(2,1)} %get-tuple-element.16), calls=%async_computation | async-start | bytes 917504 | tf_op jit(solution)/shard_map/all_to_all | solution.py:299
  16.2 0.0 copy-done.4
  16.2 3.2 %collective-permute-start = (bf16[32,384]{1,0:T(8,128)(2,1)S(1)}, bf16[32,384]{1,0:T(8,128)(2,1)S(1)}, u32[]{:S(2)}, u32[]{:S(2)}) collective-permute-start(bf16[32,384]{1,0:T(8,128)(2,1)S(1)} %copy-done.4), channel_id=1, source_target_pairs={{0,32},{32,64},{64,96},{96,0},{1,33},{33,65},{65,97},{97,1},{2,34}... | collective-permute-start | bytes 73736 | tf_op jit(solution)/shard_map/ppermute | solution.py:329
  19.4 0.0 copy-done.3
  19.5 4.2 %collective-permute-start.1 = (bf16[32,384]{1,0:T(8,128)(2,1)S(1)}, bf16[32,384]{1,0:T(8,128)(2,1)S(1)}, u32[]{:S(2)}, u32[]{:S(2)}) collective-permute-start(bf16[32,384]{1,0:T(8,128)(2,1)S(1)} %copy-done.3), channel_id=1, source_target_pairs={{0,64},{32,96},{64,0},{96,32},{1,65},{33,97},{65,1},{97,33},{2,66}... | collective-permute-start | bytes 73736 | tf_op jit(solution)/shard_map/ppermute | solution.py:329
  23.7 0.0 copy-done.2
  23.7 3.0 %collective-permute-start.2 = (bf16[32,384]{1,0:T(8,128)(2,1)S(1)}, bf16[32,384]{1,0:T(8,128)(2,1)S(1)}, u32[]{:S(2)}, u32[]{:S(2)}) collective-permute-start(bf16[32,384]{1,0:T(8,128)(2,1)S(1)} %copy-done.2), channel_id=1, source_target_pairs={{0,96},{32,0},{64,32},{96,64},{1,97},{33,1},{65,33},{97,65},{2,98}... | collective-permute-start | bytes 73736 | tf_op jit(solution)/shard_map/ppermute | solution.py:329
  26.7 0.0 copy-start
  26.7 0.1 pad_add_fusion.where_ref
  27.4 0.0 copy-start.1
  28.1 0.0 copy-done.1
  28.1 0.7 shard_map.86
  28.8 0.0 collective-permute-done.r1_ref
  28.8 0.0 collective-permute-done.1.r2_ref
  28.9 0.0 collective-permute-done.2.r3_ref
  28.9 1.8 %all-to-all-done.w_ref = bf16[32,56,128]{2,1,0:T(8,128)(2,1)S(1)} async-done(((bf16[32,56,128]{2,1,0:T(8,128)(2,1)}), bf16[32,56,128]{2,1,0:T(8,128)(2,1)S(1)}, u32[]{:S(2)}, u32[]{:S(2)}) %all-to-all-start) | async-done | bytes 458784 | tf_op jit(solution)/shard_map/all_to_all | solution.py:299
  30.7 0.0 copy-done
  30.7 1.3 %shard_map.88 = bf16[8,72,128]{2,1,0:T(8,128)(2,1)S(1)} custom-call(s32[4]{0:T(128)S(1)} %pad_add_fusion.where_ref, bf16[384,384]{1,0:T(8,128)(2,1)S(1)} %get-tuple-element.14.sort_ref, bf16[384,128]{1,0:T(8,128)(2,1)S(1)} %get-tuple-element.15.split_ref, bf16[32,56,128]{2,1,0:T(8,128)(2,1)S(1)} %all-to-all-done.w_ref, bf16[32,384]{1,0:T(8,128)(2,1)S(1)} %copy-done, ...), custom_call_target="tpu_custom_call" | custom-call | tf_op jit(solution)/shard_map/pallas_call | solution.py:35
  32.0 13.4 %all_to_all.20.got_ref = bf16[8,72,128]{2,1,0:T(8,128)(2,1)S(1)} all-to-all(bf16[8,72,128]{2,1,0:T(8,128)(2,1)S(1)} %shard_map.88), channel_id=1, replica_groups=mesh['x1'=2,'x0'=2,'y'=4,'z2'=2,'z1'=2,'z0'=2,'m0'=2,'m1'=2] {'y','m0'}, dimensions={0} | all-to-all | bytes 294912 | tf_op jit(solution)/shard_map/all_to_all | solution.py:299
  45.4 6.0 %all_gather.3.got_ref = f32[4,72,128]{2,1,0:T(8,128)S(1)} all-gather(f32[2,72,128]{2,1,0:T(8,128)S(1)} %shard_map.89), channel_id=1, replica_groups=mesh['x1'=2,'x0'=2,'y'=4,'z2'=2,'z1'=2,'z0'=2,'m0'=2,'m1'=2] {'m1'}, dimensions={0}, use_global_device_ids=true | all-gather | bytes 221184 | tf_op jit(solution)/shard_map/all_gather | solution.py:362
  51.4 0.2 shard_map.90.own_ref
  51.7 3.5 %collective-permute-start.3 = (bf16[296,128]{1,0:T(8,128)(2,1)S(1)}, bf16[296,128]{1,0:T(8,128)(2,1)S(1)}, u32[]{:S(2)}, u32[]{:S(2)}) collective-permute-start(bf16[296,128]{1,0:T(8,128)(2,1)S(1)} %shard_map.90.own_ref), channel_id=1, source_target_pairs={{0,32},{1,65},{2,482},{3,451},{4,36},{5,69},{6,486},{7,455},{8,40}... | collective-permute-start | bytes 227336 | tf_op jit(solution)/shard_map/ppermute | solution.py:369
  55.2 4.6 %collective-permute-done.3.other_ref = bf16[296,128]{1,0:T(8,128)(2,1)S(1)} collective-permute-done((bf16[296,128]{1,0:T(8,128)(2,1)S(1)}, bf16[296,128]{1,0:T(8,128)(2,1)S(1)}, u32[]{:S(2)}, u32[]{:S(2)}) %collective-permute-start.3) | collective-permute-done | bytes 75808 | tf_op jit(solution)/shard_map/ppermute | solution.py:369
  59.8 0.6 shard_map.91
  60.4 16.1 %all_to_all.21.got_ref = bf16[8,296,128]{2,1,0:T(8,128)(2,1)S(1)} all-to-all(bf16[8,296,128]{2,1,0:T(8,128)(2,1)S(1)} %shard_map.91), channel_id=1, replica_groups=mesh['x1'=2,'x0'=2,'y'=4,'z2'=2,'z1'=2,'z0'=2,'m0'=2,'m1'=2] {'z1','z0',..., dimensions={0} | all-to-all | bytes 1212416 | tf_op jit(solution)/shard_map/all_to_all | solution.py:299
  76.5 1.1 %shard_map.92 = bf16[4,72,128]{2,1,0:T(8,128)(2,1)S(1)} custom-call(s32[4]{0:T(128)S(1)} %pad_add_fusion.where_ref, f32[16,128]{1,0:T(8,128)S(1)} %get-tuple-element.12.scalars_ref, s32[16,128]{1,0:T(8,128)S(1)} %get-tuple-element.13.pair_ref, bf16[296,128]{1,0:T(8,128)(2,1)S(1)} %shard_map.90.own_ref, bf16[8,296,128]{2,1,0:T(8,128)(2,1)S(1)} %all_to_all.21.got_ref), custom_call_target="tpu_custom_call" | custom-call | tf_op jit(solution)/shard_map/pallas_call | solution.py:35
  77.5 14.9 %all_to_all.22.got_ref = bf16[4,72,128]{2,1,0:T(8,128)(2,1)S(1)} all-to-all(bf16[4,72,128]{2,1,0:T(8,128)(2,1)S(1)} %shard_map.92), channel_id=1, replica_groups=mesh['x1'=2,'x0'=2,'y'=4,'z2'=2,'z1'=2,'z0'=2,'m0'=2,'m1'=2] {'m0','m1'}, dimensions={0} | all-to-all | bytes 147456 | tf_op jit(solution)/shard_map/all_to_all | solution.py:299
  92.4 0.7 shard_map.93
  (1 shorter events, 0.0 us)
Async XLA Ops:
  2.3 13.9 %copy-start.4 = (bf16[32,384]{1,0:T(8,128)(2,1)S(1)}, bf16[32,384]{1,0:T(8,128)(2,1)}, u32[]{:S(2)}) copy-start(bf16[32,384]{1,0:T(8,128)(2,1)} %get-tuple-element.18) | copy-start | bytes 73732
  2.4 17.1 %copy-start.3 = (bf16[32,384]{1,0:T(8,128)(2,1)S(1)}, bf16[32,384]{1,0:T(8,128)(2,1)}, u32[]{:S(2)}) copy-start(bf16[32,384]{1,0:T(8,128)(2,1)} %get-tuple-element.19) | copy-start | bytes 73732
  2.4 21.3 %copy-start.2 = (bf16[32,384]{1,0:T(8,128)(2,1)S(1)}, bf16[32,384]{1,0:T(8,128)(2,1)}, u32[]{:S(2)}) copy-start(bf16[32,384]{1,0:T(8,128)(2,1)} %get-tuple-element.20) | copy-start | bytes 73732
  2.4 28.3 %all-to-all-start = ((bf16[32,56,128]{2,1,0:T(8,128)(2,1)}), bf16[32,56,128]{2,1,0:T(8,128)(2,1)S(1)}, u32[]{:S(2)}, u32[]{:S(2)}) async-start(bf16[32,56,128]{2,1,0:T(8,128)(2,1)} %get-tuple-element.16), calls=%async_computation | async-start | bytes 917504 | tf_op jit(solution)/shard_map/all_to_all | solution.py:299
  16.2 12.6 %collective-permute-start = (bf16[32,384]{1,0:T(8,128)(2,1)S(1)}, bf16[32,384]{1,0:T(8,128)(2,1)S(1)}, u32[]{:S(2)}, u32[]{:S(2)}) collective-permute-start(bf16[32,384]{1,0:T(8,128)(2,1)S(1)} %copy-done.4), channel_id=1, source_target_pairs={{0,32},{32,64},{64,96},{96,0},{1,33},{33,65},{65,97},{97,1},{2,34}... | collective-permute-start | bytes 73736 | tf_op jit(solution)/shard_map/ppermute | solution.py:329
  19.5 9.4 %collective-permute-start.1 = (bf16[32,384]{1,0:T(8,128)(2,1)S(1)}, bf16[32,384]{1,0:T(8,128)(2,1)S(1)}, u32[]{:S(2)}, u32[]{:S(2)}) collective-permute-start(bf16[32,384]{1,0:T(8,128)(2,1)S(1)} %copy-done.3), channel_id=1, source_target_pairs={{0,64},{32,96},{64,0},{96,32},{1,65},{33,97},{65,1},{97,33},{2,66}... | collective-permute-start | bytes 73736 | tf_op jit(solution)/shard_map/ppermute | solution.py:329
  23.7 5.2 %collective-permute-start.2 = (bf16[32,384]{1,0:T(8,128)(2,1)S(1)}, bf16[32,384]{1,0:T(8,128)(2,1)S(1)}, u32[]{:S(2)}, u32[]{:S(2)}) collective-permute-start(bf16[32,384]{1,0:T(8,128)(2,1)S(1)} %copy-done.2), channel_id=1, source_target_pairs={{0,96},{32,0},{64,32},{96,64},{1,97},{33,1},{65,33},{97,65},{2,98}... | collective-permute-start | bytes 73736 | tf_op jit(solution)/shard_map/ppermute | solution.py:329
  26.7 4.0 %copy-start = (bf16[32,384]{1,0:T(8,128)(2,1)S(1)}, bf16[32,384]{1,0:T(8,128)(2,1)}, u32[]{:S(2)}) copy-start(bf16[32,384]{1,0:T(8,128)(2,1)} %get-tuple-element.17.r0_ref) | copy-start | bytes 73732
  27.4 0.7 copy-start.1
  51.7 8.1 %collective-permute-start.3 = (bf16[296,128]{1,0:T(8,128)(2,1)S(1)}, bf16[296,128]{1,0:T(8,128)(2,1)S(1)}, u32[]{:S(2)}, u32[]{:S(2)}) collective-permute-start(bf16[296,128]{1,0:T(8,128)(2,1)S(1)} %shard_map.90.own_ref), channel_id=1, source_target_pairs={{0,32},{1,65},{2,482},{3,451},{4,36},{5,69},{6,486},{7,455},{8,40}... | collective-permute-start | bytes 227336 | tf_op jit(solution)/shard_map/ppermute | solution.py:369

commit v12 on v11

--- a/solution.py
+++ b/solution.py
@@ -117,22 +117,28 @@
     sort = sort_ref[...]
     low = split_ref[0:192, :]
     high = split_ref[192:384, :]
-    weights = [[], []]
+    mains = []
+    tails = []
     for half in range(2):
         places = [
             place_in(SPREAD, x=q >> 3, z=q & 7) for q in range(16 * half, 16 * half + 16)
         ]
         some = jnp.stack([w_ref[place] for place in places], axis=0)
-        main = jnp.concatenate(
-            [some[:, 0:24].reshape(384, 128), some[:, 24:48].reshape(384, 128)], axis=1
-        )
-        tail = some[:, 48:56].reshape(128, 128)
-        main = jnp.dot(sort, main, preferred_element_type=f32).astype(bf16)
-        low_tail = jnp.dot(low, tail, preferred_element_type=f32)
-        high_tail = jnp.dot(high, tail, preferred_element_type=f32)
+        mains.append(
+            jnp.concatenate(
+                [some[:, 0:24].reshape(384, 128), some[:, 24:48].reshape(384, 128)], axis=1
+            )
+        )
+        tails.append(some[:, 48:56].reshape(128, 128))
+    mains = [jnp.dot(sort, main, preferred_element_type=f32) for main in mains]
+    lows = [jnp.dot(low, tail, preferred_element_type=f32) for tail in tails]
+    highs = [jnp.dot(high, tail, preferred_element_type=f32) for tail in tails]
+    weights = [[], []]
+    for half in range(2):
+        main = mains[half].astype(bf16)
         for which in range(2):
             at = 64 * which
-            tail = low_tail[:, at : at + 32] + high_tail[:, at + 32 : at + 64]
+            tail = lows[half][:, at : at + 32] + highs[half][:, at + 32 : at + 64]
             tail = tail.astype(bf16)
             weights[which].append(
                 jnp.concatenate([main[192 * which : 192 * which + 192]] + [tail] * 4, axis=1)

time: 93.7 us -> 93.7 us (level)
  no operation moved by 1% of the time
where the time goes in v12:
time: 93.7 us; the launch traced here: 93.1 us
  blocking collectives  50.3 us (54%)
  starting transfers between devices  27.8 us (30%)
  waiting for transfers between devices  6.4 us (7%)
  Pallas kernels  6.38 us (7%)
  between operations  2.14 us (2%)
    all_to_all x3, blocking collectives, exchange(): return lax.all_to_all(value, axes, split_axis=0, concat_axis=0, tiled=True)  44.3 us
    all_to_all x1, starting transfers between devices, exchange(): return lax.all_to_all(value, axes, split_axis=0, concat_axis=0, tiled=True)  13.8 us
    ppermute x3, starting transfers between devices, local(): lax.ppermute(chosen[k], 'y', [(s, (s + k) % 4) for s in range(4)])  10.4 us
    pallas_call x8, Pallas kernels, call(): pl.pallas_call(body, out_shape=out_shape, in_specs=specs, out_specs=outs,...  6.38 us
    all_gather x1, blocking collectives, local(): got = lax.all_gather(half, 'm1', axis=0, tiled=True)  6 us
    ppermute x1, waiting for transfers between devices, local(): other = lax.ppermute(own, BATCH + MP, moves)  4.58 us
    ppermute x1, starting transfers between devices, local(): other = lax.ppermute(own, BATCH + MP, moves)  3.54 us
  transfers between devices with their start and end apart: 5, of which 2 were waited for; matrix products, arithmetic and copies ran while one was open for 0% of the time, Pallas kernels for 1%

profile of v12, /device:TPU:1, one launch (start us, length us, event | category | flops | bytes accessed | tf_op | source)
XLA Modules:
  0.0 93.1 jit_solution(4872595431445422838)
XLA Ops:
  0.6 1.7 %shard_map.87 = (bf16[32,56,128]{2,1,0:T(8,128)(2,1)}, bf16[32,384]{1,0:T(8,128)(2,1)}, bf16[32,384]{1,0:T(8,128)(2,1)}, bf16[32,384]{1,0:T(8,128)(2,1)}, bf16[32,384]{1,0:T(8,128)(2,1)}) custom-call(bf16[12,288]{1,0:T(8,128)(2,1)} %w_img_ref.1, bf16[12,288]{1,0:T(8,128)(2,1)} %w_txt_ref.1, bf16[16,1536]{1,0:T(8,128)(2,1)} %img_ref.1, bf16[16,1536]{1,0:T(8,128)(2,1)} %txt_ref.1), custom_call_target="tpu_custom_call" | custom-call | tf_op jit(solution)/shard_map/pallas_call | solution.py:35
  2.3 0.0 copy-start.4
  2.4 0.0 copy-start.3
  2.4 0.0 copy-start.2
  2.4 13.8 %all-to-all-start = ((bf16[32,56,128]{2,1,0:T(8,128)(2,1)}), bf16[32,56,128]{2,1,0:T(8,128)(2,1)S(1)}, u32[]{:S(2)}, u32[]{:S(2)}) async-start(bf16[32,56,128]{2,1,0:T(8,128)(2,1)} %get-tuple-element.16), calls=%async_computation | async-start | bytes 917504 | tf_op jit(solution)/shard_map/all_to_all | solution.py:305
  16.2 0.0 copy-done.4
  16.2 3.2 %collective-permute-start = (bf16[32,384]{1,0:T(8,128)(2,1)S(1)}, bf16[32,384]{1,0:T(8,128)(2,1)S(1)}, u32[]{:S(2)}, u32[]{:S(2)}) collective-permute-start(bf16[32,384]{1,0:T(8,128)(2,1)S(1)} %copy-done.4), channel_id=1, source_target_pairs={{0,32},{32,64},{64,96},{96,0},{1,33},{33,65},{65,97},{97,1},{2,34}... | collective-permute-start | bytes 73736 | tf_op jit(solution)/shard_map/ppermute | solution.py:335
  19.4 0.0 copy-done.3
  19.5 4.2 %collective-permute-start.1 = (bf16[32,384]{1,0:T(8,128)(2,1)S(1)}, bf16[32,384]{1,0:T(8,128)(2,1)S(1)}, u32[]{:S(2)}, u32[]{:S(2)}) collective-permute-start(bf16[32,384]{1,0:T(8,128)(2,1)S(1)} %copy-done.3), channel_id=1, source_target_pairs={{0,64},{32,96},{64,0},{96,32},{1,65},{33,97},{65,1},{97,33},{2,66}... | collective-permute-start | bytes 73736 | tf_op jit(solution)/shard_map/ppermute | solution.py:335
  23.7 0.0 copy-done.2
  23.7 3.0 %collective-permute-start.2 = (bf16[32,384]{1,0:T(8,128)(2,1)S(1)}, bf16[32,384]{1,0:T(8,128)(2,1)S(1)}, u32[]{:S(2)}, u32[]{:S(2)}) collective-permute-start(bf16[32,384]{1,0:T(8,128)(2,1)S(1)} %copy-done.2), channel_id=1, source_target_pairs={{0,96},{32,0},{64,32},{96,64},{1,97},{33,1},{65,33},{97,65},{2,98}... | collective-permute-start | bytes 73736 | tf_op jit(solution)/shard_map/ppermute | solution.py:335
  26.7 0.0 copy-start
  26.7 0.1 pad_add_fusion.where_ref
  27.4 0.0 copy-start.1
  28.1 0.0 copy-done.1
  28.1 0.7 shard_map.86
  28.8 0.0 collective-permute-done.r1_ref
  28.8 0.0 collective-permute-done.1.r2_ref
  28.9 0.0 collective-permute-done.2.r3_ref
  28.9 1.8 %all-to-all-done.w_ref = bf16[32,56,128]{2,1,0:T(8,128)(2,1)S(1)} async-done(((bf16[32,56,128]{2,1,0:T(8,128)(2,1)}), bf16[32,56,128]{2,1,0:T(8,128)(2,1)S(1)}, u32[]{:S(2)}, u32[]{:S(2)}) %all-to-all-start) | async-done | bytes 458784 | tf_op jit(solution)/shard_map/all_to_all | solution.py:305
  30.7 0.0 copy-done
  30.7 1.4 %shard_map.88 = bf16[8,72,128]{2,1,0:T(8,128)(2,1)S(1)} custom-call(s32[4]{0:T(128)S(1)} %pad_add_fusion.where_ref, bf16[384,384]{1,0:T(8,128)(2,1)S(1)} %get-tuple-element.14.sort_ref, bf16[384,128]{1,0:T(8,128)(2,1)S(1)} %get-tuple-element.15.split_ref, bf16[32,56,128]{2,1,0:T(8,128)(2,1)S(1)} %all-to-all-done.w_ref, bf16[32,384]{1,0:T(8,128)(2,1)S(1)} %copy-done, ...), custom_call_target="tpu_custom_call" | custom-call | tf_op jit(solution)/shard_map/pallas_call | solution.py:35
  32.0 13.4 %all_to_all.20.got_ref = bf16[8,72,128]{2,1,0:T(8,128)(2,1)S(1)} all-to-all(bf16[8,72,128]{2,1,0:T(8,128)(2,1)S(1)} %shard_map.88), channel_id=1, replica_groups=mesh['x1'=2,'x0'=2,'y'=4,'z2'=2,'z1'=2,'z0'=2,'m0'=2,'m1'=2] {'y','m0'}, dimensions={0} | all-to-all | bytes 294912 | tf_op jit(solution)/shard_map/all_to_all | solution.py:305
  45.4 6.0 %all_gather.3.got_ref = f32[4,72,128]{2,1,0:T(8,128)S(1)} all-gather(f32[2,72,128]{2,1,0:T(8,128)S(1)} %shard_map.89), channel_id=1, replica_groups=mesh['x1'=2,'x0'=2,'y'=4,'z2'=2,'z1'=2,'z0'=2,'m0'=2,'m1'=2] {'m1'}, dimensions={0}, use_global_device_ids=true | all-gather | bytes 221184 | tf_op jit(solution)/shard_map/all_gather | solution.py:368
  51.4 0.2 shard_map.90.own_ref
  51.7 3.5 %collective-permute-start.3 = (bf16[296,128]{1,0:T(8,128)(2,1)S(1)}, bf16[296,128]{1,0:T(8,128)(2,1)S(1)}, u32[]{:S(2)}, u32[]{:S(2)}) collective-permute-start(bf16[296,128]{1,0:T(8,128)(2,1)S(1)} %shard_map.90.own_ref), channel_id=1, source_target_pairs={{0,32},{1,65},{2,482},{3,451},{4,36},{5,69},{6,486},{7,455},{8,40}... | collective-permute-start | bytes 227336 | tf_op jit(solution)/shard_map/ppermute | solution.py:375
  55.2 4.6 %collective-permute-done.3.other_ref = bf16[296,128]{1,0:T(8,128)(2,1)S(1)} collective-permute-done((bf16[296,128]{1,0:T(8,128)(2,1)S(1)}, bf16[296,128]{1,0:T(8,128)(2,1)S(1)}, u32[]{:S(2)}, u32[]{:S(2)}) %collective-permute-start.3) | collective-permute-done | bytes 75808 | tf_op jit(solution)/shard_map/ppermute | solution.py:375
  59.8 0.6 shard_map.91
  60.4 16.1 %all_to_all.21.got_ref = bf16[8,296,128]{2,1,0:T(8,128)(2,1)S(1)} all-to-all(bf16[8,296,128]{2,1,0:T(8,128)(2,1)S(1)} %shard_map.91), channel_id=1, replica_groups=mesh['x1'=2,'x0'=2,'y'=4,'z2'=2,'z1'=2,'z0'=2,'m0'=2,'m1'=2] {'z1','z0',..., dimensions={0} | all-to-all | bytes 1212416 | tf_op jit(solution)/shard_map/all_to_all | solution.py:305
  76.5 1.1 %shard_map.92 = bf16[4,72,128]{2,1,0:T(8,128)(2,1)S(1)} custom-call(s32[4]{0:T(128)S(1)} %pad_add_fusion.where_ref, f32[16,128]{1,0:T(8,128)S(1)} %get-tuple-element.12.scalars_ref, s32[16,128]{1,0:T(8,128)S(1)} %get-tuple-element.13.pair_ref, bf16[296,128]{1,0:T(8,128)(2,1)S(1)} %shard_map.90.own_ref, bf16[8,296,128]{2,1,0:T(8,128)(2,1)S(1)} %all_to_all.21.got_ref), custom_call_target="tpu_custom_call" | custom-call | tf_op jit(solution)/shard_map/pallas_call | solution.py:35
  77.5 14.9 %all_to_all.22.got_ref = bf16[4,72,128]{2,1,0:T(8,128)(2,1)S(1)} all-to-all(bf16[4,72,128]{2,1,0:T(8,128)(2,1)S(1)} %shard_map.92), channel_id=1, replica_groups=mesh['x1'=2,'x0'=2,'y'=4,'z2'=2,'z1'=2,'z0'=2,'m0'=2,'m1'=2] {'m0','m1'}, dimensions={0} | all-to-all | bytes 147456 | tf_op jit(solution)/shard_map/all_to_all | solution.py:305
  92.4 0.7 shard_map.93
  (1 shorter events, 0.0 us)
Async XLA Ops:
  2.3 13.9 %copy-start.4 = (bf16[32,384]{1,0:T(8,128)(2,1)S(1)}, bf16[32,384]{1,0:T(8,128)(2,1)}, u32[]{:S(2)}) copy-start(bf16[32,384]{1,0:T(8,128)(2,1)} %get-tuple-element.18) | copy-start | bytes 73732
  2.4 17.1 %copy-start.3 = (bf16[32,384]{1,0:T(8,128)(2,1)S(1)}, bf16[32,384]{1,0:T(8,128)(2,1)}, u32[]{:S(2)}) copy-start(bf16[32,384]{1,0:T(8,128)(2,1)} %get-tuple-element.19) | copy-start | bytes 73732
  2.4 21.3 %copy-start.2 = (bf16[32,384]{1,0:T(8,128)(2,1)S(1)}, bf16[32,384]{1,0:T(8,128)(2,1)}, u32[]{:S(2)}) copy-start(bf16[32,384]{1,0:T(8,128)(2,1)} %get-tuple-element.20) | copy-start | bytes 73732
  2.4 28.3 %all-to-all-start = ((bf16[32,56,128]{2,1,0:T(8,128)(2,1)}), bf16[32,56,128]{2,1,0:T(8,128)(2,1)S(1)}, u32[]{:S(2)}, u32[]{:S(2)}) async-start(bf16[32,56,128]{2,1,0:T(8,128)(2,1)} %get-tuple-element.16), calls=%async_computation | async-start | bytes 917504 | tf_op jit(solution)/shard_map/all_to_all | solution.py:305
  16.2 12.6 %collective-permute-start = (bf16[32,384]{1,0:T(8,128)(2,1)S(1)}, bf16[32,384]{1,0:T(8,128)(2,1)S(1)}, u32[]{:S(2)}, u32[]{:S(2)}) collective-permute-start(bf16[32,384]{1,0:T(8,128)(2,1)S(1)} %copy-done.4), channel_id=1, source_target_pairs={{0,32},{32,64},{64,96},{96,0},{1,33},{33,65},{65,97},{97,1},{2,34}... | collective-permute-start | bytes 73736 | tf_op jit(solution)/shard_map/ppermute | solution.py:335
  19.5 9.4 %collective-permute-start.1 = (bf16[32,384]{1,0:T(8,128)(2,1)S(1)}, bf16[32,384]{1,0:T(8,128)(2,1)S(1)}, u32[]{:S(2)}, u32[]{:S(2)}) collective-permute-start(bf16[32,384]{1,0:T(8,128)(2,1)S(1)} %copy-done.3), channel_id=1, source_target_pairs={{0,64},{32,96},{64,0},{96,32},{1,65},{33,97},{65,1},{97,33},{2,66}... | collective-permute-start | bytes 73736 | tf_op jit(solution)/shard_map/ppermute | solution.py:335
  23.7 5.2 %collective-permute-start.2 = (bf16[32,384]{1,0:T(8,128)(2,1)S(1)}, bf16[32,384]{1,0:T(8,128)(2,1)S(1)}, u32[]{:S(2)}, u32[]{:S(2)}) collective-permute-start(bf16[32,384]{1,0:T(8,128)(2,1)S(1)} %copy-done.2), channel_id=1, source_target_pairs={{0,96},{32,0},{64,32},{96,64},{1,97},{33,1},{65,33},{97,65},{2,98}... | collective-permute-start | bytes 73736 | tf_op jit(solution)/shard_map/ppermute | solution.py:335
  26.7 4.0 %copy-start = (bf16[32,384]{1,0:T(8,128)(2,1)S(1)}, bf16[32,384]{1,0:T(8,128)(2,1)}, u32[]{:S(2)}) copy-start(bf16[32,384]{1,0:T(8,128)(2,1)} %get-tuple-element.17.r0_ref) | copy-start | bytes 73732
  27.4 0.7 copy-start.1
  51.7 8.1 %collective-permute-start.3 = (bf16[296,128]{1,0:T(8,128)(2,1)S(1)}, bf16[296,128]{1,0:T(8,128)(2,1)S(1)}, u32[]{:S(2)}, u32[]{:S(2)}) collective-permute-start(bf16[296,128]{1,0:T(8,128)(2,1)S(1)} %shard_map.90.own_ref), channel_id=1, source_target_pairs={{0,32},{1,65},{2,482},{3,451},{4,36},{5,69},{6,486},{7,455},{8,40}... | collective-permute-start | bytes 227336 | tf_op jit(solution)/shard_map/ppermute | solution.py:375
